TPU v7x, 1024 devices: a whole 4x4x32 slice. The times are simulated.
1024 devices in a mesh: grp: 16 (over x, z_hi), seq: 16 (over z_lo, core), tp: 4 (over y).
Axes of the slice: x: 4, y: 4, z: 32 (z_hi: 4, z_lo: 8; z = z_hi * 8 + z_lo), core: 2. Of those that a mesh axis runs over, the one named last changes fastest.
Arguments:
- hidden: bfloat16 [32768, 8192], P(('grp', 'seq')), may hold values from -6 to 6
- queries: bfloat16 [32768, 4096], P(('grp', 'seq'), 'tp'), may hold values from -900 to 900, as said below
- vis_rows: bfloat16 [256, 16, 4, 8192], P(('grp', 'seq')), may hold values from -6 to 6
- vis_slot: int32 [256, 16, 4], P(('grp', 'seq')), may hold values from -1 to 127, as said below
- doc_ids: int32 [16, 2048], P('grp', 'seq'), may hold values from 0 to 7, never falling along the last dimension, each value on 1 to 1024 neighbouring positions
- w_key: bfloat16 [8192, 512], P('grp', 'tp'), may hold values from -0.0625 to 0.0625
- w_value: bfloat16 [8192, 512], P('grp', 'tp'), may hold values from -0.0625 to 0.0625
Outputs:
- attended: bfloat16 [32768, 4096], P(('grp', 'seq'), 'tp')
Inputs may be any that keep to these rules, and one draw needn't show every extreme that they name: `queries`: a row may be scaled far from one. `vis_slot`: entry [g * 16 + s, d, c] names a position within the 128 positions of index d of seq in group g, or -1. Live positions are distinct within a destination; each device sends 1 to 4 live rows to every destination, slots 0 upward; in every group one destination receives 4 from every device.
All inputs are finite; a program needn't handle non-finite values.
Results may differ from a plain program's by a relative error of at most 0.024.
Values may be sent and summed in bfloat16 or wider, within the bound.
No kernel may reach another device: no remote copies, remote signals or barrier semaphores. Data moves between devices by JAX's collectives and lax.ppermute only.
A program may use at most 32 MiB of HBM per device.

v0:
```python
import jax
import jax.numpy as jnp
from jax import lax
from jax.sharding import PartitionSpec as P

HEAD = 128
QPK = 8
CAP = 4


def in_one_piece(arrays, axis, dim, along):
    widths = [a.shape[along] for a in arrays]
    both = jnp.concatenate(arrays, axis=along)
    out = lax.all_gather(both, axis, axis=dim, tiled=True)
    return tuple(jnp.split(out, [sum(widths[:k]) for k in range(1, len(widths))], axis=along))


def side_by_side(arrays, axis, split_dim, concat_dim, along):
    ends, at = ([], 0)
    for a in arrays[:-1]:
        at += a.shape[along]
        ends.append(at)
    both = jnp.concatenate(arrays, axis=along)
    return tuple(
        jnp.split(
            lax.all_to_all(both, axis, split_axis=split_dim, concat_axis=concat_dim, tiled=True),
            ends,
            axis=along,
        )
    )


def from_everyone(array, axis):
    copies = jnp.broadcast_to(array, (lax.axis_size(axis), *array.shape))
    return lax.all_to_all(copies, axis, split_axis=0, concat_axis=0, tiled=True)


def in_order(parts, dim):
    dims = list(parts.shape[1:])
    dims[dim] *= parts.shape[0]
    return jnp.moveaxis(parts, 0, dim).reshape(dims)


def gathered_copies(array, axis, dim):
    parts = from_everyone(array, axis)
    return in_order(parts, dim)


def sent_together(arrays, axis, dim, along):
    both = jnp.concatenate(arrays, axis=along)
    out, at, finished = (gathered_copies(both, axis, dim), 0, [])
    for a in arrays:
        finished.append(lax.slice_in_dim(out, at, at + a.shape[along], axis=along))
        at += a.shape[along]
    return tuple(finished)


def shards(hidden, queries, vis_rows, vis_slot, doc_ids, w_key, w_value):
    tokens = hidden.shape[0]
    width = hidden.shape[1]
    kv_cols = w_key.shape[1]
    kv_local = kv_cols // HEAD
    seq_place = lax.axis_index("seq")
    extra = vis_rows.reshape(-1, width)
    piece_key, piece_value = in_one_piece((w_key, w_value), "grp", 0, 1)
    span = piece_key.shape[0]
    text_keys = jnp.dot(hidden, piece_key, preferred_element_type=jnp.float32)
    text_values = jnp.dot(hidden, piece_value, preferred_element_type=jnp.float32)
    vis_keys = jnp.dot(extra, piece_key, preferred_element_type=jnp.float32)
    vis_values = jnp.dot(extra, piece_value, preferred_element_type=jnp.float32)
    text_keys = text_keys.astype(jnp.bfloat16)
    text_values = text_values.astype(jnp.bfloat16)
    vis_keys = vis_keys.astype(jnp.bfloat16)
    vis_values = vis_values.astype(jnp.bfloat16)
    senders = vis_slot.shape[1]
    sent_keys = vis_keys.reshape(1, senders, CAP, kv_cols)
    sent_values = vis_values.reshape(1, senders, CAP, kv_cols)
    got_keys, got_values, got_slot = (
        *side_by_side((sent_keys, sent_values), "seq", 1, 0, 2),
        lax.all_to_all(vis_slot, "seq", split_axis=1, concat_axis=0, tiled=True),
    )
    vis_keys = got_keys.reshape(-1, kv_cols)
    vis_values = got_values.reshape(-1, kv_cols)
    slots = got_slot.reshape(-1)
    positions = lax.broadcasted_iota(jnp.int32, (tokens, slots.shape[0]), 0)
    matches = slots[None, :] == positions
    chooser = matches.astype(jnp.bfloat16)
    used = jnp.any(matches, axis=1)[:, None]
    keys = jnp.where(
        used,
        jnp.dot(chooser, vis_keys, preferred_element_type=jnp.float32).astype(jnp.bfloat16),
        text_keys,
    )
    values = jnp.where(
        used,
        jnp.dot(chooser, vis_values, preferred_element_type=jnp.float32).astype(jnp.bfloat16),
        text_values,
    )
    my_docs = doc_ids.reshape(-1)
    query_pos = seq_place * tokens + jnp.arange(tokens, dtype=jnp.int32)
    last_query = seq_place * tokens + tokens - 1
    q_local = queries.reshape(tokens, kv_local, QPK, HEAD)
    scale = 1.0 / jnp.sqrt(jnp.float32(HEAD))
    init_top = jnp.full((kv_local, QPK, tokens), -1e30, jnp.float32)
    init_total = jnp.zeros((kv_local, QPK, tokens), jnp.float32)
    init_acc = jnp.zeros((kv_local, QPK, tokens, HEAD), jnp.float32)
    piece_key, piece_value, piece_doc = (
        *sent_together((keys, values), "seq", 0, 1),
        gathered_copies(my_docs, "seq", 0),
    )
    span = piece_key.shape[0]

    def work(state):
        top, total, acc = state
        k_rows = piece_key.reshape(span, kv_local, HEAD)
        v_rows = piece_value.reshape(span, kv_local, HEAD)
        scores = (
            jnp.einsum("tgqd,rgd->gqtr", q_local, k_rows, preferred_element_type=jnp.float32)
            * scale
        )
        key_pos = jnp.arange(span, dtype=jnp.int32)
        allowed = (key_pos[None, :] <= query_pos[:, None]) & (
            piece_doc[None, :] == my_docs[:, None]
        )
        scores = jnp.where(allowed, scores, jnp.float32(-1e30))
        new_top = jnp.maximum(top, jnp.max(scores, axis=-1))
        weights = jnp.where(allowed, jnp.exp(scores - new_top[..., None]), jnp.float32(0.0))
        total = jnp.sum(weights, axis=-1)
        acc = jnp.einsum(
            "gqtr,rgd->gqtd",
            weights.astype(jnp.bfloat16),
            v_rows,
            preferred_element_type=jnp.float32,
        )
        return (new_top, total, acc)

    top, total, acc = lax.cond(
        jnp.int32(0) > last_query, lambda state: state, work, (init_top, init_total, init_acc)
    )
    result = acc / total[..., None]
    return result.transpose(2, 0, 1, 3).reshape(tokens, kv_local * QPK * HEAD).astype(jnp.bfloat16)


def solution(mesh):
    return jax.shard_map(
        shards,
        mesh=mesh,
        in_specs=(
            P(("grp", "seq"), None),
            P(("grp", "seq"), "tp"),
            P(("grp", "seq"), None, None, None),
            P(("grp", "seq"), None, None),
            P("grp", "seq"),
            P("grp", "tp"),
            P("grp", "tp"),
        ),
        out_specs=P(("grp", "seq"), "tp"),
        check_vma=False,
    )
```

profile of v0, /device:TPU:33, one launch (start us, length us, event | category | flops | bytes accessed | tf_op | source)
XLA Modules:
  0.0 366.5 jit_solution(16787598866303129055)
XLA Ops:
  6.5 0.0 copy-start
  6.5 0.0 all-gather.2.cloned.1.call-start
  6.5 1.8 pad_maximum_fusion
  8.4 0.0 all-gather.2.cloned.1.call-update
  8.4 1.3 copy.28
  9.8 16.3 %all-to-all-start.1 = ((s32[1,16,4]{2,0,1:T(1,128)}), s32[1,16,4]{2,0,1:T(1,128)S(1)}, u32[]{:S(2)}, u32[]{:S(2)}) async-start(s32[1,16,4]{2,0,1:T(1,128)} %copy.28), calls=%async_computation.1 | async-start | bytes 16384 | tf_op jit(solution)/shard_map/all_to_all | solution.py:80
  26.0 1.3 reshape.80
  27.4 7.4 %all-to-all-done.1 = s32[1,16,4]{2,0,1:T(1,128)S(1)} async-done(((s32[1,16,4]{2,0,1:T(1,128)}), s32[1,16,4]{2,0,1:T(1,128)S(1)}, u32[]{:S(2)}, u32[]{:S(2)}) %all-to-all-start.1) | async-done | bytes 288 | tf_op jit(solution)/shard_map/all_to_all | solution.py:80
  34.8 0.5 broadcast.32
  35.3 0.6 reduce.7
  35.9 0.1 eq.32
  36.0 0.1 fusion.46
  36.1 221.6 %all-gather.2.cloned.1.call-done = bf16[8192,256]{1,0:T(8,128)(2,1)} async-done(((bf16[512,256]{1,0:T(8,128)(2,1)}), bf16[8192,256]{1,0:T(8,128)(2,1)}) %all-gather.2.cloned.1.call-update) | async-done | bytes 4194320 | tf_op jit(solution)/shard_map/all_gather | solution.py:14
  257.8 2.1 fusion.39
  259.8 2.1 fusion.42
  261.9 0.6 pad_maximum_fusion.2
  262.6 12.1 %all-to-all-start.2 = ((bf16[1,16,8,128]{3,2,0,1:T(8,128)(2,1)}), bf16[1,16,8,128]{3,2,0,1:T(8,128)(2,1)S(1)}, u32[]{:S(2)}, u32[]{:S(2)}) async-start(bf16[1,16,8,128]{3,2,0,1:T(8,128)(2,1)} %pad_maximum_fusion.2), calls=%async_computation.2 | async-start | bytes 65536 | tf_op jit(solution)/shard_map/all_to_all | solution.py:26
  274.6 0.0 copy-done
  274.6 0.0 copy-start.2
  274.6 0.0 copy-start.1
  274.7 2.5 fusion.36
  277.2 0.3 copy-done.2
  277.5 0.0 copy-start.3
  277.5 0.8 fusion.33
  278.3 5.4 %all-to-all-done.2 = bf16[1,16,8,128]{3,2,0,1:T(8,128)(2,1)S(1)} async-done(((bf16[1,16,8,128]{3,2,0,1:T(8,128)(2,1)}), bf16[1,16,8,128]{3,2,0,1:T(8,128)(2,1)S(1)}, u32[]{:S(2)}, u32[]{:S(2)}) %all-to-all-start.2) | async-done | bytes 32800 | tf_op jit(solution)/shard_map/all_to_all | solution.py:26
  283.6 0.0 copy-done.1
  283.6 0.6 broadcast_in_dim.46
  284.2 5.0 %all-to-all-start = ((s32[16,1,128]{2,1,0:T(1,128)}), s32[16,1,128]{2,1,0:T(1,128)S(1)}, u32[]{:S(2)}, u32[]{:S(2)}) async-start(s32[16,1,128]{2,1,0:T(1,128)} %broadcast_in_dim.46), calls=%async_computation | async-start | bytes 16384 | tf_op jit(solution)/shard_map/all_to_all | solution.py:35
  289.3 0.2 fusion.31
  289.5 0.2 fusion.32
  289.8 0.1 copy.31
  289.9 8.0 %all-to-all-done = s32[16,1,128]{2,1,0:T(1,128)S(1)} async-done(((s32[16,1,128]{2,1,0:T(1,128)}), s32[16,1,128]{2,1,0:T(1,128)S(1)}, u32[]{:S(2)}, u32[]{:S(2)}) %all-to-all-start) | async-done | bytes 8224 | tf_op jit(solution)/shard_map/all_to_all | solution.py:35
  297.9 1.1 broadcast_in_dim.48
  299.0 5.2 %all-to-all-start.3 = ((bf16[16,128,256]{2,1,0:T(8,128)(2,1)}), bf16[16,128,256]{2,1,0:T(8,128)(2,1)S(1)}, u32[]{:S(2)}, u32[]{:S(2)}) async-start(bf16[16,128,256]{2,1,0:T(8,128)(2,1)} %broadcast_in_dim.48), calls=%async_computation.3 | async-start | bytes 2097152 | tf_op jit(solution)/shard_map/all_to_all | solution.py:35
  304.2 48.1 %all-to-all-done.3 = bf16[16,128,256]{2,1,0:T(8,128)(2,1)S(1)} async-done(((bf16[16,128,256]{2,1,0:T(8,128)(2,1)}), bf16[16,128,256]{2,1,0:T(8,128)(2,1)S(1)}, u32[]{:S(2)}, u32[]{:S(2)}) %all-to-all-start.3) | async-done | bytes 1048608 | tf_op jit(solution)/shard_map/all_to_all | solution.py:35
  352.4 0.0 copy-done.3
  352.4 6.1 %conditional.1 = (f32[1,8,128]{2,1,0:T(8,128)S(1)}, f32[1,8,128,128]{3,2,1,0:T(8,128)S(1)}) conditional(s32[]{:T(128)} %convert_element_type.47, (s32[]{:T(128)}, s32[128]{0:T(128)S(1)}, s32[16,1,128]{2,1,0:T(1,128)S(1)}, s32[1,128]{1,0:T(1,128)S(1)}, bf16[16,128,256]{2,1,0:T(8,128)(2,1)S(1)}, /*index=5*/bf16[128,1024]{1,0:T(8,128)(2,1)S(1)}) %tuple.25, ...), branch_computations={%region_1.4_spmd, %region_4.5_spmd} | conditional | flops 1101790336 | bytes 28084244 | solution.py:137
  352.4 0.3 fusion.10
  352.7 1.3 fusion
  354.1 2.4 fusion.7
  356.5 2.0 fusion.2
  358.5 0.2 fusion.45
  358.7 0.2 copy.32
  358.9 0.8 copy.43
  (5 shorter events, 0.0 us)
Async XLA Ops:
  6.5 268.1 %copy-start = (bf16[128,8192]{1,0:T(8,128)(2,1)S(1)}, bf16[128,8192]{1,0:T(8,128)(2,1)}, u32[]{:S(2)}) copy-start(bf16[128,8192]{1,0:T(8,128)(2,1)} %param.9) | copy-start | bytes 6291460
  6.5 251.2 %all-gather.2.cloned.1.call-start = ((), (), s32[]{:S(2)}) async-start(), calls=%async_computation.4 | async-start | bytes 4456448 | tf_op jit(solution)/shard_map/all_gather | solution.py:14
  9.8 25.0 %all-to-all-start.1 = ((s32[1,16,4]{2,0,1:T(1,128)}), s32[1,16,4]{2,0,1:T(1,128)S(1)}, u32[]{:S(2)}, u32[]{:S(2)}) async-start(s32[1,16,4]{2,0,1:T(1,128)} %copy.28), calls=%async_computation.1 | async-start | bytes 16384 | tf_op jit(solution)/shard_map/all_to_all | solution.py:80
  262.6 21.1 %all-to-all-start.2 = ((bf16[1,16,8,128]{3,2,0,1:T(8,128)(2,1)}), bf16[1,16,8,128]{3,2,0,1:T(8,128)(2,1)S(1)}, u32[]{:S(2)}, u32[]{:S(2)}) async-start(bf16[1,16,8,128]{3,2,0,1:T(8,128)(2,1)} %pad_maximum_fusion.2), calls=%async_computation.2 | async-start | bytes 65536 | tf_op jit(solution)/shard_map/all_to_all | solution.py:26
  274.6 2.8 copy-start.2
  274.6 9.0 %copy-start.1 = (s32[1,128]{1,0:T(1,128)S(1)}, s32[1,128]{1,0:T(1,128)}, u32[]{:S(2)}) copy-start(s32[1,128]{1,0:T(1,128)} %param.13) | copy-start | bytes 1540
  277.5 74.9 %copy-start.3 = (bf16[128,1024]{1,0:T(8,128)(2,1)S(1)}, bf16[128,1024]{1,0:T(8,128)(2,1)}, u32[]{:S(2)}) copy-start(bf16[128,1024]{1,0:T(8,128)(2,1)} %param.10) | copy-start | bytes 786436
  284.2 13.7 %all-to-all-start = ((s32[16,1,128]{2,1,0:T(1,128)}), s32[16,1,128]{2,1,0:T(1,128)S(1)}, u32[]{:S(2)}, u32[]{:S(2)}) async-start(s32[16,1,128]{2,1,0:T(1,128)} %broadcast_in_dim.46), calls=%async_computation | async-start | bytes 16384 | tf_op jit(solution)/shard_map/all_to_all | solution.py:35
  299.0 53.4 %all-to-all-start.3 = ((bf16[16,128,256]{2,1,0:T(8,128)(2,1)}), bf16[16,128,256]{2,1,0:T(8,128)(2,1)S(1)}, u32[]{:S(2)}, u32[]{:S(2)}) async-start(bf16[16,128,256]{2,1,0:T(8,128)(2,1)} %broadcast_in_dim.48), calls=%async_computation.3 | async-start | bytes 2097152 | tf_op jit(solution)/shard_map/all_to_all | solution.py:35
Sparse Core Ops, SparseCore 0:
  11.5 246.2 all-gather.1
where the time goes:
time: 367 us; the launch traced here: 366 us
  waiting for transfers between devices  291 us (79%)
  starting transfers between devices  38.6 us (11%)
  between operations  13.5 us (4%)
  matrix products  11.6 us (3%)
  local copies, waits for them, and re-layouts  6.35 us (2%)
  other arithmetic  5.78 us (2%)
    all_gather x1, waiting for transfers between devices, in_one_piece(): out = lax.all_gather(both, axis, axis=dim, tiled=True)  222 us
    all_to_all x2, waiting for transfers between devices, from_everyone(): return lax.all_to_all(copies, axis, split_axis=0, concat_axis=0, tiled=True)  56.2 us
    all_to_all x1, starting transfers between devices, shards(): lax.all_to_all(vis_slot, 'seq', split_axis=1, concat_axis=0, tiled=True)  16.3 us
    all_to_all x1, starting transfers between devices, side_by_side(): lax.all_to_all(both, axis, split_axis=split_dim, concat_axis=concat_dim,...  12.1 us
    all_to_all x2, starting transfers between devices, from_everyone(): return lax.all_to_all(copies, axis, split_axis=0, concat_axis=0, tiled=True)  10.3 us
    all_to_all x1, waiting for transfers between devices, shards(): lax.all_to_all(vis_slot, 'seq', split_axis=1, concat_axis=0, tiled=True)  7.39 us
  transfers between devices with their start and end apart: 5, of which 5 were waited for; matrix products, arithmetic and copies ran while one was open for 2% of the time, Pallas kernels for 0%

commit v1 on v0

v1 whole, which is shorter than its diff:
```python
import jax
import jax.numpy as jnp
from jax import lax
from jax.experimental import pallas as pl
from jax.experimental.pallas import tpu as pltpu
from jax.sharding import PartitionSpec as P


HEAD = 128
QPK = 8
CAP = 4
NX = 4
NZ = 4
NLO = 8
NS = 16
NT = 4
REACH = 4
AXES = ("grp", "seq", "tp")
OVER_X = [[x * NZ + z for x in range(NX)] for z in range(NZ)]
OVER_Z = [[x * NZ + z for z in range(NZ)] for x in range(NX)]


def seq_permute(array, move):
    pairs = []
    for g in range(NX * NZ):
        for s in range(NS):
            to = move(s // 2, s % 2)
            if to is None:
                continue
            for t in range(NT):
                pairs.append(((g * NS + s) * NT + t, (g * NS + to[0] * 2 + to[1]) * NT + t))
    return lax.ppermute(array, AXES, pairs)


def x_permute(array, d):
    step, size = NZ * NS * NT, NX * NZ * NS * NT
    return lax.ppermute(array, AXES, [(i, (i + d * step) % size) for i in range(size)])


def sibling(z, c):
    return z, 1 - c


def flip(mask):
    return lambda z, c: (z ^ mask, c)


def later(d):
    return lambda z, c: (z + d, c) if z + d < NLO else None


MIB = 1 << 20
IN_VMEM = pl.BlockSpec(memory_space=pltpu.VMEM)


def in_vmem(array):
    return pltpu.with_memory_space_constraint(array, pltpu.VMEM)


def pack(_, text_ref, extra_ref, out_ref):
    tokens = text_ref.shape[0]
    out_ref[:tokens, :] = text_ref[...]
    out_ref[tokens:, :] = extra_ref[...]


def packed(which, hidden, extra):
    tokens, width = hidden.shape
    count = tokens + extra.shape[0]
    part = width // NX
    return pl.pallas_call(
        pack,
        grid_spec=pltpu.PrefetchScalarGridSpec(
            num_scalar_prefetch=1,
            grid=(1,),
            in_specs=[
                pl.BlockSpec((tokens, part), lambda i, at: (0, at[0])),
                pl.BlockSpec((extra.shape[0], part), lambda i, at: (0, at[0])),
            ],
            out_specs=IN_VMEM,
        ),
        out_shape=pltpu.VMEM((count, part), hidden.dtype),
        compiler_params=pltpu.CompilerParams(vmem_limit_bytes=8 * MIB),
        name="pack",
    )(which, hidden, extra)


def project(place_ref, text_ref, extra_ref, *refs):
    *moved_refs, mine_ref, other_ref, out_ref, weights_ref = refs
    steps, sources, part, cols = mine_ref.shape
    tokens = text_ref.shape[0]
    s, x = place_ref[0], place_ref[1]
    core, chip = lax.rem(s, 2), lax.rem(s // 2, 4)
    for side, ref in enumerate((mine_ref, other_ref)):
        at = pl.ds(pl.multiple_of(jnp.where(core == side, 0, cols), cols), cols)
        for k in range(steps):
            piece = 2 * lax.rem(chip // 2 + k // 2, 2) + lax.rem(chip + k % 2, 2)
            for z in range(sources):
                row = pl.ds(pl.multiple_of(z * steps * part + piece * part, part), part)
                weights_ref[row, at] = ref[k, z]
    weights = weights_ref[...]
    out_ref[x, :tokens, :] = jnp.dot(text_ref[...], weights, preferred_element_type=jnp.float32)
    out_ref[x, tokens:, :] = jnp.dot(extra_ref[...], weights, preferred_element_type=jnp.float32)
    for d, ref in enumerate(moved_refs, 1):
        out_ref[lax.rem(x + NX - d, NX)] = jnp.dot(
            ref[...], weights, preferred_element_type=jnp.float32
        )


def projection(place, hidden, extra, moved, mine, other):
    tokens, width = hidden.shape
    count = tokens + extra.shape[0]
    part = width // NX
    cols = 2 * mine.shape[-1]
    return pl.pallas_call(
        project,
        grid_spec=pltpu.PrefetchScalarGridSpec(
            num_scalar_prefetch=1,
            grid=(1,),
            in_specs=[
                pl.BlockSpec((tokens, part), lambda i, at: (0, at[1])),
                pl.BlockSpec((extra.shape[0], part), lambda i, at: (0, at[1])),
            ]
            + [IN_VMEM] * (len(moved) + 2),
            out_specs=IN_VMEM,
            scratch_shapes=[pltpu.VMEM((part, cols), jnp.bfloat16)],
        ),
        out_shape=pltpu.VMEM((NX, count, cols), jnp.float32),
        compiler_params=pltpu.CompilerParams(vmem_limit_bytes=16 * MIB),
        name="project",
    )(place, hidden, extra, *map(in_vmem, (*moved, mine, other)))


def merge(sums_ref, vis_ref, docs_ref, out_ref):
    tokens, cols = sums_ref.shape[1:]
    text = jnp.sum(sums_ref[...], axis=0)
    slots = vis_ref[:, cols:].astype(jnp.float32)
    matches = slots == lax.broadcasted_iota(jnp.int32, slots.shape, 1).astype(jnp.float32)
    chooser = matches.astype(jnp.float32).astype(jnp.bfloat16)
    dims = (((0,), (0,)), ((), ()))
    moved = lax.dot_general(chooser, vis_ref[:, :cols], dims, preferred_element_type=jnp.float32)
    ones = jnp.ones((slots.shape[0], cols), jnp.bfloat16)
    used = lax.dot_general(chooser, ones, dims, preferred_element_type=jnp.float32)
    out_ref[:tokens, :] = jnp.where(used > 0.5, moved, text).astype(jnp.bfloat16)
    out_ref[tokens:, :] = docs_ref[...]


def merged_block(sums, vis, docs):
    _, tokens, cols = sums.shape
    extra = docs.shape[0]
    return pl.pallas_call(
        merge,
        in_specs=[IN_VMEM] * 3,
        out_specs=IN_VMEM,
        out_shape=pltpu.VMEM((tokens + extra, cols), jnp.bfloat16),
        compiler_params=pltpu.CompilerParams(vmem_limit_bytes=8 * MIB),
        name="merge",
    )(in_vmem(sums), in_vmem(vis), docs)


def attend(place_ref, q_ref, mine_ref, other_ref, my_docs_ref, out_ref, bias_ref, keys_ref, values_ref):
    tokens = q_ref.shape[0]
    blocks = mine_ref.shape[0]

    @pl.when(pl.program_id(0) == 0)
    def _():
        s = place_ref[0]
        core, chip = lax.rem(s, 2), s // 2
        my_docs = jnp.broadcast_to(my_docs_ref[...], (tokens, tokens))
        row = lax.broadcasted_iota(jnp.int32, (tokens, tokens), 0) + s * tokens
        col = lax.broadcasted_iota(jnp.int32, (tokens, tokens), 1)
        for side, ref in enumerate((mine_ref, other_ref)):
            for d in range(blocks):
                block = 2 * (chip - d) + (core if side == 0 else 1 - core)
                docs = ref[d, tokens : tokens + 8, :tokens].astype(jnp.float32)[:1]
                spot = col + block * tokens
                allowed = (docs == my_docs) & (spot <= row) & (spot >= 0)
                at = (side * blocks + d) * tokens
                bias_ref[:, at : at + tokens] = jnp.where(allowed, 0.0, -1e30)
                keys_ref[at : at + tokens, :] = ref[d, :tokens, :HEAD]
                values_ref[at : at + tokens, :] = ref[d, :tokens, HEAD:]

    scale = 1.0 / jnp.sqrt(jnp.float32(HEAD))
    scores = lax.dot_general(
        q_ref[...], keys_ref[...], (((1,), (1,)), ((), ())), preferred_element_type=jnp.float32
    )
    scores = scores * scale + bias_ref[...]
    top = jnp.max(scores, axis=1, keepdims=True)
    weights = jnp.exp(scores - top)
    total = jnp.sum(weights, axis=1, keepdims=True)
    mixed = jnp.dot(weights.astype(jnp.bfloat16), values_ref[...], preferred_element_type=jnp.float32)
    out_ref[...] = (mixed / total).astype(out_ref.dtype)


def attention(place, queries, mine, other, my_docs):
    tokens = queries.shape[0]
    span = 2 * mine.shape[0] * tokens
    return pl.pallas_call(
        attend,
        grid_spec=pltpu.PrefetchScalarGridSpec(
            num_scalar_prefetch=1,
            grid=(QPK,),
            in_specs=[
                pl.BlockSpec((tokens, HEAD), lambda h, *_: (0, h)),
                IN_VMEM,
                IN_VMEM,
                IN_VMEM,
            ],
            out_specs=pl.BlockSpec((tokens, HEAD), lambda h, *_: (0, h)),
            scratch_shapes=[
                pltpu.VMEM((tokens, span), jnp.float32),
                pltpu.VMEM((span, HEAD), jnp.bfloat16),
                pltpu.VMEM((span, HEAD), jnp.bfloat16),
            ],
        ),
        out_shape=jax.ShapeDtypeStruct(queries.shape, jnp.bfloat16),
        compiler_params=pltpu.CompilerParams(vmem_limit_bytes=16 * MIB),
        name="attend",
    )(place, queries, in_vmem(mine), in_vmem(other), my_docs)


def exchange_x(array):
    return lax.all_to_all(array, "grp", 0, 0, axis_index_groups=OVER_X, tiled=True)


def program(hidden, queries, vis_rows, vis_slot, doc_ids, w_key, w_value):
    tokens, width = hidden.shape
    cols = 2 * w_key.shape[1]
    place = lax.axis_index("seq")
    core, chip = place % 2, place // 2
    x = lax.axis_index("grp") // NZ
    where = jnp.stack([place, x])

    part = w_key.shape[0] // 4
    start = (chip % 4) * part
    piece = jnp.where(
        core == 0,
        lax.dynamic_slice_in_dim(w_key, start, part, axis=0),
        lax.dynamic_slice_in_dim(w_value, start, part, axis=0),
    )
    got = lax.all_to_all(
        jnp.broadcast_to(piece, (NZ, *piece.shape)), "grp", 0, 0, axis_index_groups=OVER_Z, tiled=True
    )

    extra = vis_rows.reshape(-1, width)
    moved = {}
    for d in (2, 1, 3):
        part_d = packed(((x + d) % NX).reshape(1), hidden, extra)
        moved[d] = x_permute(part_d, d)

    near = seq_permute(got, flip(1))
    pair = jnp.stack([got, near])
    far = seq_permute(pair, flip(2))
    four = jnp.concatenate([pair, far])
    rest = seq_permute(four, sibling)

    sums = exchange_x(projection(where, hidden, extra, [moved[d] for d in (1, 2, 3)], four, rest))
    vis = jnp.sum(sums[:, tokens:], axis=0).astype(jnp.bfloat16).reshape(NS, CAP, cols)
    marks = jnp.broadcast_to(vis_slot.reshape(NS, CAP, 1), (NS, CAP, tokens)).astype(jnp.bfloat16)
    vis = lax.all_to_all(jnp.concatenate([vis, marks], axis=2), "seq", 0, 0, tiled=True)
    docs = jnp.broadcast_to(jnp.tile(doc_ids, (1, cols // tokens)), (8, cols)).astype(jnp.bfloat16)
    block = merged_block(sums[:, :tokens], vis.reshape(NS * CAP, -1), docs)

    back = [seq_permute(block, later(d)) for d in range(1, REACH + 1)]
    mine = jnp.stack([block, *back])
    other = seq_permute(mine, sibling)
    my_docs = doc_ids.reshape(tokens, 1).astype(jnp.float32)
    return attention(where, queries, mine, other, my_docs)


def solution(mesh):
    return jax.shard_map(
        program,
        mesh=mesh,
        in_specs=(
            P(("grp", "seq"), None),
            P(("grp", "seq"), "tp"),
            P(("grp", "seq"), None, None, None),
            P(("grp", "seq"), None, None),
            P("grp", "seq"),
            P("grp", "tp"),
            P("grp", "tp"),
        ),
        out_specs=P(("grp", "seq"), "tp"),
        check_vma=False,
    )
```

time: 367 us -> 173 us (0.47)
  the two profiles are of different devices: /device:TPU:33 before, /device:TPU:97 now
where the time goes in v1:
time: 173 us; the launch traced here: 172 us
  waiting for transfers between devices  54 us (31%)
  blocking collectives  51.4 us (30%)
  starting transfers between devices  48.6 us (28%)
  Pallas kernels  11.9 us (7%)
  other arithmetic  3.41 us (2%)
  local copies, waits for them, and re-layouts  2.66 us (2%)
    all_to_all x1, blocking collectives, program(): lax.all_to_all(jnp.broadcast_to(piece, (NZ, *piece.shape)), 'grp', 0, 0,...  51.4 us
    ppermute x8, starting transfers between devices, seq_permute(): return lax.ppermute(array, AXES, pairs)  26.1 us
    ppermute x3, waiting for transfers between devices, x_permute(): lax.ppermute(array, AXES, [(i, (i + d * step) % size) for i in range(size)])  20.9 us
    ppermute x8, waiting for transfers between devices, seq_permute(): return lax.ppermute(array, AXES, pairs)  14.9 us
    all_to_all x1, waiting for transfers between devices, exchange_x(): lax.all_to_all(array, 'grp', 0, 0, axis_index_groups=OVER_X, tiled=True)  11.1 us
    ppermute x3, starting transfers between devices, x_permute(): lax.ppermute(array, AXES, [(i, (i + d * step) % size) for i in range(size)])  10.5 us
    all_to_all x1, starting transfers between devices, program(): lax.all_to_all(jnp.concatenate([vis, marks], axis=2), 'seq', 0, 0, tiled=...  7.22 us
    all_to_all x1, waiting for transfers between devices, program(): lax.all_to_all(jnp.concatenate([vis, marks], axis=2), 'seq', 0, 0, tiled=...  7.14 us
  transfers between devices with their start and end apart: 13, of which 9 were waited for; matrix products, arithmetic and copies ran while one was open for 2% of the time, Pallas kernels for 1%

profile of v1, /device:TPU:97, one launch (start us, length us, event | category | flops | bytes accessed | tf_op | source)
XLA Modules:
  0.0 172.3 jit_solution(16651024600227951339)
XLA Ops:
  0.0 0.0 copy-start
  0.0 0.9 dynamic-slice_select_fusion
  1.0 51.4 %all_to_all.15 = bf16[4,128,128]{2,1,0:T(8,128)(2,1)S(1)} all-to-all(bf16[4,128,128]{2,1,0:T(8,128)(2,1)S(1)} %broadcast_in_dim.6), channel_id=1, replica_groups={{0,64,128,192},{256,320,384,448},{512,576,640,704},{768,832,896,960},{1..., dimensions={0} | all-to-all | bytes 262144 | tf_op jit(solution)/shard_map/all_to_all | solution.py:240
  52.3 1.9 %collective-permute-start.3 = (bf16[4,128,128]{2,1,0:T(8,128)(2,1)S(1)}, bf16[4,128,128]{2,1,0:T(8,128)(2,1)S(1)}, u32[]{:S(2)}, u32[]{:S(2)}) collective-permute-start(bf16[4,128,128]{2,1,0:T(8,128)(2,1)S(1)} %all_to_all.15), channel_id=1, source_target_pairs={{0,8},{1,9},{2,10},{3,11},{4,12},{5,13},{6,14},{7,15},{8,0},{9,1},... | collective-permute-start | bytes 393224 | tf_op jit(solution)/shard_map/ppermute | solution.py:32
  54.2 3.8 %collective-permute-done.3 = bf16[4,128,128]{2,1,0:T(8,128)(2,1)S(1)} collective-permute-done((bf16[4,128,128]{2,1,0:T(8,128)(2,1)S(1)}, bf16[4,128,128]{2,1,0:T(8,128)(2,1)S(1)}, u32[]{:S(2)}, u32[]{:S(2)}) %collective-permute-start.3) | collective-permute-done | bytes 131104 | tf_op jit(solution)/shard_map/ppermute | solution.py:32
  58.0 0.7 pad_maximum_fusion.1
  58.8 4.9 %collective-permute-start.4 = (bf16[2,4,128,128]{3,2,1,0:T(8,128)(2,1)}, bf16[2,4,128,128]{3,2,1,0:T(8,128)(2,1)}, u32[]{:S(2)}, u32[]{:S(2)}) collective-permute-start(bf16[2,4,128,128]{3,2,1,0:T(8,128)(2,1)} %pad_maximum_fusion.1), channel_id=1, source_target_pairs={{0,16},{1,17},{2,18},{3,19},{4,20},{5,21},{6,22},{7,23},{8,24},{9,... | collective-permute-start | bytes 786440 | tf_op jit(solution)/shard_map/ppermute | solution.py:32
  63.6 1.3 reshape.43.extra_ref
  65.0 0.0 copy-done
  65.0 0.9 pack.3
  66.0 3.1 %collective-permute-start = (bf16[192,2048]{1,0:T(8,128)(2,1)}, bf16[192,2048]{1,0:T(8,128)(2,1)}, u32[]{:S(2)}, u32[]{:S(2)}) collective-permute-start(bf16[192,2048]{1,0:T(8,128)(2,1)} %pack.3), channel_id=1, source_target_pairs={{0,256},{1,257},{2,258},{3,259},{4,260},{5,261},{6,262},{7,263},{8... | collective-permute-start | bytes 2359304 | tf_op jit(solution)/shard_map/ppermute | solution.py:37
  69.1 0.9 pack.4
  70.0 4.3 %collective-permute-start.1 = (bf16[192,2048]{1,0:T(8,128)(2,1)}, bf16[192,2048]{1,0:T(8,128)(2,1)}, u32[]{:S(2)}, u32[]{:S(2)}) collective-permute-start(bf16[192,2048]{1,0:T(8,128)(2,1)} %pack.4), channel_id=1, source_target_pairs={{0,512},{1,513},{2,514},{3,515},{4,516},{5,517},{6,518},{7,519},{8... | collective-permute-start | bytes 2359304 | tf_op jit(solution)/shard_map/ppermute | solution.py:37
  74.4 0.1 pack.5
  74.5 3.1 %collective-permute-start.2 = (bf16[192,2048]{1,0:T(8,128)(2,1)S(1)}, bf16[192,2048]{1,0:T(8,128)(2,1)S(1)}, u32[]{:S(2)}, u32[]{:S(2)}) collective-permute-start(bf16[192,2048]{1,0:T(8,128)(2,1)S(1)} %pack.5), channel_id=1, source_target_pairs={{0,768},{1,769},{2,770},{3,771},{4,772},{5,773},{6,774},{7,775},{8... | collective-permute-start | bytes 2359304 | tf_op jit(solution)/shard_map/ppermute | solution.py:37
  77.5 0.0 collective-permute-done.4
  77.5 1.0 pad_maximum_fusion.refs_3_
  78.6 8.5 %collective-permute-start.5 = (bf16[4,4,128,128]{3,2,1,0:T(8,128)(2,1)S(1)}, bf16[4,4,128,128]{3,2,1,0:T(8,128)(2,1)S(1)}, u32[]{:S(2)}, u32[]{:S(2)}) collective-permute-start(bf16[4,4,128,128]{3,2,1,0:T(8,128)(2,1)S(1)} %pad_maximum_fusion.refs_3_), channel_id=1, source_target_pairs={{0,4},{1,5},{2,6},{3,7},{4,0},{5,1},{6,2},{7,3},{8,12},{9,13},{10,... | collective-permute-start | bytes 1572872 | tf_op jit(solution)/shard_map/ppermute | solution.py:32
  87.1 0.1 pad_add_fusion.place_ref
  87.1 0.0 copy-start.3
  87.1 0.0 collective-permute-done.refs_0_
  87.1 13.4 %collective-permute-done.1.refs_1_ = bf16[192,2048]{1,0:T(8,128)(2,1)} collective-permute-done((bf16[192,2048]{1,0:T(8,128)(2,1)}, bf16[192,2048]{1,0:T(8,128)(2,1)}, u32[]{:S(2)}, u32[]{:S(2)}) %collective-permute-start.1) | collective-permute-done | bytes 786464 | tf_op jit(solution)/shard_map/ppermute | solution.py:37
  100.6 7.4 %collective-permute-done.2.refs_2_ = bf16[192,2048]{1,0:T(8,128)(2,1)S(1)} collective-permute-done((bf16[192,2048]{1,0:T(8,128)(2,1)S(1)}, bf16[192,2048]{1,0:T(8,128)(2,1)S(1)}, u32[]{:S(2)}, u32[]{:S(2)}) %collective-permute-start.2) | collective-permute-done | bytes 786464 | tf_op jit(solution)/shard_map/ppermute | solution.py:37
  108.0 0.0 collective-permute-done.5.refs_4_
  108.0 3.2 %project.1 = f32[4,192,256]{2,1,0:T(8,128)S(1)} custom-call(s32[2]{0:T(128)S(1)} %pad_add_fusion.place_ref, bf16[128,8192]{1,0:T(8,128)(2,1)S(1)} %copy-done, bf16[64,8192]{1,0:T(8,128)(2,1)S(1)} %reshape.43.extra_ref, bf16[192,2048]{1,0:T(8,128)(2,1)} %collective-permute-done.refs_0_, bf16[192,2048]{1,0:T(8,128)(2,1)} %collective-permute-done.1.refs_1_, ...), custom_call_target="tpu_custom_call" | custom-call | tf_op jit(solution)/shard_map/project/pallas_call | solution.py:114
  111.2 0.0 copy-start.1
  111.2 0.9 copy-done.1
  112.1 0.0 copy-start.4
  112.1 0.0 copy-start.2
  112.1 4.8 %all-to-all-start.1 = ((f32[4,192,256]{2,1,0:T(8,128)}), f32[4,192,256]{2,1,0:T(8,128)S(1)}, u32[]{:S(2)}, u32[]{:S(2)}) async-start(f32[4,192,256]{2,1,0:T(8,128)} %copy-done.1), calls=%async_computation.1 | async-start | bytes 1572864 | tf_op jit(solution)/shard_map/all_to_all | solution.py:222
  116.9 0.0 copy-done.3
  116.9 0.1 copy.8
  117.0 11.1 %all-to-all-done.1 = f32[4,192,256]{2,1,0:T(8,128)S(1)} async-done(((f32[4,192,256]{2,1,0:T(8,128)}), f32[4,192,256]{2,1,0:T(8,128)S(1)}, u32[]{:S(2)}, u32[]{:S(2)}) %all-to-all-start.1) | async-done | bytes 786464 | tf_op jit(solution)/shard_map/all_to_all | solution.py:222
  128.2 0.1 broadcast_in_dim.14
  128.3 0.6 pad_maximum_fusion.2
  128.9 7.2 %all-to-all-start.2 = ((bf16[16,4,384]{2,1,0:T(4,128)(2,1)}), bf16[16,4,384]{2,1,0:T(4,128)(2,1)S(1)}, u32[]{:S(2)}, u32[]{:S(2)}) async-start(bf16[16,4,384]{2,1,0:T(4,128)(2,1)} %pad_maximum_fusion.2), calls=%async_computation.2 | async-start | bytes 98304 | tf_op jit(solution)/shard_map/all_to_all | solution.py:259
  136.1 0.0 copy-done.4
  136.2 7.1 %all-to-all-done.2 = bf16[16,4,384]{2,1,0:T(4,128)(2,1)S(1)} async-done(((bf16[16,4,384]{2,1,0:T(4,128)(2,1)}), bf16[16,4,384]{2,1,0:T(4,128)(2,1)S(1)}, u32[]{:S(2)}, u32[]{:S(2)}) %all-to-all-start.2) | async-done | bytes 49184 | tf_op jit(solution)/shard_map/all_to_all | solution.py:259
  143.4 0.2 merge.1
  143.6 2.2 %collective-permute-start.6 = (bf16[136,256]{1,0:T(8,128)(2,1)S(1)}, bf16[136,256]{1,0:T(8,128)(2,1)S(1)}, u32[]{:S(2)}, u32[]{:S(2)}) collective-permute-start(bf16[136,256]{1,0:T(8,128)(2,1)S(1)} %merge.1), channel_id=1, source_target_pairs={{0,8},{1,9},{2,10},{3,11},{4,12},{5,13},{6,14},{7,15},{8,16},{9,17... | collective-permute-start | bytes 208904 | tf_op jit(solution)/shard_map/ppermute | solution.py:32
  145.8 2.3 %collective-permute-start.7 = (bf16[136,256]{1,0:T(8,128)(2,1)S(1)}, bf16[136,256]{1,0:T(8,128)(2,1)S(1)}, u32[]{:S(2)}, u32[]{:S(2)}) collective-permute-start(bf16[136,256]{1,0:T(8,128)(2,1)S(1)} %merge.1), channel_id=1, source_target_pairs={{0,16},{1,17},{2,18},{3,19},{4,20},{5,21},{6,22},{7,23},{8,24},{9,... | collective-permute-start | bytes 208904 | tf_op jit(solution)/shard_map/ppermute | solution.py:32
  148.1 2.3 %collective-permute-start.8 = (bf16[136,256]{1,0:T(8,128)(2,1)S(1)}, bf16[136,256]{1,0:T(8,128)(2,1)S(1)}, u32[]{:S(2)}, u32[]{:S(2)}) collective-permute-start(bf16[136,256]{1,0:T(8,128)(2,1)S(1)} %merge.1), channel_id=1, source_target_pairs={{0,24},{1,25},{2,26},{3,27},{4,28},{5,29},{6,30},{7,31},{8,32},{9,... | collective-permute-start | bytes 208904 | tf_op jit(solution)/shard_map/ppermute | solution.py:32
  150.4 1.3 collective-permute-start.9
  151.7 0.0 collective-permute-done.6
  151.8 0.1 collective-permute-done.7
  151.8 3.1 %collective-permute-done.8 = bf16[136,256]{1,0:T(8,128)(2,1)S(1)} collective-permute-done((bf16[136,256]{1,0:T(8,128)(2,1)S(1)}, bf16[136,256]{1,0:T(8,128)(2,1)S(1)}, u32[]{:S(2)}, u32[]{:S(2)}) %collective-permute-start.8) | collective-permute-done | bytes 69664 | tf_op jit(solution)/shard_map/ppermute | solution.py:32
  155.0 6.7 %collective-permute-done.9 = bf16[136,256]{1,0:T(8,128)(2,1)S(1)} collective-permute-done((bf16[136,256]{1,0:T(8,128)(2,1)S(1)}, bf16[136,256]{1,0:T(8,128)(2,1)S(1)}, u32[]{:S(2)}, u32[]{:S(2)}) %collective-permute-start.9) | collective-permute-done | bytes 69664 | tf_op jit(solution)/shard_map/ppermute | solution.py:32
  161.8 2.7 %collective-permute-start.10 = (bf16[5,136,256]{2,1,0:T(8,128)(2,1)S(1)}, bf16[5,136,256]{2,1,0:T(8,128)(2,1)S(1)}, u32[]{:S(2)}, u32[]{:S(2)}) collective-permute-start(bf16[5,136,256]{2,1,0:T(8,128)(2,1)S(1)} %bitcast_dynamic-update-slice_fusion.mine_ref), channel_id=1, source_target_pairs={{0,4},{1,5},{2,6},{3,7},{4,0},{5,1},{6,2},{7,3},{8,12},{9,13},{10,... | collective-permute-start | bytes 1044488 | tf_op jit(solution)/shard_map/ppermute | solution.py:32
  164.5 0.1 copy.9.my_docs_ref
  164.6 1.1 collective-permute-done.10.other_ref
  165.7 0.0 copy-done.2
  165.7 6.6 %attend.1 = bf16[128,1024]{1,0:T(8,128)(2,1)} custom-call(s32[2]{0:T(128)S(1)} %pad_add_fusion.place_ref, bf16[128,1024]{1,0:T(8,128)(2,1)S(1)} %copy-done.2, bf16[5,136,256]{2,1,0:T(8,128)(2,1)S(1)} %bitcast_dynamic-update-slice_fusion.mine_ref, bf16[5,136,256]{2,1,0:T(8,128)(2,1)S(1)} %collective-permute-done.10.other_ref, f32[128,1]{1,0:T(8,128)S(1)} %copy.9.my_docs_ref), custom_call_target="tpu_custom_call" | custom-call | tf_op jit(solution)/shard_map/attend/pallas_call | solution.py:197
  (14 shorter events, 0.2 us)
Async XLA Ops:
  0.0 65.0 %copy-start = (bf16[128,8192]{1,0:T(8,128)(2,1)S(1)}, bf16[128,8192]{1,0:T(8,128)(2,1)}, u32[]{:S(2)}) copy-start(bf16[128,8192]{1,0:T(8,128)(2,1)} %text_ref.7) | copy-start | bytes 6291460
  52.3 5.7 %collective-permute-start.3 = (bf16[4,128,128]{2,1,0:T(8,128)(2,1)S(1)}, bf16[4,128,128]{2,1,0:T(8,128)(2,1)S(1)}, u32[]{:S(2)}, u32[]{:S(2)}) collective-permute-start(bf16[4,128,128]{2,1,0:T(8,128)(2,1)S(1)} %all_to_all.15), channel_id=1, source_target_pairs={{0,8},{1,9},{2,10},{3,11},{4,12},{5,13},{6,14},{7,15},{8,0},{9,1},... | collective-permute-start | bytes 393224 | tf_op jit(solution)/shard_map/ppermute | solution.py:32
  58.8 18.8 %collective-permute-start.4 = (bf16[2,4,128,128]{3,2,1,0:T(8,128)(2,1)}, bf16[2,4,128,128]{3,2,1,0:T(8,128)(2,1)}, u32[]{:S(2)}, u32[]{:S(2)}) collective-permute-start(bf16[2,4,128,128]{3,2,1,0:T(8,128)(2,1)} %pad_maximum_fusion.1), channel_id=1, source_target_pairs={{0,16},{1,17},{2,18},{3,19},{4,20},{5,21},{6,22},{7,23},{8,24},{9,... | collective-permute-start | bytes 786440 | tf_op jit(solution)/shard_map/ppermute | solution.py:32
  66.0 21.2 %collective-permute-start = (bf16[192,2048]{1,0:T(8,128)(2,1)}, bf16[192,2048]{1,0:T(8,128)(2,1)}, u32[]{:S(2)}, u32[]{:S(2)}) collective-permute-start(bf16[192,2048]{1,0:T(8,128)(2,1)} %pack.3), channel_id=1, source_target_pairs={{0,256},{1,257},{2,258},{3,259},{4,260},{5,261},{6,262},{7,263},{8... | collective-permute-start | bytes 2359304 | tf_op jit(solution)/shard_map/ppermute | solution.py:37
  70.0 30.5 %collective-permute-start.1 = (bf16[192,2048]{1,0:T(8,128)(2,1)}, bf16[192,2048]{1,0:T(8,128)(2,1)}, u32[]{:S(2)}, u32[]{:S(2)}) collective-permute-start(bf16[192,2048]{1,0:T(8,128)(2,1)} %pack.4), channel_id=1, source_target_pairs={{0,512},{1,513},{2,514},{3,515},{4,516},{5,517},{6,518},{7,519},{8... | collective-permute-start | bytes 2359304 | tf_op jit(solution)/shard_map/ppermute | solution.py:37
  74.5 33.5 %collective-permute-start.2 = (bf16[192,2048]{1,0:T(8,128)(2,1)S(1)}, bf16[192,2048]{1,0:T(8,128)(2,1)S(1)}, u32[]{:S(2)}, u32[]{:S(2)}) collective-permute-start(bf16[192,2048]{1,0:T(8,128)(2,1)S(1)} %pack.5), channel_id=1, source_target_pairs={{0,768},{1,769},{2,770},{3,771},{4,772},{5,773},{6,774},{7,775},{8... | collective-permute-start | bytes 2359304 | tf_op jit(solution)/shard_map/ppermute | solution.py:37
  78.6 29.4 %collective-permute-start.5 = (bf16[4,4,128,128]{3,2,1,0:T(8,128)(2,1)S(1)}, bf16[4,4,128,128]{3,2,1,0:T(8,128)(2,1)S(1)}, u32[]{:S(2)}, u32[]{:S(2)}) collective-permute-start(bf16[4,4,128,128]{3,2,1,0:T(8,128)(2,1)S(1)} %pad_maximum_fusion.refs_3_), channel_id=1, source_target_pairs={{0,4},{1,5},{2,6},{3,7},{4,0},{5,1},{6,2},{7,3},{8,12},{9,13},{10,... | collective-permute-start | bytes 1572872 | tf_op jit(solution)/shard_map/ppermute | solution.py:32
  87.1 29.8 %copy-start.3 = (s32[1,16,4]{1,2,0:T(4,128)S(1)}, s32[1,16,4]{1,2,0:T(4,128)}, u32[]{:S(2)}) copy-start(s32[1,16,4]{1,2,0:T(4,128)} %param.10) | copy-start | bytes 772
  111.2 0.9 copy-start.1
  112.1 24.0 %copy-start.4 = (s32[1,128]{1,0:T(1,128)S(1)}, s32[1,128]{1,0:T(1,128)}, u32[]{:S(2)}) copy-start(s32[1,128]{1,0:T(1,128)} %param.11) | copy-start | bytes 1540
  112.1 53.6 %copy-start.2 = (bf16[128,1024]{1,0:T(8,128)(2,1)S(1)}, bf16[128,1024]{1,0:T(8,128)(2,1)}, u32[]{:S(2)}) copy-start(bf16[128,1024]{1,0:T(8,128)(2,1)} %q_ref.1) | copy-start | bytes 786436
  112.1 16.0 %all-to-all-start.1 = ((f32[4,192,256]{2,1,0:T(8,128)}), f32[4,192,256]{2,1,0:T(8,128)S(1)}, u32[]{:S(2)}, u32[]{:S(2)}) async-start(f32[4,192,256]{2,1,0:T(8,128)} %copy-done.1), calls=%async_computation.1 | async-start | bytes 1572864 | tf_op jit(solution)/shard_map/all_to_all | solution.py:222
  128.9 14.4 %all-to-all-start.2 = ((bf16[16,4,384]{2,1,0:T(4,128)(2,1)}), bf16[16,4,384]{2,1,0:T(4,128)(2,1)S(1)}, u32[]{:S(2)}, u32[]{:S(2)}) async-start(bf16[16,4,384]{2,1,0:T(4,128)(2,1)} %pad_maximum_fusion.2), calls=%async_computation.2 | async-start | bytes 98304 | tf_op jit(solution)/shard_map/all_to_all | solution.py:259
  143.6 8.2 %collective-permute-start.6 = (bf16[136,256]{1,0:T(8,128)(2,1)S(1)}, bf16[136,256]{1,0:T(8,128)(2,1)S(1)}, u32[]{:S(2)}, u32[]{:S(2)}) collective-permute-start(bf16[136,256]{1,0:T(8,128)(2,1)S(1)} %merge.1), channel_id=1, source_target_pairs={{0,8},{1,9},{2,10},{3,11},{4,12},{5,13},{6,14},{7,15},{8,16},{9,17... | collective-permute-start | bytes 208904 | tf_op jit(solution)/shard_map/ppermute | solution.py:32
  145.8 6.0 %collective-permute-start.7 = (bf16[136,256]{1,0:T(8,128)(2,1)S(1)}, bf16[136,256]{1,0:T(8,128)(2,1)S(1)}, u32[]{:S(2)}, u32[]{:S(2)}) collective-permute-start(bf16[136,256]{1,0:T(8,128)(2,1)S(1)} %merge.1), channel_id=1, source_target_pairs={{0,16},{1,17},{2,18},{3,19},{4,20},{5,21},{6,22},{7,23},{8,24},{9,... | collective-permute-start | bytes 208904 | tf_op jit(solution)/shard_map/ppermute | solution.py:32
  148.1 6.9 %collective-permute-start.8 = (bf16[136,256]{1,0:T(8,128)(2,1)S(1)}, bf16[136,256]{1,0:T(8,128)(2,1)S(1)}, u32[]{:S(2)}, u32[]{:S(2)}) collective-permute-start(bf16[136,256]{1,0:T(8,128)(2,1)S(1)} %merge.1), channel_id=1, source_target_pairs={{0,24},{1,25},{2,26},{3,27},{4,28},{5,29},{6,30},{7,31},{8,32},{9,... | collective-permute-start | bytes 208904 | tf_op jit(solution)/shard_map/ppermute | solution.py:32
  150.4 11.3 %collective-permute-start.9 = (bf16[136,256]{1,0:T(8,128)(2,1)S(1)}, bf16[136,256]{1,0:T(8,128)(2,1)S(1)}, u32[]{:S(2)}, u32[]{:S(2)}) collective-permute-start(bf16[136,256]{1,0:T(8,128)(2,1)S(1)} %merge.1), channel_id=1, source_target_pairs={{0,32},{1,33},{2,34},{3,35},{4,36},{5,37},{6,38},{7,39},{8,40},{9,... | collective-permute-start | bytes 208904 | tf_op jit(solution)/shard_map/ppermute | solution.py:32
  161.8 4.0 %collective-permute-start.10 = (bf16[5,136,256]{2,1,0:T(8,128)(2,1)S(1)}, bf16[5,136,256]{2,1,0:T(8,128)(2,1)S(1)}, u32[]{:S(2)}, u32[]{:S(2)}) collective-permute-start(bf16[5,136,256]{2,1,0:T(8,128)(2,1)S(1)} %bitcast_dynamic-update-slice_fusion.mine_ref), channel_id=1, source_target_pairs={{0,4},{1,5},{2,6},{3,7},{4,0},{5,1},{6,2},{7,3},{8,12},{9,13},{10,... | collective-permute-start | bytes 1044488 | tf_op jit(solution)/shard_map/ppermute | solution.py:32

commit v2 on v1

v2 whole, which is shorter than its diff:
```python
import jax
import jax.numpy as jnp
from jax import lax
from jax.experimental import pallas as pl
from jax.experimental.pallas import tpu as pltpu
from jax.sharding import PartitionSpec as P


HEAD = 128
QPK = 8
CAP = 4
HEADS_STEP = 4
NX = 4
NZ = 4
NLO = 8
NS = 16
NT = 4
REACH = 4
AXES = ("grp", "seq", "tp")
OVER_X = [[x * NZ + z for x in range(NX)] for z in range(NZ)]
OVER_X_SEQ = [[(x * NZ + z) * NS + s for x in range(NX) for s in range(NS)] for z in range(NZ)]
OVER_Z = [[x * NZ + z for z in range(NZ)] for x in range(NX)]


def seq_permute(array, move):
    pairs = []
    for g in range(NX * NZ):
        for s in range(NS):
            to = move(s // 2, s % 2)
            if to is None:
                continue
            for t in range(NT):
                pairs.append(((g * NS + s) * NT + t, (g * NS + to[0] * 2 + to[1]) * NT + t))
    return lax.ppermute(array, AXES, pairs)


def x_permute(array, d):
    step, size = NZ * NS * NT, NX * NZ * NS * NT
    return lax.ppermute(array, AXES, [(i, (i + d * step) % size) for i in range(size)])


def sibling(z, c):
    return z, 1 - c


def flip(mask):
    return lambda z, c: (z ^ mask, c)


def later(d):
    return lambda z, c: (z + d, c) if z + d < NLO else None


MIB = 1 << 20
IN_VMEM = pl.BlockSpec(memory_space=pltpu.VMEM)


def in_vmem(array):
    return pltpu.with_memory_space_constraint(array, pltpu.VMEM)


def in_hbm(array):
    return pltpu.with_memory_space_constraint(array, pltpu.HBM)


def pack(text_ref, extra_ref, out_ref):
    tokens = text_ref.shape[0]
    out_ref[0, :tokens, :] = text_ref[...]
    out_ref[0, tokens:, :] = extra_ref[0].reshape(NS * CAP, -1)


def packed(hidden, vis_rows):
    tokens, width = hidden.shape
    count = tokens + NS * CAP
    part = width // NX
    return pl.pallas_call(
        pack,
        grid=(NX,),
        in_specs=[
            pl.BlockSpec((tokens, part), lambda i: (0, i)),
            pl.BlockSpec((1, NS, CAP, part), lambda i: (0, 0, 0, i)),
        ],
        out_specs=pl.BlockSpec((1, count, part), lambda i: (i, 0, 0)),
        out_shape=pltpu.HBM((NX, count, part), hidden.dtype),
        compiler_params=pltpu.CompilerParams(vmem_limit_bytes=16 * MIB),
        name="pack",
    )(in_hbm(hidden), in_hbm(vis_rows))


def project(place_ref, rows_ref, mine_ref, other_ref, marks_ref, vis_ref, *refs):
    *text_refs, weights_ref = refs
    steps, sources, part, cols = mine_ref.shape
    tokens = text_refs[0].shape[0]
    s, x = place_ref[0], place_ref[1]
    core, chip = lax.rem(s, 2), lax.rem(s // 2, 4)
    for side, ref in enumerate((mine_ref, other_ref)):
        at = pl.ds(pl.multiple_of(jnp.where(core == side, 0, cols), cols), cols)
        for k in range(steps):
            piece = 2 * lax.rem(chip // 2 + k % 2, 2) + lax.rem(chip + k // 2, 2)
            for z in range(sources):
                row = pl.ds(pl.multiple_of(z * steps * part + piece * part, part), part)
                weights_ref[row, at] = ref[k, z]
    weights = weights_ref[...]
    marks = marks_ref[...]
    for block in range(NX):
        vis = jnp.dot(rows_ref[block, tokens:, :], weights, preferred_element_type=jnp.float32)
        slots = jnp.where(x == block, marks, jnp.zeros_like(marks))
        for i in range(NS):
            vis_ref[block * NS + i, :, : 2 * cols] = vis[i * CAP : (i + 1) * CAP]
            vis_ref[block * NS + i, :, 2 * cols :] = slots[i * CAP : (i + 1) * CAP]
    for d, ref in enumerate(text_refs):
        ref[...] = jnp.dot(
            rows_ref[lax.rem(x + d, NX), :tokens, :], weights, preferred_element_type=jnp.float32
        )


def projection(place, rows, mine, other, marks):
    blocks, count, part = rows.shape
    cols = 2 * mine.shape[-1]
    extra = NS * CAP
    text = pltpu.VMEM((count - extra, cols), jnp.float32)
    vis = jax.ShapeDtypeStruct((blocks * NS, CAP, cols + marks.shape[1]), jnp.float32)
    return pl.pallas_call(
        project,
        grid_spec=pltpu.PrefetchScalarGridSpec(
            num_scalar_prefetch=1,
            grid=(1,),
            in_specs=[IN_VMEM] * 4,
            out_specs=[pl.BlockSpec(vis.shape, lambda i, _: (0, 0, 0))] + [IN_VMEM] * blocks,
            scratch_shapes=[pltpu.VMEM((part, cols), jnp.bfloat16)],
        ),
        out_shape=[vis] + [text] * blocks,
        compiler_params=pltpu.CompilerParams(vmem_limit_bytes=16 * MIB),
        name="project",
    )(place, *map(in_vmem, (rows, mine, other)), marks)


def merge(vis_ref, docs_ref, *refs):
    *text_refs, out_ref = refs
    tokens, cols = text_refs[0].shape
    text = (text_refs[0][...] + text_refs[1][...]) + (text_refs[2][...] + text_refs[3][...])
    vis = vis_ref[...]
    vis = (vis[:NS] + vis[NS : 2 * NS]) + (vis[2 * NS : 3 * NS] + vis[3 * NS :])
    vis = vis.reshape(NS * CAP, vis.shape[-1])
    slots = vis[:, cols:]
    matches = slots == lax.broadcasted_iota(jnp.int32, slots.shape, 1).astype(jnp.float32)
    chooser = matches.astype(jnp.float32).astype(jnp.bfloat16)
    dims = (((0,), (0,)), ((), ()))
    moved = lax.dot_general(
        chooser, vis[:, :cols].astype(jnp.bfloat16), dims, preferred_element_type=jnp.float32
    )
    ones = jnp.ones((slots.shape[0], cols), jnp.bfloat16)
    used = lax.dot_general(chooser, ones, dims, preferred_element_type=jnp.float32)
    out_ref[:tokens, :] = jnp.where(used > 0.5, moved, text).astype(jnp.bfloat16)
    out_ref[tokens:, :] = docs_ref[...]


def merged_block(vis, docs, text):
    tokens, cols = text[0].shape
    return pl.pallas_call(
        merge,
        in_specs=[IN_VMEM] * (2 + len(text)),
        out_specs=IN_VMEM,
        out_shape=pltpu.VMEM((tokens + docs.shape[0], cols), jnp.bfloat16),
        compiler_params=pltpu.CompilerParams(vmem_limit_bytes=8 * MIB),
        name="merge",
    )(in_vmem(vis), docs, *map(in_vmem, text))


def attend(place_ref, q_ref, mine_ref, other_ref, my_docs_ref, out_ref, bias_ref, keys_ref, values_ref):
    tokens = q_ref.shape[0]
    blocks = mine_ref.shape[0]

    @pl.when(pl.program_id(0) == 0)
    def _():
        s = place_ref[0]
        core, chip = lax.rem(s, 2), s // 2
        my_docs = jnp.broadcast_to(my_docs_ref[...], (tokens, tokens))
        row = lax.broadcasted_iota(jnp.int32, (tokens, tokens), 0) + s * tokens
        col = lax.broadcasted_iota(jnp.int32, (tokens, tokens), 1)
        for side, ref in enumerate((mine_ref, other_ref)):
            for d in range(blocks):
                block = 2 * (chip - d) + (core if side == 0 else 1 - core)
                docs = ref[d, tokens : tokens + 8, :tokens].astype(jnp.float32)[:1]
                spot = col + block * tokens
                allowed = (docs == my_docs) & (spot <= row) & (spot >= 0)
                at = (side * blocks + d) * tokens
                bias_ref[:, at : at + tokens] = jnp.where(allowed, 0.0, -1e30)
                keys_ref[at : at + tokens, :] = ref[d, :tokens, :HEAD]
                values_ref[at : at + tokens, :] = ref[d, :tokens, HEAD:]

    scale = 1.0 / jnp.sqrt(jnp.float32(HEAD))
    for h in range(HEADS_STEP):
        head = slice(h * HEAD, (h + 1) * HEAD)
        scores = lax.dot_general(
            q_ref[:, head], keys_ref[...], (((1,), (1,)), ((), ())), preferred_element_type=jnp.float32
        )
        scores = scores * scale + bias_ref[...]
        top = jnp.max(scores, axis=1, keepdims=True)
        weights = jnp.exp(scores - top)
        total = jnp.sum(weights, axis=1, keepdims=True)
        mixed = jnp.dot(
            weights.astype(jnp.bfloat16), values_ref[...], preferred_element_type=jnp.float32
        )
        out_ref[:, head] = (mixed / total).astype(out_ref.dtype)


def attention(place, queries, mine, other, my_docs):
    tokens = queries.shape[0]
    span = 2 * mine.shape[0] * tokens
    return pl.pallas_call(
        attend,
        grid_spec=pltpu.PrefetchScalarGridSpec(
            num_scalar_prefetch=1,
            grid=(QPK // HEADS_STEP,),
            in_specs=[
                pl.BlockSpec((tokens, HEADS_STEP * HEAD), lambda h, *_: (0, h)),
                IN_VMEM,
                IN_VMEM,
                IN_VMEM,
            ],
            out_specs=pl.BlockSpec((tokens, HEADS_STEP * HEAD), lambda h, *_: (0, h)),
            scratch_shapes=[
                pltpu.VMEM((tokens, span), jnp.float32),
                pltpu.VMEM((span, HEAD), jnp.bfloat16),
                pltpu.VMEM((span, HEAD), jnp.bfloat16),
            ],
        ),
        out_shape=jax.ShapeDtypeStruct(queries.shape, jnp.bfloat16),
        compiler_params=pltpu.CompilerParams(vmem_limit_bytes=16 * MIB),
        name="attend",
    )(place, queries, in_vmem(mine), in_vmem(other), my_docs)


def exchange_x(array):
    return lax.all_to_all(array, "grp", 0, 0, axis_index_groups=OVER_X, tiled=True)


def program(hidden, queries, vis_rows, vis_slot, doc_ids, w_key, w_value):
    tokens = hidden.shape[0]
    cols = 2 * w_key.shape[1]
    place = lax.axis_index("seq")
    core, chip = place % 2, place // 2
    x = lax.axis_index("grp") // NZ
    where = jnp.stack([place, x])

    part = w_key.shape[0] // 4
    start = (chip % 4) * part
    piece = jnp.where(
        core == 0,
        lax.dynamic_slice_in_dim(w_key, start, part, axis=0),
        lax.dynamic_slice_in_dim(w_value, start, part, axis=0),
    )
    got = lax.all_gather(piece, "grp", axis=0, axis_index_groups=OVER_Z)

    rows = exchange_x(packed(hidden, vis_rows))

    far = seq_permute(got, flip(2))
    pair = jnp.stack([got, far])
    near = seq_permute(pair, flip(1))
    four = jnp.concatenate([pair, near])
    rest = seq_permute(four, sibling)

    marks = jnp.broadcast_to(vis_slot.reshape(NS * CAP, 1), (NS * CAP, tokens)).astype(jnp.float32)
    vis, *text = projection(where, rows, four, rest, marks)
    vis = lax.all_to_all(
        vis, ("grp", "seq"), 0, 0, axis_index_groups=OVER_X_SEQ, tiled=True
    )
    for d in (2, 1, 3):
        text[d] = x_permute(in_vmem(text[d]), d)
    docs = jnp.broadcast_to(jnp.tile(doc_ids, (1, cols // tokens)), (8, cols)).astype(jnp.bfloat16)
    block = merged_block(vis, docs, text)

    back = [seq_permute(block, later(d)) for d in range(1, REACH + 1)]
    mine = jnp.stack([block, *back])
    other = seq_permute(mine, sibling)
    my_docs = doc_ids.reshape(tokens, 1).astype(jnp.float32)
    return attention(where, queries, mine, other, my_docs)


def solution(mesh):
    return jax.shard_map(
        program,
        mesh=mesh,
        in_specs=(
            P(("grp", "seq"), None),
            P(("grp", "seq"), "tp"),
            P(("grp", "seq"), None, None, None),
            P(("grp", "seq"), None, None),
            P("grp", "seq"),
            P("grp", "tp"),
            P("grp", "tp"),
        ),
        out_specs=P(("grp", "seq"), "tp"),
        check_vma=False,
    )
```

time: 173 us -> 141 us (0.82)
  the two profiles are of different devices: /device:TPU:97 before, /device:TPU:121 now
where the time goes in v2:
time: 141 us; the launch traced here: 140 us
  starting transfers between devices  55.9 us (40%)
  blocking collectives  38.4 us (27%)
  waiting for transfers between devices  28.2 us (20%)
  Pallas kernels  13.5 us (10%)
  local copies, waits for them, and re-layouts  2.36 us (2%)
  other arithmetic  1.74 us (1%)
    all_gather x1, blocking collectives, program(): got = lax.all_gather(piece, 'grp', axis=0, axis_index_groups=OVER_Z)  38.4 us
    ppermute x8, starting transfers between devices, seq_permute(): return lax.ppermute(array, AXES, pairs)  31.3 us
    ppermute x8, waiting for transfers between devices, seq_permute(): return lax.ppermute(array, AXES, pairs)  16.5 us
    ppermute x3, starting transfers between devices, x_permute(): lax.ppermute(array, AXES, [(i, (i + d * step) % size) for i in range(size)])  10.6 us
    all_to_all x1, starting transfers between devices, program(): lax.all_to_all(vis, ('grp', 'seq'), 0, 0, axis_index_groups=OVER_X_SEQ, t...  9.86 us
    all_to_all x1, waiting for transfers between devices, program(): lax.all_to_all(vis, ('grp', 'seq'), 0, 0, axis_index_groups=OVER_X_SEQ, t...  8.23 us
    pallas_call x1, Pallas kernels, attention(): pl.pallas_call(attend, grid_spec=pltpu.PrefetchScalarGridSpec(num_scalar_...  5.11 us
    pallas_call x1, Pallas kernels, packed(): pl.pallas_call(pack, grid=(NX,), in_specs=[pl.BlockSpec((tokens, part), l...  4.17 us
  transfers between devices with their start and end apart: 13, of which 9 were waited for; matrix products, arithmetic and copies ran while one was open for 1% of the time, Pallas kernels for 0%

profile of v2, /device:TPU:121, one launch (start us, length us, event | category | flops | bytes accessed | tf_op | source)
XLA Modules:
  0.0 140.4 jit_solution(8661571076667808008)
XLA Ops:
  0.0 4.2 %pack.1 = bf16[4,192,2048]{2,1,0:T(8,128)(2,1)} custom-call(bf16[128,8192]{1,0:T(8,128)(2,1)} %text_ref.1, bf16[1,16,4,8192]{3,2,1,0:T(4,128)(2,1)} %extra_ref.1), custom_call_target="tpu_custom_call" | custom-call | tf_op jit(solution)/shard_map/pack/pallas_call | solution.py:76
  4.2 0.0 copy-start.4
  4.2 4.1 %all-to-all-start = ((bf16[4,192,2048]{2,1,0:T(8,128)(2,1)}), bf16[4,192,2048]{2,1,0:T(8,128)(2,1)S(1)}, u32[]{:S(2)}, u32[]{:S(2)}) async-start(bf16[4,192,2048]{2,1,0:T(8,128)(2,1)} %pack.1), calls=%async_computation | async-start | bytes 6291456 | tf_op jit(solution)/shard_map/all_to_all | solution.py:236
  8.3 0.8 dynamic-slice_select_fusion
  9.1 38.4 %all-gather = bf16[512,128]{1,0:T(8,128)(2,1)S(1)} all-gather(bf16[128,128]{1,0:T(8,128)(2,1)S(1)} %dynamic-slice_select_fusion), channel_id=2, replica_groups={{0,64,128,192},{256,320,384,448},{512,576,640,704},{768,832,896,960},{1..., dimensions={0}, use_global_device_ids=true | all-gather | bytes 163840 | tf_op jit(solution)/shard_map/all_gather | solution.py:254
  47.5 4.1 %collective-permute-start = (bf16[4,128,128]{2,1,0:T(8,128)(2,1)S(1)}, bf16[4,128,128]{2,1,0:T(8,128)(2,1)S(1)}, u32[]{:S(2)}, u32[]{:S(2)}) collective-permute-start(bf16[4,128,128]{2,1,0:T(8,128)(2,1)S(1)} %bitcast.21), channel_id=1, source_target_pairs={{0,16},{1,17},{2,18},{3,19},{4,20},{5,21},{6,22},{7,23},{8,24},{9,... | collective-permute-start | bytes 393224 | tf_op jit(solution)/shard_map/ppermute | solution.py:34
  51.6 3.9 %collective-permute-done = bf16[4,128,128]{2,1,0:T(8,128)(2,1)S(1)} collective-permute-done((bf16[4,128,128]{2,1,0:T(8,128)(2,1)S(1)}, bf16[4,128,128]{2,1,0:T(8,128)(2,1)S(1)}, u32[]{:S(2)}, u32[]{:S(2)}) %collective-permute-start) | collective-permute-done | bytes 131104 | tf_op jit(solution)/shard_map/ppermute | solution.py:34
  55.5 0.0 copy-start.5
  55.5 1.9 %collective-permute-start.1 = (bf16[2,4,128,128]{3,2,1,0:T(8,128)(2,1)S(1)}, bf16[2,4,128,128]{3,2,1,0:T(8,128)(2,1)S(1)}, u32[]{:S(2)}, u32[]{:S(2)}) collective-permute-start(bf16[2,4,128,128]{3,2,1,0:T(8,128)(2,1)S(1)} %pad_maximum_fusion.1), channel_id=1, source_target_pairs={{0,8},{1,9},{2,10},{3,11},{4,12},{5,13},{6,14},{7,15},{8,0},{9,1},... | collective-permute-start | bytes 786440 | tf_op jit(solution)/shard_map/ppermute | solution.py:34
  57.5 5.8 %collective-permute-done.1 = bf16[2,4,128,128]{3,2,1,0:T(8,128)(2,1)S(1)} collective-permute-done((bf16[2,4,128,128]{3,2,1,0:T(8,128)(2,1)S(1)}, bf16[2,4,128,128]{3,2,1,0:T(8,128)(2,1)S(1)}, u32[]{:S(2)}, u32[]{:S(2)}) %collective-permute-start.1) | collective-permute-done | bytes 262176 | tf_op jit(solution)/shard_map/ppermute | solution.py:34
  63.2 0.8 pad_maximum_fusion.mine_ref
  64.1 8.2 %collective-permute-start.2 = (bf16[4,4,128,128]{3,2,1,0:T(8,128)(2,1)}, bf16[4,4,128,128]{3,2,1,0:T(8,128)(2,1)}, u32[]{:S(2)}, u32[]{:S(2)}) collective-permute-start(bf16[4,4,128,128]{3,2,1,0:T(8,128)(2,1)} %pad_maximum_fusion.mine_ref), channel_id=1, source_target_pairs={{0,4},{1,5},{2,6},{3,7},{4,0},{5,1},{6,2},{7,3},{8,12},{9,13},{10,... | collective-permute-start | bytes 1572872 | tf_op jit(solution)/shard_map/ppermute | solution.py:34
  72.3 0.0 copy-done.4
  72.3 0.1 copy.10
  72.4 0.1 convert_element_type.18
  72.5 0.1 pad_add_fusion.place_ref
  72.5 1.6 %collective-permute-done.2.other_ref = bf16[4,4,128,128]{3,2,1,0:T(8,128)(2,1)} collective-permute-done((bf16[4,4,128,128]{3,2,1,0:T(8,128)(2,1)}, bf16[4,4,128,128]{3,2,1,0:T(8,128)(2,1)}, u32[]{:S(2)}, u32[]{:S(2)}) %collective-permute-start.2) | collective-permute-done | bytes 524320 | tf_op jit(solution)/shard_map/ppermute | solution.py:34
  74.1 0.0 all-to-all-done.rows_ref
  74.1 0.1 broadcast_in_dim.4.marks_ref
  74.2 0.0 copy-start
  74.2 4.0 %project.1 = (f32[64,4,384]{2,1,0:T(4,128)}, f32[128,256]{1,0:T(8,128)S(1)}, f32[128,256]{1,0:T(8,128)S(1)}, f32[128,256]{1,0:T(8,128)S(1)}, f32[128,256]{1,0:T(8,128)S(1)}) custom-call(s32[2]{0:T(128)S(1)} %pad_add_fusion.place_ref, bf16[4,192,2048]{2,1,0:T(8,128)(2,1)S(1)} %all-to-all-done.rows_ref, bf16[4,4,128,128]{3,2,1,0:T(8,128)(2,1)} %pad_maximum_fusion.mine_ref, ...), custom_call_target="tpu_custom_call" | custom-call | tf_op jit(solution)/shard_map/project/pallas_call | solution.py:123
  78.2 0.0 copy-start.1
  78.2 0.6 copy-done.1
  78.9 0.0 copy-start.2
  78.9 0.7 copy-done.2
  79.5 0.0 copy-start.3
  79.5 0.7 copy-done.3
  80.2 9.9 %all-to-all-start.1 = ((f32[64,4,384]{2,1,0:T(4,128)}), f32[64,4,384]{2,1,0:T(4,128)S(1)}, u32[]{:S(2)}, u32[]{:S(2)}) async-start(f32[64,4,384]{2,1,0:T(4,128)} %get-tuple-element.10), calls=%async_computation.1 | async-start | bytes 786432 | tf_op jit(solution)/shard_map/all_to_all | solution.py:266
  90.0 0.0 copy-done.5
  90.1 3.1 %collective-permute-start.3 = (f32[128,256]{1,0:T(8,128)}, f32[128,256]{1,0:T(8,128)S(1)}, u32[]{:S(2)}, u32[]{:S(2)}) collective-permute-start(f32[128,256]{1,0:T(8,128)} %copy-done.3), channel_id=1, source_target_pairs={{0,256},{1,257},{2,258},{3,259},{4,260},{5,261},{6,262},{7,263},{8... | collective-permute-start | bytes 393224 | tf_op jit(solution)/shard_map/ppermute | solution.py:39
  93.2 4.5 %collective-permute-start.4 = (f32[128,256]{1,0:T(8,128)}, f32[128,256]{1,0:T(8,128)S(1)}, u32[]{:S(2)}, u32[]{:S(2)}) collective-permute-start(f32[128,256]{1,0:T(8,128)} %copy-done.2), channel_id=1, source_target_pairs={{0,512},{1,513},{2,514},{3,515},{4,516},{5,517},{6,518},{7,519},{8... | collective-permute-start | bytes 393224 | tf_op jit(solution)/shard_map/ppermute | solution.py:39
  97.7 3.0 %collective-permute-start.5 = (f32[128,256]{1,0:T(8,128)}, f32[128,256]{1,0:T(8,128)S(1)}, u32[]{:S(2)}, u32[]{:S(2)}) collective-permute-start(f32[128,256]{1,0:T(8,128)} %copy-done.1), channel_id=1, source_target_pairs={{0,768},{1,769},{2,770},{3,771},{4,772},{5,773},{6,774},{7,775},{8... | collective-permute-start | bytes 393224 | tf_op jit(solution)/shard_map/ppermute | solution.py:39
  100.7 0.0 collective-permute-done.3.refs_1_
  100.7 3.0 %collective-permute-done.4.refs_2_ = f32[128,256]{1,0:T(8,128)S(1)} collective-permute-done((f32[128,256]{1,0:T(8,128)}, f32[128,256]{1,0:T(8,128)S(1)}, u32[]{:S(2)}, u32[]{:S(2)}) %collective-permute-start.4) | collective-permute-done | bytes 131104 | tf_op jit(solution)/shard_map/ppermute | solution.py:39
  103.7 0.5 collective-permute-done.5.refs_3_
  104.3 8.2 %all-to-all-done.1.vis_ref = f32[64,4,384]{2,1,0:T(4,128)S(1)} async-done(((f32[64,4,384]{2,1,0:T(4,128)}), f32[64,4,384]{2,1,0:T(4,128)S(1)}, u32[]{:S(2)}, u32[]{:S(2)}) %all-to-all-start.1) | async-done | bytes 393248 | tf_op jit(solution)/shard_map/all_to_all | solution.py:266
  112.5 0.2 merge.1
  112.7 2.1 %collective-permute-start.6 = (bf16[136,256]{1,0:T(8,128)(2,1)S(1)}, bf16[136,256]{1,0:T(8,128)(2,1)S(1)}, u32[]{:S(2)}, u32[]{:S(2)}) collective-permute-start(bf16[136,256]{1,0:T(8,128)(2,1)S(1)} %merge.1), channel_id=1, source_target_pairs={{0,8},{1,9},{2,10},{3,11},{4,12},{5,13},{6,14},{7,15},{8,16},{9,17... | collective-permute-start | bytes 208904 | tf_op jit(solution)/shard_map/ppermute | solution.py:34
  114.8 1.9 %collective-permute-start.7 = (bf16[136,256]{1,0:T(8,128)(2,1)S(1)}, bf16[136,256]{1,0:T(8,128)(2,1)S(1)}, u32[]{:S(2)}, u32[]{:S(2)}) collective-permute-start(bf16[136,256]{1,0:T(8,128)(2,1)S(1)} %merge.1), channel_id=1, source_target_pairs={{0,16},{1,17},{2,18},{3,19},{4,20},{5,21},{6,22},{7,23},{8,24},{9,... | collective-permute-start | bytes 208904 | tf_op jit(solution)/shard_map/ppermute | solution.py:34
  116.8 3.3 %collective-permute-start.8 = (bf16[136,256]{1,0:T(8,128)(2,1)S(1)}, bf16[136,256]{1,0:T(8,128)(2,1)S(1)}, u32[]{:S(2)}, u32[]{:S(2)}) collective-permute-start(bf16[136,256]{1,0:T(8,128)(2,1)S(1)} %merge.1), channel_id=1, source_target_pairs={{0,24},{1,25},{2,26},{3,27},{4,28},{5,29},{6,30},{7,31},{8,32},{9,... | collective-permute-start | bytes 208904 | tf_op jit(solution)/shard_map/ppermute | solution.py:34
  120.0 1.3 collective-permute-start.9
  121.3 0.0 collective-permute-done.6
  121.4 0.0 collective-permute-done.7
  121.4 2.3 %collective-permute-done.8 = bf16[136,256]{1,0:T(8,128)(2,1)S(1)} collective-permute-done((bf16[136,256]{1,0:T(8,128)(2,1)S(1)}, bf16[136,256]{1,0:T(8,128)(2,1)S(1)}, u32[]{:S(2)}, u32[]{:S(2)}) %collective-permute-start.8) | collective-permute-done | bytes 69664 | tf_op jit(solution)/shard_map/ppermute | solution.py:34
  123.7 1.7 %collective-permute-done.9 = bf16[136,256]{1,0:T(8,128)(2,1)S(1)} collective-permute-done((bf16[136,256]{1,0:T(8,128)(2,1)S(1)}, bf16[136,256]{1,0:T(8,128)(2,1)S(1)}, u32[]{:S(2)}, u32[]{:S(2)}) %collective-permute-start.9) | collective-permute-done | bytes 69664 | tf_op jit(solution)/shard_map/ppermute | solution.py:34
  125.5 8.6 %collective-permute-start.10 = (bf16[5,136,256]{2,1,0:T(8,128)(2,1)S(1)}, bf16[5,136,256]{2,1,0:T(8,128)(2,1)S(1)}, u32[]{:S(2)}, u32[]{:S(2)}) collective-permute-start(bf16[5,136,256]{2,1,0:T(8,128)(2,1)S(1)} %bitcast_dynamic-update-slice_fusion.mine_ref), channel_id=1, source_target_pairs={{0,4},{1,5},{2,6},{3,7},{4,0},{5,1},{6,2},{7,3},{8,12},{9,13},{10,... | collective-permute-start | bytes 1044488 | tf_op jit(solution)/shard_map/ppermute | solution.py:34
  134.0 0.1 copy.11.my_docs_ref
  134.2 1.1 collective-permute-done.10.other_ref
  135.3 0.0 copy-done
  135.3 5.1 %attend.1 = bf16[128,1024]{1,0:T(8,128)(2,1)} custom-call(s32[2]{0:T(128)S(1)} %pad_add_fusion.place_ref, bf16[128,1024]{1,0:T(8,128)(2,1)S(1)} %copy-done, bf16[5,136,256]{2,1,0:T(8,128)(2,1)S(1)} %bitcast_dynamic-update-slice_fusion.mine_ref, bf16[5,136,256]{2,1,0:T(8,128)(2,1)S(1)} %collective-permute-done.10.other_ref, f32[128,1]{1,0:T(8,128)S(1)} %copy.11.my_docs_ref), custom_call_target="tpu_custom_call" | custom-call | tf_op jit(solution)/shard_map/attend/pallas_call | solution.py:211
  (10 shorter events, 0.1 us)
Async XLA Ops:
  4.2 68.1 %copy-start.4 = (s32[1,16,4]{1,2,0:T(4,128)S(1)}, s32[1,16,4]{1,2,0:T(4,128)}, u32[]{:S(2)}) copy-start(s32[1,16,4]{1,2,0:T(4,128)} %param.10) | copy-start | bytes 772
  4.2 69.9 %all-to-all-start = ((bf16[4,192,2048]{2,1,0:T(8,128)(2,1)}), bf16[4,192,2048]{2,1,0:T(8,128)(2,1)S(1)}, u32[]{:S(2)}, u32[]{:S(2)}) async-start(bf16[4,192,2048]{2,1,0:T(8,128)(2,1)} %pack.1), calls=%async_computation | async-start | bytes 6291456 | tf_op jit(solution)/shard_map/all_to_all | solution.py:236
  47.5 8.0 %collective-permute-start = (bf16[4,128,128]{2,1,0:T(8,128)(2,1)S(1)}, bf16[4,128,128]{2,1,0:T(8,128)(2,1)S(1)}, u32[]{:S(2)}, u32[]{:S(2)}) collective-permute-start(bf16[4,128,128]{2,1,0:T(8,128)(2,1)S(1)} %bitcast.21), channel_id=1, source_target_pairs={{0,16},{1,17},{2,18},{3,19},{4,20},{5,21},{6,22},{7,23},{8,24},{9,... | collective-permute-start | bytes 393224 | tf_op jit(solution)/shard_map/ppermute | solution.py:34
  55.5 34.5 %copy-start.5 = (s32[1,128]{1,0:T(1,128)S(1)}, s32[1,128]{1,0:T(1,128)}, u32[]{:S(2)}) copy-start(s32[1,128]{1,0:T(1,128)} %param.11) | copy-start | bytes 1540
  55.5 7.7 %collective-permute-start.1 = (bf16[2,4,128,128]{3,2,1,0:T(8,128)(2,1)S(1)}, bf16[2,4,128,128]{3,2,1,0:T(8,128)(2,1)S(1)}, u32[]{:S(2)}, u32[]{:S(2)}) collective-permute-start(bf16[2,4,128,128]{3,2,1,0:T(8,128)(2,1)S(1)} %pad_maximum_fusion.1), channel_id=1, source_target_pairs={{0,8},{1,9},{2,10},{3,11},{4,12},{5,13},{6,14},{7,15},{8,0},{9,1},... | collective-permute-start | bytes 786440 | tf_op jit(solution)/shard_map/ppermute | solution.py:34
  64.1 10.0 %collective-permute-start.2 = (bf16[4,4,128,128]{3,2,1,0:T(8,128)(2,1)}, bf16[4,4,128,128]{3,2,1,0:T(8,128)(2,1)}, u32[]{:S(2)}, u32[]{:S(2)}) collective-permute-start(bf16[4,4,128,128]{3,2,1,0:T(8,128)(2,1)} %pad_maximum_fusion.mine_ref), channel_id=1, source_target_pairs={{0,4},{1,5},{2,6},{3,7},{4,0},{5,1},{6,2},{7,3},{8,12},{9,13},{10,... | collective-permute-start | bytes 1572872 | tf_op jit(solution)/shard_map/ppermute | solution.py:34
  74.2 61.1 %copy-start = (bf16[128,1024]{1,0:T(8,128)(2,1)S(1)}, bf16[128,1024]{1,0:T(8,128)(2,1)}, u32[]{:S(2)}) copy-start(bf16[128,1024]{1,0:T(8,128)(2,1)} %q_ref.1) | copy-start | bytes 786436
  78.2 0.6 copy-start.1
  78.9 0.7 copy-start.2
  79.5 0.7 copy-start.3
  80.2 32.3 %all-to-all-start.1 = ((f32[64,4,384]{2,1,0:T(4,128)}), f32[64,4,384]{2,1,0:T(4,128)S(1)}, u32[]{:S(2)}, u32[]{:S(2)}) async-start(f32[64,4,384]{2,1,0:T(4,128)} %get-tuple-element.10), calls=%async_computation.1 | async-start | bytes 786432 | tf_op jit(solution)/shard_map/all_to_all | solution.py:266
  90.1 10.7 %collective-permute-start.3 = (f32[128,256]{1,0:T(8,128)}, f32[128,256]{1,0:T(8,128)S(1)}, u32[]{:S(2)}, u32[]{:S(2)}) collective-permute-start(f32[128,256]{1,0:T(8,128)} %copy-done.3), channel_id=1, source_target_pairs={{0,256},{1,257},{2,258},{3,259},{4,260},{5,261},{6,262},{7,263},{8... | collective-permute-start | bytes 393224 | tf_op jit(solution)/shard_map/ppermute | solution.py:39
  93.2 10.5 %collective-permute-start.4 = (f32[128,256]{1,0:T(8,128)}, f32[128,256]{1,0:T(8,128)S(1)}, u32[]{:S(2)}, u32[]{:S(2)}) collective-permute-start(f32[128,256]{1,0:T(8,128)} %copy-done.2), channel_id=1, source_target_pairs={{0,512},{1,513},{2,514},{3,515},{4,516},{5,517},{6,518},{7,519},{8... | collective-permute-start | bytes 393224 | tf_op jit(solution)/shard_map/ppermute | solution.py:39
  97.7 6.6 %collective-permute-start.5 = (f32[128,256]{1,0:T(8,128)}, f32[128,256]{1,0:T(8,128)S(1)}, u32[]{:S(2)}, u32[]{:S(2)}) collective-permute-start(f32[128,256]{1,0:T(8,128)} %copy-done.1), channel_id=1, source_target_pairs={{0,768},{1,769},{2,770},{3,771},{4,772},{5,773},{6,774},{7,775},{8... | collective-permute-start | bytes 393224 | tf_op jit(solution)/shard_map/ppermute | solution.py:39
  112.7 8.6 %collective-permute-start.6 = (bf16[136,256]{1,0:T(8,128)(2,1)S(1)}, bf16[136,256]{1,0:T(8,128)(2,1)S(1)}, u32[]{:S(2)}, u32[]{:S(2)}) collective-permute-start(bf16[136,256]{1,0:T(8,128)(2,1)S(1)} %merge.1), channel_id=1, source_target_pairs={{0,8},{1,9},{2,10},{3,11},{4,12},{5,13},{6,14},{7,15},{8,16},{9,17... | collective-permute-start | bytes 208904 | tf_op jit(solution)/shard_map/ppermute | solution.py:34
  114.8 6.5 %collective-permute-start.7 = (bf16[136,256]{1,0:T(8,128)(2,1)S(1)}, bf16[136,256]{1,0:T(8,128)(2,1)S(1)}, u32[]{:S(2)}, u32[]{:S(2)}) collective-permute-start(bf16[136,256]{1,0:T(8,128)(2,1)S(1)} %merge.1), channel_id=1, source_target_pairs={{0,16},{1,17},{2,18},{3,19},{4,20},{5,21},{6,22},{7,23},{8,24},{9,... | collective-permute-start | bytes 208904 | tf_op jit(solution)/shard_map/ppermute | solution.py:34
  116.8 7.0 %collective-permute-start.8 = (bf16[136,256]{1,0:T(8,128)(2,1)S(1)}, bf16[136,256]{1,0:T(8,128)(2,1)S(1)}, u32[]{:S(2)}, u32[]{:S(2)}) collective-permute-start(bf16[136,256]{1,0:T(8,128)(2,1)S(1)} %merge.1), channel_id=1, source_target_pairs={{0,24},{1,25},{2,26},{3,27},{4,28},{5,29},{6,30},{7,31},{8,32},{9,... | collective-permute-start | bytes 208904 | tf_op jit(solution)/shard_map/ppermute | solution.py:34
  120.0 5.4 %collective-permute-start.9 = (bf16[136,256]{1,0:T(8,128)(2,1)S(1)}, bf16[136,256]{1,0:T(8,128)(2,1)S(1)}, u32[]{:S(2)}, u32[]{:S(2)}) collective-permute-start(bf16[136,256]{1,0:T(8,128)(2,1)S(1)} %merge.1), channel_id=1, source_target_pairs={{0,32},{1,33},{2,34},{3,35},{4,36},{5,37},{6,38},{7,39},{8,40},{9,... | collective-permute-start | bytes 208904 | tf_op jit(solution)/shard_map/ppermute | solution.py:34
  125.5 9.8 %collective-permute-start.10 = (bf16[5,136,256]{2,1,0:T(8,128)(2,1)S(1)}, bf16[5,136,256]{2,1,0:T(8,128)(2,1)S(1)}, u32[]{:S(2)}, u32[]{:S(2)}) collective-permute-start(bf16[5,136,256]{2,1,0:T(8,128)(2,1)S(1)} %bitcast_dynamic-update-slice_fusion.mine_ref), channel_id=1, source_target_pairs={{0,4},{1,5},{2,6},{3,7},{4,0},{5,1},{6,2},{7,3},{8,12},{9,13},{10,... | collective-permute-start | bytes 1044488 | tf_op jit(solution)/shard_map/ppermute | solution.py:34

commit v3 on v2

--- a/solution.py
+++ b/solution.py
@@ -18,8 +18,11 @@
 REACH = 4
 AXES = ("grp", "seq", "tp")
 OVER_X = [[x * NZ + z for x in range(NX)] for z in range(NZ)]
-OVER_X_SEQ = [[(x * NZ + z) * NS + s for x in range(NX) for s in range(NS)] for z in range(NZ)]
 OVER_Z = [[x * NZ + z for z in range(NZ)] for x in range(NX)]
+NEAR = 4
+OVER_NEAR = [
+    [(first + i) * 2 + core for i in range(NEAR)] for first in range(0, NLO, NEAR) for core in range(2)
+]
 
 
 def seq_permute(array, move):
@@ -41,10 +44,6 @@
 
 def sibling(z, c):
     return z, 1 - c
-
-
-def flip(mask):
-    return lambda z, c: (z ^ mask, c)
 
 
 def later(d):
@@ -87,68 +86,102 @@
     )(in_hbm(hidden), in_hbm(vis_rows))
 
 
-def project(place_ref, rows_ref, mine_ref, other_ref, marks_ref, vis_ref, *refs):
-    *text_refs, weights_ref = refs
+def project_extra(place_ref, rows_ref, mine_ref, other_ref, vis_ref, weights_ref):
     steps, sources, part, cols = mine_ref.shape
-    tokens = text_refs[0].shape[0]
-    s, x = place_ref[0], place_ref[1]
-    core, chip = lax.rem(s, 2), lax.rem(s // 2, 4)
+    tokens = rows_ref.shape[1] - NS * CAP
+    core = lax.rem(place_ref[0], 2)
     for side, ref in enumerate((mine_ref, other_ref)):
         at = pl.ds(pl.multiple_of(jnp.where(core == side, 0, cols), cols), cols)
         for k in range(steps):
-            piece = 2 * lax.rem(chip // 2 + k % 2, 2) + lax.rem(chip + k // 2, 2)
             for z in range(sources):
-                row = pl.ds(pl.multiple_of(z * steps * part + piece * part, part), part)
-                weights_ref[row, at] = ref[k, z]
+                row = (z * steps + k) * part
+                weights_ref[row : row + part, at] = ref[k, z]
     weights = weights_ref[...]
-    marks = marks_ref[...]
     for block in range(NX):
-        vis = jnp.dot(rows_ref[block, tokens:, :], weights, preferred_element_type=jnp.float32)
-        slots = jnp.where(x == block, marks, jnp.zeros_like(marks))
-        for i in range(NS):
-            vis_ref[block * NS + i, :, : 2 * cols] = vis[i * CAP : (i + 1) * CAP]
-            vis_ref[block * NS + i, :, 2 * cols :] = slots[i * CAP : (i + 1) * CAP]
-    for d, ref in enumerate(text_refs):
-        ref[...] = jnp.dot(
-            rows_ref[lax.rem(x + d, NX), :tokens, :], weights, preferred_element_type=jnp.float32
+        vis_ref[block] = jnp.dot(
+            rows_ref[block, tokens:, :], weights, preferred_element_type=jnp.float32
         )
 
 
-def projection(place, rows, mine, other, marks):
-    blocks, count, part = rows.shape
+def projected_extra(place, rows, mine, other):
+    blocks, _, part = rows.shape
     cols = 2 * mine.shape[-1]
-    extra = NS * CAP
-    text = pltpu.VMEM((count - extra, cols), jnp.float32)
-    vis = jax.ShapeDtypeStruct((blocks * NS, CAP, cols + marks.shape[1]), jnp.float32)
-    return pl.pallas_call(
-        project,
+    vis = pltpu.HBM((blocks, NS * CAP, cols), jnp.float32)
+    return pl.pallas_call(
+        project_extra,
         grid_spec=pltpu.PrefetchScalarGridSpec(
             num_scalar_prefetch=1,
             grid=(1,),
-            in_specs=[IN_VMEM] * 4,
-            out_specs=[pl.BlockSpec(vis.shape, lambda i, _: (0, 0, 0))] + [IN_VMEM] * blocks,
-            scratch_shapes=[pltpu.VMEM((part, cols), jnp.bfloat16)],
+            in_specs=[IN_VMEM] * 3,
+            out_specs=[pl.BlockSpec(vis.shape, lambda i, _: (0, 0, 0)), IN_VMEM],
         ),
-        out_shape=[vis] + [text] * blocks,
+        out_shape=[vis, pltpu.VMEM((part, cols), jnp.bfloat16)],
         compiler_params=pltpu.CompilerParams(vmem_limit_bytes=16 * MIB),
-        name="project",
-    )(place, *map(in_vmem, (rows, mine, other)), marks)
+        name="project_extra",
+    )(place, *map(in_vmem, (rows, mine, other)))
+
+
+def project_text(place_ref, rows_ref, weights_ref, own_ref, *text_refs):
+    tokens = own_ref.shape[0]
+    x = place_ref[1]
+    for d, ref in enumerate((own_ref, *text_refs)):
+        ref[...] = jnp.dot(
+            rows_ref[lax.rem(x + d, NX), :tokens, :],
+            weights_ref[...],
+            preferred_element_type=jnp.float32,
+        )
+
+
+def projected_text(place, rows, weights):
+    blocks, count, _ = rows.shape
+    shape = (count - NS * CAP, weights.shape[1])
+    return pl.pallas_call(
+        project_text,
+        grid_spec=pltpu.PrefetchScalarGridSpec(
+            num_scalar_prefetch=1,
+            grid=(1,),
+            in_specs=[IN_VMEM] * 2,
+            out_specs=[IN_VMEM] + [pl.BlockSpec(shape, lambda i, _: (0, 0))] * (blocks - 1),
+        ),
+        out_shape=[pltpu.VMEM(shape, jnp.float32)]
+        + [pltpu.HBM(shape, jnp.float32)] * (blocks - 1),
+        compiler_params=pltpu.CompilerParams(vmem_limit_bytes=16 * MIB),
+        name="project_text",
+    )(place, *map(in_vmem, (rows, weights)))
+
+
+def settle(sums_ref, marks_ref, out_ref):
+    cols = sums_ref.shape[-1]
+    rows = (sums_ref[0] + sums_ref[1]) + (sums_ref[2] + sums_ref[3])
+    for i in range(NS):
+        at = slice(i * CAP, (i + 1) * CAP)
+        out_ref[i, :, :cols] = rows[at].astype(jnp.bfloat16)
+        out_ref[i, :, cols:] = marks_ref[at, :].astype(jnp.bfloat16)
+
+
+def settled(sums, marks):
+    shape = (NS, CAP, sums.shape[-1] + marks.shape[-1])
+    return pl.pallas_call(
+        settle,
+        grid=(1,),
+        in_specs=[IN_VMEM] * 2,
+        out_specs=pl.BlockSpec(shape, lambda i: (0, 0, 0)),
+        out_shape=pltpu.HBM(shape, jnp.bfloat16),
+        compiler_params=pltpu.CompilerParams(vmem_limit_bytes=8 * MIB),
+        name="settle",
+    )(in_vmem(sums), marks)
 
 
 def merge(vis_ref, docs_ref, *refs):
     *text_refs, out_ref = refs
     tokens, cols = text_refs[0].shape
     text = (text_refs[0][...] + text_refs[1][...]) + (text_refs[2][...] + text_refs[3][...])
-    vis = vis_ref[...]
-    vis = (vis[:NS] + vis[NS : 2 * NS]) + (vis[2 * NS : 3 * NS] + vis[3 * NS :])
-    vis = vis.reshape(NS * CAP, vis.shape[-1])
-    slots = vis[:, cols:]
+    vis = vis_ref[...].reshape(NS * CAP, vis_ref.shape[-1])
+    slots = vis[:, cols:].astype(jnp.float32)
     matches = slots == lax.broadcasted_iota(jnp.int32, slots.shape, 1).astype(jnp.float32)
     chooser = matches.astype(jnp.float32).astype(jnp.bfloat16)
     dims = (((0,), (0,)), ((), ()))
-    moved = lax.dot_general(
-        chooser, vis[:, :cols].astype(jnp.bfloat16), dims, preferred_element_type=jnp.float32
-    )
+    moved = lax.dot_general(chooser, vis[:, :cols], dims, preferred_element_type=jnp.float32)
     ones = jnp.ones((slots.shape[0], cols), jnp.bfloat16)
     used = lax.dot_general(chooser, ones, dims, preferred_element_type=jnp.float32)
     out_ref[:tokens, :] = jnp.where(used > 0.5, moved, text).astype(jnp.bfloat16)
@@ -244,8 +277,8 @@
     x = lax.axis_index("grp") // NZ
     where = jnp.stack([place, x])
 
-    part = w_key.shape[0] // 4
-    start = (chip % 4) * part
+    part = w_key.shape[0] // NEAR
+    start = (chip % NEAR) * part
     piece = jnp.where(
         core == 0,
         lax.dynamic_slice_in_dim(w_key, start, part, axis=0),
@@ -255,19 +288,17 @@
 
     rows = exchange_x(packed(hidden, vis_rows))
 
-    far = seq_permute(got, flip(2))
-    pair = jnp.stack([got, far])
-    near = seq_permute(pair, flip(1))
-    four = jnp.concatenate([pair, near])
-    rest = seq_permute(four, sibling)
-
+    mine = lax.all_gather(got, "seq", axis=0, axis_index_groups=OVER_NEAR)
+    other = seq_permute(mine, sibling)
+
+    vis, weights = projected_extra(where, rows, mine, other)
+    vis = exchange_x(vis)
+    text = list(projected_text(where, rows, weights))
+    for d in (2, 1, 3):
+        text[d] = x_permute(text[d], d)
     marks = jnp.broadcast_to(vis_slot.reshape(NS * CAP, 1), (NS * CAP, tokens)).astype(jnp.float32)
-    vis, *text = projection(where, rows, four, rest, marks)
-    vis = lax.all_to_all(
-        vis, ("grp", "seq"), 0, 0, axis_index_groups=OVER_X_SEQ, tiled=True
-    )
-    for d in (2, 1, 3):
-        text[d] = x_permute(in_vmem(text[d]), d)
+    vis = settled(vis, marks)
+    vis = lax.all_to_all(vis, "seq", 0, 0, tiled=True)
     docs = jnp.broadcast_to(jnp.tile(doc_ids, (1, cols // tokens)), (8, cols)).astype(jnp.bfloat16)
     block = merged_block(vis, docs, text)
 

time: 141 us -> 145 us (1.028)
  the two profiles are of different devices: /device:TPU:121 before, /device:TPU:127 now
where the time goes in v3:
time: 145 us; the launch traced here: 144 us
  blocking collectives  51.7 us (36%)
  starting transfers between devices  48 us (33%)
  waiting for transfers between devices  23.8 us (16%)
  Pallas kernels  15.5 us (11%)
  local copies, waits for them, and re-layouts  4.16 us (3%)
    all_gather x1, blocking collectives, program(): got = lax.all_gather(piece, 'grp', axis=0, axis_index_groups=OVER_Z)  38.4 us
    ppermute x6, starting transfers between devices, seq_permute(): return lax.ppermute(array, AXES, pairs)  23.3 us
    all_gather x1, blocking collectives, program(): mine = lax.all_gather(got, 'seq', axis=0, axis_index_groups=OVER_NEAR)  13.2 us
    ppermute x6, waiting for transfers between devices, seq_permute(): return lax.ppermute(array, AXES, pairs)  13 us
    all_to_all x2, starting transfers between devices, exchange_x(): lax.all_to_all(array, 'grp', 0, 0, axis_index_groups=OVER_X, tiled=True)  8.45 us
    ppermute x3, starting transfers between devices, x_permute(): lax.ppermute(array, AXES, [(i, (i + d * step) % size) for i in range(size)])  8.36 us
    all_to_all x1, starting transfers between devices, program(): vis = lax.all_to_all(vis, 'seq', 0, 0, tiled=True)  7.9 us
    ppermute x3, waiting for transfers between devices, x_permute(): lax.ppermute(array, AXES, [(i, (i + d * step) % size) for i in range(size)])  6.94 us
  transfers between devices with their start and end apart: 12, of which 7 were waited for; matrix products, arithmetic and copies ran while one was open for 1% of the time, Pallas kernels for 1%

profile of v3, /device:TPU:127, one launch (start us, length us, event | category | flops | bytes accessed | tf_op | source)
XLA Modules:
  0.0 144.3 jit_solution(1611770040465850126)
XLA Ops:
  0.0 4.2 %pack.1 = bf16[4,192,2048]{2,1,0:T(8,128)(2,1)} custom-call(bf16[128,8192]{1,0:T(8,128)(2,1)} %text_ref.1, bf16[1,16,4,8192]{3,2,1,0:T(4,128)(2,1)} %extra_ref.1), custom_call_target="tpu_custom_call" | custom-call | tf_op jit(solution)/shard_map/pack/pallas_call | solution.py:75
  4.2 4.2 %all-to-all-start = ((bf16[4,192,2048]{2,1,0:T(8,128)(2,1)}), bf16[4,192,2048]{2,1,0:T(8,128)(2,1)S(1)}, u32[]{:S(2)}, u32[]{:S(2)}) async-start(bf16[4,192,2048]{2,1,0:T(8,128)(2,1)} %pack.1), calls=%async_computation | async-start | bytes 6291456 | tf_op jit(solution)/shard_map/all_to_all | solution.py:269
  8.4 0.0 copy-start.5
  8.4 0.0 copy-start.6
  8.4 0.8 dynamic-slice_select_fusion
  9.2 38.4 %all-gather = bf16[512,128]{1,0:T(8,128)(2,1)S(1)} all-gather(bf16[128,128]{1,0:T(8,128)(2,1)S(1)} %dynamic-slice_select_fusion), channel_id=2, replica_groups={{0,64,128,192},{256,320,384,448},{512,576,640,704},{768,832,896,960},{1..., dimensions={0}, use_global_device_ids=true | all-gather | bytes 163840 | tf_op jit(solution)/shard_map/all_gather | solution.py:287
  47.6 13.2 %all-gather.1 = bf16[16,128,128]{2,1,0:T(8,128)(2,1)} all-gather(bf16[4,128,128]{2,1,0:T(8,128)(2,1)S(1)} %bitcast.20), channel_id=3, replica_groups={{0,8,16,24},{4,12,20,28},{32,40,48,56},{36,44,52,60},{1,9,17,25},{5,13,..., dimensions={0}, use_global_device_ids=true | all-gather | bytes 655360 | tf_op jit(solution)/shard_map/all_gather | solution.py:291
  60.9 8.9 %collective-permute-start = (bf16[4,4,128,128]{3,2,1,0:T(8,128)(2,1)}, bf16[4,4,128,128]{3,2,1,0:T(8,128)(2,1)}, u32[]{:S(2)}, u32[]{:S(2)}) collective-permute-start(bf16[4,4,128,128]{3,2,1,0:T(8,128)(2,1)} %bitcast.3.mine_ref), channel_id=1, source_target_pairs={{0,4},{1,5},{2,6},{3,7},{4,0},{5,1},{6,2},{7,3},{8,12},{9,13},{10,... | collective-permute-start | bytes 1572872 | tf_op jit(solution)/shard_map/ppermute | solution.py:37
  69.8 0.1 pad_add_fusion.place_ref
  69.9 1.8 %collective-permute-done.other_ref = bf16[4,4,128,128]{3,2,1,0:T(8,128)(2,1)} collective-permute-done((bf16[4,4,128,128]{3,2,1,0:T(8,128)(2,1)}, bf16[4,4,128,128]{3,2,1,0:T(8,128)(2,1)}, u32[]{:S(2)}, u32[]{:S(2)}) %collective-permute-start) | collective-permute-done | bytes 524320 | tf_op jit(solution)/shard_map/ppermute | solution.py:37
  71.7 0.0 all-to-all-done.rows_ref
  71.7 3.4 %project_extra.1 = (f32[4,64,256]{2,1,0:T(8,128)}, bf16[2048,256]{1,0:T(8,128)(2,1)S(1)}) custom-call(s32[2]{0:T(128)S(1)} %pad_add_fusion.place_ref, bf16[4,192,2048]{2,1,0:T(8,128)(2,1)S(1)} %all-to-all-done.rows_ref, bf16[4,4,128,128]{3,2,1,0:T(8,128)(2,1)} %bitcast.3.mine_ref, bf16[4,4,128,128]{3,2,1,0:T(8,128)(2,1)} %collective-permute-done.other_ref), custom_call_target="tpu_custom_call" | custom-call | tf_op jit(solution)/shard_map/project_extra/pallas_call | solution.py:110
  75.1 0.0 copy-start
  75.1 1.0 copy-done
  76.1 4.2 %all-to-all-start.1 = ((f32[4,64,256]{2,1,0:T(8,128)}), f32[4,64,256]{2,1,0:T(8,128)S(1)}, u32[]{:S(2)}, u32[]{:S(2)}) async-start(f32[4,64,256]{2,1,0:T(8,128)} %get-tuple-element.11), calls=%async_computation.1 | async-start | bytes 524288 | tf_op jit(solution)/shard_map/all_to_all | solution.py:269
  80.4 0.0 copy-done.5
  80.4 0.1 copy.12
  80.5 0.1 convert_element_type.18
  80.5 3.9 %all-to-all-done.1.sums_ref = f32[4,64,256]{2,1,0:T(8,128)S(1)} async-done(((f32[4,64,256]{2,1,0:T(8,128)}), f32[4,64,256]{2,1,0:T(8,128)S(1)}, u32[]{:S(2)}, u32[]{:S(2)}) %all-to-all-start.1) | async-done | bytes 262176 | tf_op jit(solution)/shard_map/all_to_all | solution.py:269
  84.4 0.1 broadcast_in_dim.4.marks_ref
  84.5 0.6 settle.1
  85.1 7.9 %all-to-all-start.2 = ((bf16[16,4,384]{2,1,0:T(4,128)(2,1)}), bf16[16,4,384]{2,1,0:T(4,128)(2,1)S(1)}, u32[]{:S(2)}, u32[]{:S(2)}) async-start(bf16[16,4,384]{2,1,0:T(4,128)(2,1)} %settle.1), calls=%async_computation.2 | async-start | bytes 98304 | tf_op jit(solution)/shard_map/all_to_all | solution.py:301
  93.0 0.0 copy-done.6
  93.0 0.0 copy-start.1
  93.0 1.2 copy-done.1
  94.2 0.0 copy-start.2
  94.2 2.0 %project_text.1 = (f32[128,256]{1,0:T(8,128)S(1)}, f32[128,256]{1,0:T(8,128)}, f32[128,256]{1,0:T(8,128)}, f32[128,256]{1,0:T(8,128)}) custom-call(s32[2]{0:T(128)S(1)} %pad_add_fusion.place_ref, bf16[4,192,2048]{2,1,0:T(8,128)(2,1)S(1)} %all-to-all-done.rows_ref, bf16[2048,256]{1,0:T(8,128)(2,1)S(1)} %copy-done.1), custom_call_target="tpu_custom_call" | custom-call | tf_op jit(solution)/shard_map/project_text/pallas_call | solution.py:138
  96.2 0.0 copy-start.3
  96.2 0.6 copy-done.3
  96.9 3.7 %collective-permute-start.1 = (f32[128,256]{1,0:T(8,128)}, f32[128,256]{1,0:T(8,128)S(1)}, u32[]{:S(2)}, u32[]{:S(2)}) collective-permute-start(f32[128,256]{1,0:T(8,128)} %get-tuple-element.14), channel_id=1, source_target_pairs={{0,256},{1,257},{2,258},{3,259},{4,260},{5,261},{6,262},{7,263},{8... | collective-permute-start | bytes 393224 | tf_op jit(solution)/shard_map/ppermute | solution.py:42
  100.5 1.9 %collective-permute-start.2 = (f32[128,256]{1,0:T(8,128)}, f32[128,256]{1,0:T(8,128)S(1)}, u32[]{:S(2)}, u32[]{:S(2)}) collective-permute-start(f32[128,256]{1,0:T(8,128)} %get-tuple-element.15), channel_id=1, source_target_pairs={{0,512},{1,513},{2,514},{3,515},{4,516},{5,517},{6,518},{7,519},{8... | collective-permute-start | bytes 393224 | tf_op jit(solution)/shard_map/ppermute | solution.py:42
  102.5 2.8 %collective-permute-start.3 = (f32[128,256]{1,0:T(8,128)}, f32[128,256]{1,0:T(8,128)S(1)}, u32[]{:S(2)}, u32[]{:S(2)}) collective-permute-start(f32[128,256]{1,0:T(8,128)} %get-tuple-element.16), channel_id=1, source_target_pairs={{0,768},{1,769},{2,770},{3,771},{4,772},{5,773},{6,774},{7,775},{8... | collective-permute-start | bytes 393224 | tf_op jit(solution)/shard_map/ppermute | solution.py:42
  105.2 0.0 collective-permute-done.1.refs_1_
  105.3 3.3 %collective-permute-done.2.refs_2_ = f32[128,256]{1,0:T(8,128)S(1)} collective-permute-done((f32[128,256]{1,0:T(8,128)}, f32[128,256]{1,0:T(8,128)S(1)}, u32[]{:S(2)}, u32[]{:S(2)}) %collective-permute-start.2) | collective-permute-done | bytes 131104 | tf_op jit(solution)/shard_map/ppermute | solution.py:42
  108.5 3.7 %collective-permute-done.3.refs_3_ = f32[128,256]{1,0:T(8,128)S(1)} collective-permute-done((f32[128,256]{1,0:T(8,128)}, f32[128,256]{1,0:T(8,128)S(1)}, u32[]{:S(2)}, u32[]{:S(2)}) %collective-permute-start.3) | collective-permute-done | bytes 131104 | tf_op jit(solution)/shard_map/ppermute | solution.py:42
  112.2 0.0 all-to-all-done.2.vis_ref
  112.2 0.0 copy-start.4
  112.2 0.9 copy-done.4
  113.1 0.2 merge.1
  113.3 4.3 %collective-permute-start.4 = (bf16[136,256]{1,0:T(8,128)(2,1)S(1)}, bf16[136,256]{1,0:T(8,128)(2,1)S(1)}, u32[]{:S(2)}, u32[]{:S(2)}) collective-permute-start(bf16[136,256]{1,0:T(8,128)(2,1)S(1)} %merge.1), channel_id=1, source_target_pairs={{0,8},{1,9},{2,10},{3,11},{4,12},{5,13},{6,14},{7,15},{8,16},{9,17... | collective-permute-start | bytes 208904 | tf_op jit(solution)/shard_map/ppermute | solution.py:37
  117.6 4.0 %collective-permute-start.5 = (bf16[136,256]{1,0:T(8,128)(2,1)S(1)}, bf16[136,256]{1,0:T(8,128)(2,1)S(1)}, u32[]{:S(2)}, u32[]{:S(2)}) collective-permute-start(bf16[136,256]{1,0:T(8,128)(2,1)S(1)} %merge.1), channel_id=1, source_target_pairs={{0,16},{1,17},{2,18},{3,19},{4,20},{5,21},{6,22},{7,23},{8,24},{9,... | collective-permute-start | bytes 208904 | tf_op jit(solution)/shard_map/ppermute | solution.py:37
  121.6 2.2 %collective-permute-start.6 = (bf16[136,256]{1,0:T(8,128)(2,1)S(1)}, bf16[136,256]{1,0:T(8,128)(2,1)S(1)}, u32[]{:S(2)}, u32[]{:S(2)}) collective-permute-start(bf16[136,256]{1,0:T(8,128)(2,1)S(1)} %merge.1), channel_id=1, source_target_pairs={{0,24},{1,25},{2,26},{3,27},{4,28},{5,29},{6,30},{7,31},{8,32},{9,... | collective-permute-start | bytes 208904 | tf_op jit(solution)/shard_map/ppermute | solution.py:37
  123.9 1.3 collective-permute-start.7
  125.2 0.0 collective-permute-done.4
  125.2 0.0 collective-permute-done.5
  125.2 3.5 %collective-permute-done.6 = bf16[136,256]{1,0:T(8,128)(2,1)S(1)} collective-permute-done((bf16[136,256]{1,0:T(8,128)(2,1)S(1)}, bf16[136,256]{1,0:T(8,128)(2,1)S(1)}, u32[]{:S(2)}, u32[]{:S(2)}) %collective-permute-start.6) | collective-permute-done | bytes 69664 | tf_op jit(solution)/shard_map/ppermute | solution.py:37
  128.7 6.6 %collective-permute-done.7 = bf16[136,256]{1,0:T(8,128)(2,1)S(1)} collective-permute-done((bf16[136,256]{1,0:T(8,128)(2,1)S(1)}, bf16[136,256]{1,0:T(8,128)(2,1)S(1)}, u32[]{:S(2)}, u32[]{:S(2)}) %collective-permute-start.7) | collective-permute-done | bytes 69664 | tf_op jit(solution)/shard_map/ppermute | solution.py:37
  135.3 2.6 %collective-permute-start.8 = (bf16[5,136,256]{2,1,0:T(8,128)(2,1)S(1)}, bf16[5,136,256]{2,1,0:T(8,128)(2,1)S(1)}, u32[]{:S(2)}, u32[]{:S(2)}) collective-permute-start(bf16[5,136,256]{2,1,0:T(8,128)(2,1)S(1)} %bitcast_dynamic-update-slice_fusion.mine_ref), channel_id=1, source_target_pairs={{0,4},{1,5},{2,6},{3,7},{4,0},{5,1},{6,2},{7,3},{8,12},{9,13},{10,... | collective-permute-start | bytes 1044488 | tf_op jit(solution)/shard_map/ppermute | solution.py:37
  137.9 0.1 copy.13.my_docs_ref
  138.0 1.1 collective-permute-done.8.other_ref
  139.2 0.0 copy-done.2
  139.2 5.1 %attend.1 = bf16[128,1024]{1,0:T(8,128)(2,1)} custom-call(s32[2]{0:T(128)S(1)} %pad_add_fusion.place_ref, bf16[128,1024]{1,0:T(8,128)(2,1)S(1)} %copy-done.2, bf16[5,136,256]{2,1,0:T(8,128)(2,1)S(1)} %bitcast_dynamic-update-slice_fusion.mine_ref, bf16[5,136,256]{2,1,0:T(8,128)(2,1)S(1)} %collective-permute-done.8.other_ref, f32[128,1]{1,0:T(8,128)S(1)} %copy.13.my_docs_ref), custom_call_target="tpu_custom_call" | custom-call | tf_op jit(solution)/shard_map/attend/pallas_call | solution.py:244
  (9 shorter events, 0.0 us)
Async XLA Ops:
  4.2 67.5 %all-to-all-start = ((bf16[4,192,2048]{2,1,0:T(8,128)(2,1)}), bf16[4,192,2048]{2,1,0:T(8,128)(2,1)S(1)}, u32[]{:S(2)}, u32[]{:S(2)}) async-start(bf16[4,192,2048]{2,1,0:T(8,128)(2,1)} %pack.1), calls=%async_computation | async-start | bytes 6291456 | tf_op jit(solution)/shard_map/all_to_all | solution.py:269
  8.4 72.0 %copy-start.5 = (s32[1,16,4]{1,2,0:T(4,128)S(1)}, s32[1,16,4]{1,2,0:T(4,128)}, u32[]{:S(2)}) copy-start(s32[1,16,4]{1,2,0:T(4,128)} %param.10) | copy-start | bytes 772
  8.4 84.6 %copy-start.6 = (s32[1,128]{1,0:T(1,128)S(1)}, s32[1,128]{1,0:T(1,128)}, u32[]{:S(2)}) copy-start(s32[1,128]{1,0:T(1,128)} %param.11) | copy-start | bytes 1540
  60.9 10.8 %collective-permute-start = (bf16[4,4,128,128]{3,2,1,0:T(8,128)(2,1)}, bf16[4,4,128,128]{3,2,1,0:T(8,128)(2,1)}, u32[]{:S(2)}, u32[]{:S(2)}) collective-permute-start(bf16[4,4,128,128]{3,2,1,0:T(8,128)(2,1)} %bitcast.3.mine_ref), channel_id=1, source_target_pairs={{0,4},{1,5},{2,6},{3,7},{4,0},{5,1},{6,2},{7,3},{8,12},{9,13},{10,... | collective-permute-start | bytes 1572872 | tf_op jit(solution)/shard_map/ppermute | solution.py:37
  75.1 1.0 copy-start
  76.1 8.3 %all-to-all-start.1 = ((f32[4,64,256]{2,1,0:T(8,128)}), f32[4,64,256]{2,1,0:T(8,128)S(1)}, u32[]{:S(2)}, u32[]{:S(2)}) async-start(f32[4,64,256]{2,1,0:T(8,128)} %get-tuple-element.11), calls=%async_computation.1 | async-start | bytes 524288 | tf_op jit(solution)/shard_map/all_to_all | solution.py:269
  85.1 27.1 %all-to-all-start.2 = ((bf16[16,4,384]{2,1,0:T(4,128)(2,1)}), bf16[16,4,384]{2,1,0:T(4,128)(2,1)S(1)}, u32[]{:S(2)}, u32[]{:S(2)}) async-start(bf16[16,4,384]{2,1,0:T(4,128)(2,1)} %settle.1), calls=%async_computation.2 | async-start | bytes 98304 | tf_op jit(solution)/shard_map/all_to_all | solution.py:301
  93.0 1.2 copy-start.1
  94.2 44.9 %copy-start.2 = (bf16[128,1024]{1,0:T(8,128)(2,1)S(1)}, bf16[128,1024]{1,0:T(8,128)(2,1)}, u32[]{:S(2)}) copy-start(bf16[128,1024]{1,0:T(8,128)(2,1)} %q_ref.1) | copy-start | bytes 786436
  96.2 0.6 copy-start.3
  96.9 8.4 %collective-permute-start.1 = (f32[128,256]{1,0:T(8,128)}, f32[128,256]{1,0:T(8,128)S(1)}, u32[]{:S(2)}, u32[]{:S(2)}) collective-permute-start(f32[128,256]{1,0:T(8,128)} %get-tuple-element.14), channel_id=1, source_target_pairs={{0,256},{1,257},{2,258},{3,259},{4,260},{5,261},{6,262},{7,263},{8... | collective-permute-start | bytes 393224 | tf_op jit(solution)/shard_map/ppermute | solution.py:42
  100.5 8.0 %collective-permute-start.2 = (f32[128,256]{1,0:T(8,128)}, f32[128,256]{1,0:T(8,128)S(1)}, u32[]{:S(2)}, u32[]{:S(2)}) collective-permute-start(f32[128,256]{1,0:T(8,128)} %get-tuple-element.15), channel_id=1, source_target_pairs={{0,512},{1,513},{2,514},{3,515},{4,516},{5,517},{6,518},{7,519},{8... | collective-permute-start | bytes 393224 | tf_op jit(solution)/shard_map/ppermute | solution.py:42
  102.5 9.7 %collective-permute-start.3 = (f32[128,256]{1,0:T(8,128)}, f32[128,256]{1,0:T(8,128)S(1)}, u32[]{:S(2)}, u32[]{:S(2)}) collective-permute-start(f32[128,256]{1,0:T(8,128)} %get-tuple-element.16), channel_id=1, source_target_pairs={{0,768},{1,769},{2,770},{3,771},{4,772},{5,773},{6,774},{7,775},{8... | collective-permute-start | bytes 393224 | tf_op jit(solution)/shard_map/ppermute | solution.py:42
  112.2 0.9 copy-start.4
  113.3 11.8 %collective-permute-start.4 = (bf16[136,256]{1,0:T(8,128)(2,1)S(1)}, bf16[136,256]{1,0:T(8,128)(2,1)S(1)}, u32[]{:S(2)}, u32[]{:S(2)}) collective-permute-start(bf16[136,256]{1,0:T(8,128)(2,1)S(1)} %merge.1), channel_id=1, source_target_pairs={{0,8},{1,9},{2,10},{3,11},{4,12},{5,13},{6,14},{7,15},{8,16},{9,17... | collective-permute-start | bytes 208904 | tf_op jit(solution)/shard_map/ppermute | solution.py:37
  117.6 7.5 %collective-permute-start.5 = (bf16[136,256]{1,0:T(8,128)(2,1)S(1)}, bf16[136,256]{1,0:T(8,128)(2,1)S(1)}, u32[]{:S(2)}, u32[]{:S(2)}) collective-permute-start(bf16[136,256]{1,0:T(8,128)(2,1)S(1)} %merge.1), channel_id=1, source_target_pairs={{0,16},{1,17},{2,18},{3,19},{4,20},{5,21},{6,22},{7,23},{8,24},{9,... | collective-permute-start | bytes 208904 | tf_op jit(solution)/shard_map/ppermute | solution.py:37
  121.6 7.0 %collective-permute-start.6 = (bf16[136,256]{1,0:T(8,128)(2,1)S(1)}, bf16[136,256]{1,0:T(8,128)(2,1)S(1)}, u32[]{:S(2)}, u32[]{:S(2)}) collective-permute-start(bf16[136,256]{1,0:T(8,128)(2,1)S(1)} %merge.1), channel_id=1, source_target_pairs={{0,24},{1,25},{2,26},{3,27},{4,28},{5,29},{6,30},{7,31},{8,32},{9,... | collective-permute-start | bytes 208904 | tf_op jit(solution)/shard_map/ppermute | solution.py:37
  123.9 11.5 %collective-permute-start.7 = (bf16[136,256]{1,0:T(8,128)(2,1)S(1)}, bf16[136,256]{1,0:T(8,128)(2,1)S(1)}, u32[]{:S(2)}, u32[]{:S(2)}) collective-permute-start(bf16[136,256]{1,0:T(8,128)(2,1)S(1)} %merge.1), channel_id=1, source_target_pairs={{0,32},{1,33},{2,34},{3,35},{4,36},{5,37},{6,38},{7,39},{8,40},{9,... | collective-permute-start | bytes 208904 | tf_op jit(solution)/shard_map/ppermute | solution.py:37
  135.3 3.9 %collective-permute-start.8 = (bf16[5,136,256]{2,1,0:T(8,128)(2,1)S(1)}, bf16[5,136,256]{2,1,0:T(8,128)(2,1)S(1)}, u32[]{:S(2)}, u32[]{:S(2)}) collective-permute-start(bf16[5,136,256]{2,1,0:T(8,128)(2,1)S(1)} %bitcast_dynamic-update-slice_fusion.mine_ref), channel_id=1, source_target_pairs={{0,4},{1,5},{2,6},{3,7},{4,0},{5,1},{6,2},{7,3},{8,12},{9,13},{10,... | collective-permute-start | bytes 1044488 | tf_op jit(solution)/shard_map/ppermute | solution.py:37

commit v4 on v3

--- a/solution.py
+++ b/solution.py
@@ -54,6 +54,10 @@
 IN_VMEM = pl.BlockSpec(memory_space=pltpu.VMEM)
 
 
+def whole(shape):
+    return pl.BlockSpec(shape, lambda *_: (0,) * len(shape))
+
+
 def in_vmem(array):
     return pltpu.with_memory_space_constraint(array, pltpu.VMEM)
 
@@ -62,33 +66,77 @@
     return pltpu.with_memory_space_constraint(array, pltpu.HBM)
 
 
-def pack(text_ref, extra_ref, out_ref):
+def pack(place_ref, text_ref, extra_ref, key_ref, value_ref, out_ref, piece_ref, *scratch):
+    extra_in, extra_out, key_part, value_part, text_sem, in_sem, out_sem, piece_sem = scratch
     tokens = text_ref.shape[0]
-    out_ref[0, :tokens, :] = text_ref[...]
-    out_ref[0, tokens:, :] = extra_ref[0].reshape(NS * CAP, -1)
-
-
-def packed(hidden, vis_rows):
+    width = out_ref.shape[2]
+    part = piece_ref.shape[0]
+    s = place_ref[0]
+    rows = pl.ds(pl.multiple_of(lax.rem(s // 2, NEAR) * part, part), part)
+    pieces = [
+        pltpu.make_async_copy(key_ref.at[rows], key_part, piece_sem.at[0]),
+        pltpu.make_async_copy(value_ref.at[rows], value_part, piece_sem.at[1]),
+    ]
+    texts, ins, outs = [], [], []
+    for q in range(NX):
+        cols = pl.ds(q * width, width)
+        ins.append(pltpu.make_async_copy(extra_ref.at[0, :, :, cols], extra_in.at[q], in_sem.at[q]))
+        texts.append(
+            pltpu.make_async_copy(
+                text_ref.at[:, cols], out_ref.at[q, pl.ds(0, tokens)], text_sem.at[q]
+            )
+        )
+        outs.append(
+            pltpu.make_async_copy(
+                extra_out.at[q], out_ref.at[q, pl.ds(tokens, NS * CAP)], out_sem.at[q]
+            )
+        )
+    for copy in (*ins, *texts, *pieces):
+        copy.start()
+    for q in range(NX):
+        ins[q].wait()
+        extra_out[q] = extra_in[q].reshape(NS * CAP, width)
+        outs[q].start()
+    for copy in pieces:
+        copy.wait()
+    piece_ref[...] = jnp.where(lax.rem(s, 2) == 0, key_part[...], value_part[...])
+    for copy in (*texts, *outs):
+        copy.wait()
+
+
+def packed(place, hidden, vis_rows, w_key, w_value):
     tokens, width = hidden.shape
-    count = tokens + NS * CAP
+    extra = NS * CAP
     part = width // NX
+    piece = (w_key.shape[0] // NEAR, w_key.shape[1])
+    kind = hidden.dtype
+    anywhere = pl.BlockSpec(memory_space=pl.ANY)
     return pl.pallas_call(
         pack,
-        grid=(NX,),
-        in_specs=[
-            pl.BlockSpec((tokens, part), lambda i: (0, i)),
-            pl.BlockSpec((1, NS, CAP, part), lambda i: (0, 0, 0, i)),
-        ],
-        out_specs=pl.BlockSpec((1, count, part), lambda i: (i, 0, 0)),
-        out_shape=pltpu.HBM((NX, count, part), hidden.dtype),
+        grid_spec=pltpu.PrefetchScalarGridSpec(
+            num_scalar_prefetch=1,
+            grid=(1,),
+            in_specs=[anywhere] * 4,
+            out_specs=[anywhere, IN_VMEM],
+            scratch_shapes=[
+                pltpu.VMEM((NX, NS, CAP, part), kind),
+                pltpu.VMEM((NX, extra, part), kind),
+                pltpu.VMEM(piece, kind),
+                pltpu.VMEM(piece, kind),
+                pltpu.SemaphoreType.DMA((NX,)),
+                pltpu.SemaphoreType.DMA((NX,)),
+                pltpu.SemaphoreType.DMA((NX,)),
+                pltpu.SemaphoreType.DMA((2,)),
+            ],
+        ),
+        out_shape=[pltpu.HBM((NX, tokens + extra, part), kind), pltpu.VMEM(piece, kind)],
         compiler_params=pltpu.CompilerParams(vmem_limit_bytes=16 * MIB),
         name="pack",
-    )(in_hbm(hidden), in_hbm(vis_rows))
-
-
-def project_extra(place_ref, rows_ref, mine_ref, other_ref, vis_ref, weights_ref):
+    )(place, *map(in_hbm, (hidden, vis_rows, w_key, w_value)))
+
+
+def order(place_ref, mine_ref, other_ref, weights_ref):
     steps, sources, part, cols = mine_ref.shape
-    tokens = rows_ref.shape[1] - NS * CAP
     core = lax.rem(place_ref[0], 2)
     for side, ref in enumerate((mine_ref, other_ref)):
         at = pl.ds(pl.multiple_of(jnp.where(core == side, 0, cols), cols), cols)
@@ -96,6 +144,11 @@
             for z in range(sources):
                 row = (z * steps + k) * part
                 weights_ref[row : row + part, at] = ref[k, z]
+
+
+def project_extra(place_ref, rows_ref, mine_ref, other_ref, vis_ref, weights_ref):
+    tokens = rows_ref.shape[1] - NS * CAP
+    order(place_ref, mine_ref, other_ref, weights_ref)
     weights = weights_ref[...]
     for block in range(NX):
         vis_ref[block] = jnp.dot(
@@ -112,42 +165,45 @@
         grid_spec=pltpu.PrefetchScalarGridSpec(
             num_scalar_prefetch=1,
             grid=(1,),
-            in_specs=[IN_VMEM] * 3,
-            out_specs=[pl.BlockSpec(vis.shape, lambda i, _: (0, 0, 0)), IN_VMEM],
-        ),
-        out_shape=[vis, pltpu.VMEM((part, cols), jnp.bfloat16)],
+            in_specs=[IN_VMEM, whole(mine.shape), whole(other.shape)],
+            out_specs=pl.BlockSpec(vis.shape, lambda i, _: (0, 0, 0)),
+            scratch_shapes=[pltpu.VMEM((part, cols), jnp.bfloat16)],
+        ),
+        out_shape=vis,
         compiler_params=pltpu.CompilerParams(vmem_limit_bytes=16 * MIB),
         name="project_extra",
-    )(place, *map(in_vmem, (rows, mine, other)))
-
-
-def project_text(place_ref, rows_ref, weights_ref, own_ref, *text_refs):
+    )(place, in_vmem(rows), in_hbm(mine), in_hbm(other))
+
+
+def project_text(place_ref, rows_ref, mine_ref, other_ref, own_ref, *refs):
+    *text_refs, weights_ref = refs
     tokens = own_ref.shape[0]
     x = place_ref[1]
+    order(place_ref, mine_ref, other_ref, weights_ref)
+    weights = weights_ref[...]
     for d, ref in enumerate((own_ref, *text_refs)):
         ref[...] = jnp.dot(
-            rows_ref[lax.rem(x + d, NX), :tokens, :],
-            weights_ref[...],
-            preferred_element_type=jnp.float32,
-        )
-
-
-def projected_text(place, rows, weights):
-    blocks, count, _ = rows.shape
-    shape = (count - NS * CAP, weights.shape[1])
+            rows_ref[lax.rem(x + d, NX), :tokens, :], weights, preferred_element_type=jnp.float32
+        )
+
+
+def projected_text(place, rows, mine, other):
+    blocks, count, part = rows.shape
+    shape = (count - NS * CAP, 2 * mine.shape[-1])
     return pl.pallas_call(
         project_text,
         grid_spec=pltpu.PrefetchScalarGridSpec(
             num_scalar_prefetch=1,
             grid=(1,),
-            in_specs=[IN_VMEM] * 2,
+            in_specs=[IN_VMEM, whole(mine.shape), whole(other.shape)],
             out_specs=[IN_VMEM] + [pl.BlockSpec(shape, lambda i, _: (0, 0))] * (blocks - 1),
+            scratch_shapes=[pltpu.VMEM((part, shape[1]), jnp.bfloat16)],
         ),
         out_shape=[pltpu.VMEM(shape, jnp.float32)]
         + [pltpu.HBM(shape, jnp.float32)] * (blocks - 1),
         compiler_params=pltpu.CompilerParams(vmem_limit_bytes=16 * MIB),
         name="project_text",
-    )(place, *map(in_vmem, (rows, weights)))
+    )(place, in_vmem(rows), in_hbm(mine), in_hbm(other))
 
 
 def settle(sums_ref, marks_ref, out_ref):
@@ -262,7 +318,7 @@
         out_shape=jax.ShapeDtypeStruct(queries.shape, jnp.bfloat16),
         compiler_params=pltpu.CompilerParams(vmem_limit_bytes=16 * MIB),
         name="attend",
-    )(place, queries, in_vmem(mine), in_vmem(other), my_docs)
+    )(place, in_hbm(queries), in_vmem(mine), in_vmem(other), my_docs)
 
 
 def exchange_x(array):
@@ -272,28 +328,19 @@
 def program(hidden, queries, vis_rows, vis_slot, doc_ids, w_key, w_value):
     tokens = hidden.shape[0]
     cols = 2 * w_key.shape[1]
-    place = lax.axis_index("seq")
-    core, chip = place % 2, place // 2
-    x = lax.axis_index("grp") // NZ
-    where = jnp.stack([place, x])
-
-    part = w_key.shape[0] // NEAR
-    start = (chip % NEAR) * part
-    piece = jnp.where(
-        core == 0,
-        lax.dynamic_slice_in_dim(w_key, start, part, axis=0),
-        lax.dynamic_slice_in_dim(w_value, start, part, axis=0),
-    )
+    where = jnp.stack([lax.axis_index("seq"), lax.axis_index("grp") // NZ])
+    rows, piece = packed(where, hidden, vis_rows, w_key, w_value)
+
     got = lax.all_gather(piece, "grp", axis=0, axis_index_groups=OVER_Z)
 
-    rows = exchange_x(packed(hidden, vis_rows))
+    rows = exchange_x(rows)
 
     mine = lax.all_gather(got, "seq", axis=0, axis_index_groups=OVER_NEAR)
     other = seq_permute(mine, sibling)
 
-    vis, weights = projected_extra(where, rows, mine, other)
+    vis = projected_extra(where, rows, mine, other)
     vis = exchange_x(vis)
-    text = list(projected_text(where, rows, weights))
+    text = list(projected_text(where, rows, mine, other))
     for d in (2, 1, 3):
         text[d] = x_permute(text[d], d)
     marks = jnp.broadcast_to(vis_slot.reshape(NS * CAP, 1), (NS * CAP, tokens)).astype(jnp.float32)
@@ -302,7 +349,9 @@
     docs = jnp.broadcast_to(jnp.tile(doc_ids, (1, cols // tokens)), (8, cols)).astype(jnp.bfloat16)
     block = merged_block(vis, docs, text)
 
-    back = [seq_permute(block, later(d)) for d in range(1, REACH + 1)]
+    back = [None] * REACH
+    for d in range(REACH, 0, -1):
+        back[d - 1] = seq_permute(block, later(d))
     mine = jnp.stack([block, *back])
     other = seq_permute(mine, sibling)
     my_docs = doc_ids.reshape(tokens, 1).astype(jnp.float32)

time: 145 us -> 203 us (1.40)
  Pallas kernels: 15.5 us -> 79.1 us
  local copies, waits for them, and re-layouts: 4.16 us -> 0.41 us
    pallas_call x1, Pallas kernels: 4.17 us -> 65.3 us  [packed(): pl.pallas_call(pack, grid_spec=pltpu.PrefetchScalarGridSpec(num_scalar_pr...]
    unnamed x18 -> x10, local copies, waits for them, and re-layouts: 3.79 us -> 0.04 us
  transfers between devices with their start and end apart: 12 -> 12, of which waited for: 7 -> 7; matrix products, arithmetic and copies ran while one was open for 1% -> 0% of each run, Pallas kernels for 1% -> 2%
where the time goes in v4:
time: 203 us
  Pallas kernels  79.1 us (39%)
  blocking collectives  51.1 us (25%)
  starting transfers between devices  47.9 us (24%)
  waiting for transfers between devices  24 us (12%)
    pallas_call x1, Pallas kernels, packed(): pl.pallas_call(pack, grid_spec=pltpu.PrefetchScalarGridSpec(num_scalar_pr...  65.3 us
    all_gather x1, blocking collectives, program(): got = lax.all_gather(piece, 'grp', axis=0, axis_index_groups=OVER_Z)  38.6 us
    ppermute x6, starting transfers between devices, seq_permute(): return lax.ppermute(array, AXES, pairs)  23 us
    ppermute x6, waiting for transfers between devices, seq_permute(): return lax.ppermute(array, AXES, pairs)  12.9 us
    all_gather x1, blocking collectives, program(): mine = lax.all_gather(got, 'seq', axis=0, axis_index_groups=OVER_NEAR)  12.5 us
    all_to_all x2, starting transfers between devices, exchange_x(): lax.all_to_all(array, 'grp', 0, 0, axis_index_groups=OVER_X, tiled=True)  9.01 us
    ppermute x3, starting transfers between devices, x_permute(): lax.ppermute(array, AXES, [(i, (i + d * step) % size) for i in range(size)])  8.37 us
    all_to_all x1, starting transfers between devices, program(): vis = lax.all_to_all(vis, 'seq', 0, 0, tiled=True)  7.49 us
  transfers between devices with their start and end apart: 12, of which 7 were waited for; matrix products, arithmetic and copies ran while one was open for 0% of the time, Pallas kernels for 2%

profile of v4, /device:TPU:127, one launch (start us, length us, event | category | flops | bytes accessed | tf_op | source)
XLA Modules:
  0.0 202.7 jit_solution(12217708212900945363)
XLA Ops:
  0.0 0.1 pad_add_fusion.place_ref
  0.1 65.3 %pack.1 = (bf16[4,192,2048]{2,1,0:T(8,128)(2,1)}, bf16[128,128]{1,0:T(8,128)(2,1)S(1)}) custom-call(s32[2]{0:T(128)S(1)} %pad_add_fusion.place_ref, bf16[128,8192]{1,0:T(8,128)(2,1)} %text_ref.1, bf16[1,16,4,8192]{3,2,1,0:T(4,128)(2,1)} %extra_ref.1, bf16[512,128]{1,0:T(8,128)(2,1)} %key_ref.1, bf16[512,128]{1,0:T(8,128)(2,1)} %value_ref.1), custom_call_target="tpu_custom_call" | custom-call | tf_op jit(solution)/shard_map/pack/pallas_call | solution.py:114
  65.4 4.2 %all-to-all-start = ((bf16[4,192,2048]{2,1,0:T(8,128)(2,1)}), bf16[4,192,2048]{2,1,0:T(8,128)(2,1)S(1)}, u32[]{:S(2)}, u32[]{:S(2)}) async-start(bf16[4,192,2048]{2,1,0:T(8,128)(2,1)} %get-tuple-element.11), calls=%async_computation | async-start | bytes 6291456 | tf_op jit(solution)/shard_map/all_to_all | solution.py:325
  69.6 0.0 copy-start.1
  69.6 0.0 copy-start.2
  69.6 38.6 %all-gather = bf16[512,128]{1,0:T(8,128)(2,1)S(1)} all-gather(bf16[128,128]{1,0:T(8,128)(2,1)S(1)} %get-tuple-element.12), channel_id=2, replica_groups={{0,64,128,192},{256,320,384,448},{512,576,640,704},{768,832,896,960},{1..., dimensions={0}, use_global_device_ids=true | all-gather | bytes 163840 | tf_op jit(solution)/shard_map/all_gather | solution.py:334
  108.2 12.5 %all-gather.1 = bf16[16,128,128]{2,1,0:T(8,128)(2,1)S(1)} all-gather(bf16[4,128,128]{2,1,0:T(8,128)(2,1)S(1)} %bitcast.23), channel_id=3, replica_groups={{0,8,16,24},{4,12,20,28},{32,40,48,56},{36,44,52,60},{1,9,17,25},{5,13,..., dimensions={0}, use_global_device_ids=true | all-gather | bytes 655360 | tf_op jit(solution)/shard_map/all_gather | solution.py:338
  120.7 0.0 copy-start
  120.7 8.7 %collective-permute-start = (bf16[4,4,128,128]{3,2,1,0:T(8,128)(2,1)S(1)}, bf16[4,4,128,128]{3,2,1,0:T(8,128)(2,1)}, u32[]{:S(2)}, u32[]{:S(2)}) collective-permute-start(bf16[4,4,128,128]{3,2,1,0:T(8,128)(2,1)S(1)} %bitcast.20), channel_id=1, source_target_pairs={{0,4},{1,5},{2,6},{3,7},{4,0},{5,1},{6,2},{7,3},{8,12},{9,13},{10,... | collective-permute-start | bytes 1572872 | tf_op jit(solution)/shard_map/ppermute | solution.py:37
  129.4 0.0 copy-done
  129.4 1.6 collective-permute-done.other_ref
  131.0 0.0 all-to-all-done.rows_ref
  131.0 3.5 %project_extra.1 = f32[4,64,256]{2,1,0:T(8,128)} custom-call(s32[2]{0:T(128)S(1)} %pad_add_fusion.place_ref, bf16[4,192,2048]{2,1,0:T(8,128)(2,1)S(1)} %all-to-all-done.rows_ref, bf16[4,4,128,128]{3,2,1,0:T(8,128)(2,1)} %bitcast.21, bf16[4,4,128,128]{3,2,1,0:T(8,128)(2,1)} %collective-permute-done.other_ref), custom_call_target="tpu_custom_call" | custom-call | tf_op jit(solution)/shard_map/project_extra/pallas_call | solution.py:163
  134.5 4.8 %all-to-all-start.1 = ((f32[4,64,256]{2,1,0:T(8,128)}), f32[4,64,256]{2,1,0:T(8,128)S(1)}, u32[]{:S(2)}, u32[]{:S(2)}) async-start(f32[4,64,256]{2,1,0:T(8,128)} %project_extra.1), calls=%async_computation.1 | async-start | bytes 524288 | tf_op jit(solution)/shard_map/all_to_all | solution.py:325
  139.3 0.0 copy-done.1
  139.3 0.1 copy.12
  139.4 0.1 convert_element_type.18
  139.5 4.1 %all-to-all-done.1.sums_ref = f32[4,64,256]{2,1,0:T(8,128)S(1)} async-done(((f32[4,64,256]{2,1,0:T(8,128)}), f32[4,64,256]{2,1,0:T(8,128)S(1)}, u32[]{:S(2)}, u32[]{:S(2)}) %all-to-all-start.1) | async-done | bytes 262176 | tf_op jit(solution)/shard_map/all_to_all | solution.py:325
  143.6 0.1 broadcast_in_dim.4.marks_ref
  143.7 0.6 settle.1
  144.3 7.5 %all-to-all-start.2 = ((bf16[16,4,384]{2,1,0:T(4,128)(2,1)}), bf16[16,4,384]{2,1,0:T(4,128)(2,1)S(1)}, u32[]{:S(2)}, u32[]{:S(2)}) async-start(bf16[16,4,384]{2,1,0:T(4,128)(2,1)} %settle.1), calls=%async_computation.2 | async-start | bytes 98304 | tf_op jit(solution)/shard_map/all_to_all | solution.py:348
  151.8 0.0 copy-done.2
  151.8 3.5 %project_text.1 = (f32[128,256]{1,0:T(8,128)S(1)}, f32[128,256]{1,0:T(8,128)}, f32[128,256]{1,0:T(8,128)}, f32[128,256]{1,0:T(8,128)}) custom-call(s32[2]{0:T(128)S(1)} %pad_add_fusion.place_ref, bf16[4,192,2048]{2,1,0:T(8,128)(2,1)S(1)} %all-to-all-done.rows_ref, bf16[4,4,128,128]{3,2,1,0:T(8,128)(2,1)} %bitcast.22, ...), custom_call_target="tpu_custom_call" | custom-call | tf_op jit(solution)/shard_map/project_text/pallas_call | solution.py:193
  155.3 3.7 %collective-permute-start.1 = (f32[128,256]{1,0:T(8,128)}, f32[128,256]{1,0:T(8,128)S(1)}, u32[]{:S(2)}, u32[]{:S(2)}) collective-permute-start(f32[128,256]{1,0:T(8,128)} %get-tuple-element.14), channel_id=1, source_target_pairs={{0,256},{1,257},{2,258},{3,259},{4,260},{5,261},{6,262},{7,263},{8... | collective-permute-start | bytes 393224 | tf_op jit(solution)/shard_map/ppermute | solution.py:42
  159.0 1.9 collective-permute-start.2
  160.9 2.8 %collective-permute-start.3 = (f32[128,256]{1,0:T(8,128)}, f32[128,256]{1,0:T(8,128)S(1)}, u32[]{:S(2)}, u32[]{:S(2)}) collective-permute-start(f32[128,256]{1,0:T(8,128)} %get-tuple-element.16), channel_id=1, source_target_pairs={{0,768},{1,769},{2,770},{3,771},{4,772},{5,773},{6,774},{7,775},{8... | collective-permute-start | bytes 393224 | tf_op jit(solution)/shard_map/ppermute | solution.py:42
  163.7 0.0 collective-permute-done.1.refs_1_
  163.7 3.3 %collective-permute-done.2.refs_2_ = f32[128,256]{1,0:T(8,128)S(1)} collective-permute-done((f32[128,256]{1,0:T(8,128)}, f32[128,256]{1,0:T(8,128)S(1)}, u32[]{:S(2)}, u32[]{:S(2)}) %collective-permute-start.2) | collective-permute-done | bytes 131104 | tf_op jit(solution)/shard_map/ppermute | solution.py:42
  167.0 3.7 %collective-permute-done.3.refs_3_ = f32[128,256]{1,0:T(8,128)S(1)} collective-permute-done((f32[128,256]{1,0:T(8,128)}, f32[128,256]{1,0:T(8,128)S(1)}, u32[]{:S(2)}, u32[]{:S(2)}) %collective-permute-start.3) | collective-permute-done | bytes 131104 | tf_op jit(solution)/shard_map/ppermute | solution.py:42
  170.7 0.0 all-to-all-done.2.vis_ref
  170.7 0.2 merge.1
  170.9 4.3 %collective-permute-start.4 = (bf16[136,256]{1,0:T(8,128)(2,1)S(1)}, bf16[136,256]{1,0:T(8,128)(2,1)S(1)}, u32[]{:S(2)}, u32[]{:S(2)}) collective-permute-start(bf16[136,256]{1,0:T(8,128)(2,1)S(1)} %merge.1), channel_id=1, source_target_pairs={{0,8},{1,9},{2,10},{3,11},{4,12},{5,13},{6,14},{7,15},{8,16},{9,17... | collective-permute-start | bytes 208904 | tf_op jit(solution)/shard_map/ppermute | solution.py:37
  175.2 4.0 %collective-permute-start.5 = (bf16[136,256]{1,0:T(8,128)(2,1)S(1)}, bf16[136,256]{1,0:T(8,128)(2,1)S(1)}, u32[]{:S(2)}, u32[]{:S(2)}) collective-permute-start(bf16[136,256]{1,0:T(8,128)(2,1)S(1)} %merge.1), channel_id=1, source_target_pairs={{0,16},{1,17},{2,18},{3,19},{4,20},{5,21},{6,22},{7,23},{8,24},{9,... | collective-permute-start | bytes 208904 | tf_op jit(solution)/shard_map/ppermute | solution.py:37
  179.2 2.2 %collective-permute-start.6 = (bf16[136,256]{1,0:T(8,128)(2,1)S(1)}, bf16[136,256]{1,0:T(8,128)(2,1)S(1)}, u32[]{:S(2)}, u32[]{:S(2)}) collective-permute-start(bf16[136,256]{1,0:T(8,128)(2,1)S(1)} %merge.1), channel_id=1, source_target_pairs={{0,24},{1,25},{2,26},{3,27},{4,28},{5,29},{6,30},{7,31},{8,32},{9,... | collective-permute-start | bytes 208904 | tf_op jit(solution)/shard_map/ppermute | solution.py:37
  181.4 1.3 collective-permute-start.7
  182.7 0.0 collective-permute-done.4
  182.7 0.0 collective-permute-done.5
  182.8 3.5 %collective-permute-done.6 = bf16[136,256]{1,0:T(8,128)(2,1)S(1)} collective-permute-done((bf16[136,256]{1,0:T(8,128)(2,1)S(1)}, bf16[136,256]{1,0:T(8,128)(2,1)S(1)}, u32[]{:S(2)}, u32[]{:S(2)}) %collective-permute-start.6) | collective-permute-done | bytes 69664 | tf_op jit(solution)/shard_map/ppermute | solution.py:37
  186.2 6.6 %collective-permute-done.7 = bf16[136,256]{1,0:T(8,128)(2,1)S(1)} collective-permute-done((bf16[136,256]{1,0:T(8,128)(2,1)S(1)}, bf16[136,256]{1,0:T(8,128)(2,1)S(1)}, u32[]{:S(2)}, u32[]{:S(2)}) %collective-permute-start.7) | collective-permute-done | bytes 69664 | tf_op jit(solution)/shard_map/ppermute | solution.py:37
  192.9 2.6 %collective-permute-start.8 = (bf16[5,136,256]{2,1,0:T(8,128)(2,1)S(1)}, bf16[5,136,256]{2,1,0:T(8,128)(2,1)S(1)}, u32[]{:S(2)}, u32[]{:S(2)}) collective-permute-start(bf16[5,136,256]{2,1,0:T(8,128)(2,1)S(1)} %bitcast_dynamic-update-slice_fusion.mine_ref), channel_id=1, source_target_pairs={{0,4},{1,5},{2,6},{3,7},{4,0},{5,1},{6,2},{7,3},{8,12},{9,13},{10,... | collective-permute-start | bytes 1044488 | tf_op jit(solution)/shard_map/ppermute | solution.py:37
  195.5 0.1 copy.13.my_docs_ref
  195.6 1.1 collective-permute-done.8.other_ref
  196.7 6.0 %attend.1 = bf16[128,1024]{1,0:T(8,128)(2,1)} custom-call(s32[2]{0:T(128)S(1)} %pad_add_fusion.place_ref, bf16[128,1024]{1,0:T(8,128)(2,1)} %q_ref.1, bf16[5,136,256]{2,1,0:T(8,128)(2,1)S(1)} %bitcast_dynamic-update-slice_fusion.mine_ref, bf16[5,136,256]{2,1,0:T(8,128)(2,1)S(1)} %collective-permute-done.8.other_ref, f32[128,1]{1,0:T(8,128)S(1)} %copy.13.my_docs_ref), custom_call_target="tpu_custom_call" | custom-call | tf_op jit(solution)/shard_map/attend/pallas_call | solution.py:300
  (9 shorter events, 0.0 us)
Async XLA Ops:
  65.4 65.6 %all-to-all-start = ((bf16[4,192,2048]{2,1,0:T(8,128)(2,1)}), bf16[4,192,2048]{2,1,0:T(8,128)(2,1)S(1)}, u32[]{:S(2)}, u32[]{:S(2)}) async-start(bf16[4,192,2048]{2,1,0:T(8,128)(2,1)} %get-tuple-element.11), calls=%async_computation | async-start | bytes 6291456 | tf_op jit(solution)/shard_map/all_to_all | solution.py:325
  69.6 69.7 %copy-start.1 = (s32[1,16,4]{1,2,0:T(4,128)S(1)}, s32[1,16,4]{1,2,0:T(4,128)}, u32[]{:S(2)}) copy-start(s32[1,16,4]{1,2,0:T(4,128)} %param.10) | copy-start | bytes 772
  69.6 82.2 %copy-start.2 = (s32[1,128]{1,0:T(1,128)S(1)}, s32[1,128]{1,0:T(1,128)}, u32[]{:S(2)}) copy-start(s32[1,128]{1,0:T(1,128)} %param.11) | copy-start | bytes 1540
  120.7 8.7 %copy-start = (bf16[16,128,128]{2,1,0:T(8,128)(2,1)}, bf16[16,128,128]{2,1,0:T(8,128)(2,1)S(1)}, u32[]{:S(2)}) copy-start(bf16[16,128,128]{2,1,0:T(8,128)(2,1)S(1)} %all-gather.1) | copy-start | bytes 1572868
  120.7 10.3 %collective-permute-start = (bf16[4,4,128,128]{3,2,1,0:T(8,128)(2,1)S(1)}, bf16[4,4,128,128]{3,2,1,0:T(8,128)(2,1)}, u32[]{:S(2)}, u32[]{:S(2)}) collective-permute-start(bf16[4,4,128,128]{3,2,1,0:T(8,128)(2,1)S(1)} %bitcast.20), channel_id=1, source_target_pairs={{0,4},{1,5},{2,6},{3,7},{4,0},{5,1},{6,2},{7,3},{8,12},{9,13},{10,... | collective-permute-start | bytes 1572872 | tf_op jit(solution)/shard_map/ppermute | solution.py:37
  134.5 9.1 %all-to-all-start.1 = ((f32[4,64,256]{2,1,0:T(8,128)}), f32[4,64,256]{2,1,0:T(8,128)S(1)}, u32[]{:S(2)}, u32[]{:S(2)}) async-start(f32[4,64,256]{2,1,0:T(8,128)} %project_extra.1), calls=%async_computation.1 | async-start | bytes 524288 | tf_op jit(solution)/shard_map/all_to_all | solution.py:325
  144.3 26.3 %all-to-all-start.2 = ((bf16[16,4,384]{2,1,0:T(4,128)(2,1)}), bf16[16,4,384]{2,1,0:T(4,128)(2,1)S(1)}, u32[]{:S(2)}, u32[]{:S(2)}) async-start(bf16[16,4,384]{2,1,0:T(4,128)(2,1)} %settle.1), calls=%async_computation.2 | async-start | bytes 98304 | tf_op jit(solution)/shard_map/all_to_all | solution.py:348
  155.3 8.4 %collective-permute-start.1 = (f32[128,256]{1,0:T(8,128)}, f32[128,256]{1,0:T(8,128)S(1)}, u32[]{:S(2)}, u32[]{:S(2)}) collective-permute-start(f32[128,256]{1,0:T(8,128)} %get-tuple-element.14), channel_id=1, source_target_pairs={{0,256},{1,257},{2,258},{3,259},{4,260},{5,261},{6,262},{7,263},{8... | collective-permute-start | bytes 393224 | tf_op jit(solution)/shard_map/ppermute | solution.py:42
  159.0 8.0 %collective-permute-start.2 = (f32[128,256]{1,0:T(8,128)}, f32[128,256]{1,0:T(8,128)S(1)}, u32[]{:S(2)}, u32[]{:S(2)}) collective-permute-start(f32[128,256]{1,0:T(8,128)} %get-tuple-element.15), channel_id=1, source_target_pairs={{0,512},{1,513},{2,514},{3,515},{4,516},{5,517},{6,518},{7,519},{8... | collective-permute-start | bytes 393224 | tf_op jit(solution)/shard_map/ppermute | solution.py:42
  160.9 9.7 %collective-permute-start.3 = (f32[128,256]{1,0:T(8,128)}, f32[128,256]{1,0:T(8,128)S(1)}, u32[]{:S(2)}, u32[]{:S(2)}) collective-permute-start(f32[128,256]{1,0:T(8,128)} %get-tuple-element.16), channel_id=1, source_target_pairs={{0,768},{1,769},{2,770},{3,771},{4,772},{5,773},{6,774},{7,775},{8... | collective-permute-start | bytes 393224 | tf_op jit(solution)/shard_map/ppermute | solution.py:42
  170.9 11.8 %collective-permute-start.4 = (bf16[136,256]{1,0:T(8,128)(2,1)S(1)}, bf16[136,256]{1,0:T(8,128)(2,1)S(1)}, u32[]{:S(2)}, u32[]{:S(2)}) collective-permute-start(bf16[136,256]{1,0:T(8,128)(2,1)S(1)} %merge.1), channel_id=1, source_target_pairs={{0,8},{1,9},{2,10},{3,11},{4,12},{5,13},{6,14},{7,15},{8,16},{9,17... | collective-permute-start | bytes 208904 | tf_op jit(solution)/shard_map/ppermute | solution.py:37
  175.2 7.5 %collective-permute-start.5 = (bf16[136,256]{1,0:T(8,128)(2,1)S(1)}, bf16[136,256]{1,0:T(8,128)(2,1)S(1)}, u32[]{:S(2)}, u32[]{:S(2)}) collective-permute-start(bf16[136,256]{1,0:T(8,128)(2,1)S(1)} %merge.1), channel_id=1, source_target_pairs={{0,16},{1,17},{2,18},{3,19},{4,20},{5,21},{6,22},{7,23},{8,24},{9,... | collective-permute-start | bytes 208904 | tf_op jit(solution)/shard_map/ppermute | solution.py:37
  179.2 7.0 %collective-permute-start.6 = (bf16[136,256]{1,0:T(8,128)(2,1)S(1)}, bf16[136,256]{1,0:T(8,128)(2,1)S(1)}, u32[]{:S(2)}, u32[]{:S(2)}) collective-permute-start(bf16[136,256]{1,0:T(8,128)(2,1)S(1)} %merge.1), channel_id=1, source_target_pairs={{0,24},{1,25},{2,26},{3,27},{4,28},{5,29},{6,30},{7,31},{8,32},{9,... | collective-permute-start | bytes 208904 | tf_op jit(solution)/shard_map/ppermute | solution.py:37
  181.4 11.5 %collective-permute-start.7 = (bf16[136,256]{1,0:T(8,128)(2,1)S(1)}, bf16[136,256]{1,0:T(8,128)(2,1)S(1)}, u32[]{:S(2)}, u32[]{:S(2)}) collective-permute-start(bf16[136,256]{1,0:T(8,128)(2,1)S(1)} %merge.1), channel_id=1, source_target_pairs={{0,32},{1,33},{2,34},{3,35},{4,36},{5,37},{6,38},{7,39},{8,40},{9,... | collective-permute-start | bytes 208904 | tf_op jit(solution)/shard_map/ppermute | solution.py:37
  192.9 3.9 %collective-permute-start.8 = (bf16[5,136,256]{2,1,0:T(8,128)(2,1)S(1)}, bf16[5,136,256]{2,1,0:T(8,128)(2,1)S(1)}, u32[]{:S(2)}, u32[]{:S(2)}) collective-permute-start(bf16[5,136,256]{2,1,0:T(8,128)(2,1)S(1)} %bitcast_dynamic-update-slice_fusion.mine_ref), channel_id=1, source_target_pairs={{0,4},{1,5},{2,6},{3,7},{4,0},{5,1},{6,2},{7,3},{8,12},{9,13},{10,... | collective-permute-start | bytes 1044488 | tf_op jit(solution)/shard_map/ppermute | solution.py:37

commit v5 on v4

--- a/solution.py
+++ b/solution.py
@@ -19,7 +19,7 @@
 AXES = ("grp", "seq", "tp")
 OVER_X = [[x * NZ + z for x in range(NX)] for z in range(NZ)]
 OVER_Z = [[x * NZ + z for z in range(NZ)] for x in range(NX)]
-NEAR = 4
+NEAR = 2
 OVER_NEAR = [
     [(first + i) * 2 + core for i in range(NEAR)] for first in range(0, NLO, NEAR) for core in range(2)
 ]
@@ -67,7 +67,7 @@
 
 
 def pack(place_ref, text_ref, extra_ref, key_ref, value_ref, out_ref, piece_ref, *scratch):
-    extra_in, extra_out, key_part, value_part, text_sem, in_sem, out_sem, piece_sem = scratch
+    extra_in, parts, key_part, value_part, text_sem, in_sem, out_sem, piece_sem = scratch
     tokens = text_ref.shape[0]
     width = out_ref.shape[2]
     part = piece_ref.shape[0]
@@ -82,31 +82,29 @@
         cols = pl.ds(q * width, width)
         ins.append(pltpu.make_async_copy(extra_ref.at[0, :, :, cols], extra_in.at[q], in_sem.at[q]))
         texts.append(
-            pltpu.make_async_copy(
-                text_ref.at[:, cols], out_ref.at[q, pl.ds(0, tokens)], text_sem.at[q]
-            )
-        )
-        outs.append(
-            pltpu.make_async_copy(
-                extra_out.at[q], out_ref.at[q, pl.ds(tokens, NS * CAP)], out_sem.at[q]
-            )
-        )
-    for copy in (*ins, *texts, *pieces):
+            pltpu.make_async_copy(text_ref.at[:, cols], parts.at[q, pl.ds(0, tokens)], text_sem.at[q])
+        )
+        outs.append(pltpu.make_async_copy(parts.at[q], out_ref.at[q], out_sem.at[q]))
+    for q in range(NX):
+        ins[q].start()
+        texts[q].start()
+    for copy in pieces:
         copy.start()
     for q in range(NX):
         ins[q].wait()
-        extra_out[q] = extra_in[q].reshape(NS * CAP, width)
+        parts[q, tokens:] = extra_in[q].reshape(NS * CAP, width)
+        texts[q].wait()
         outs[q].start()
     for copy in pieces:
         copy.wait()
     piece_ref[...] = jnp.where(lax.rem(s, 2) == 0, key_part[...], value_part[...])
-    for copy in (*texts, *outs):
+    for copy in outs:
         copy.wait()
 
 
 def packed(place, hidden, vis_rows, w_key, w_value):
     tokens, width = hidden.shape
-    extra = NS * CAP
+    count = tokens + NS * CAP
     part = width // NX
     piece = (w_key.shape[0] // NEAR, w_key.shape[1])
     kind = hidden.dtype
@@ -120,7 +118,7 @@
             out_specs=[anywhere, IN_VMEM],
             scratch_shapes=[
                 pltpu.VMEM((NX, NS, CAP, part), kind),
-                pltpu.VMEM((NX, extra, part), kind),
+                pltpu.VMEM((NX, count, part), kind),
                 pltpu.VMEM(piece, kind),
                 pltpu.VMEM(piece, kind),
                 pltpu.SemaphoreType.DMA((NX,)),
@@ -129,7 +127,7 @@
                 pltpu.SemaphoreType.DMA((2,)),
             ],
         ),
-        out_shape=[pltpu.HBM((NX, tokens + extra, part), kind), pltpu.VMEM(piece, kind)],
+        out_shape=[pltpu.HBM((NX, count, part), kind), pltpu.VMEM(piece, kind)],
         compiler_params=pltpu.CompilerParams(vmem_limit_bytes=16 * MIB),
         name="pack",
     )(place, *map(in_hbm, (hidden, vis_rows, w_key, w_value)))

time: 203 us -> 140 us (0.69)
  the two profiles are of different devices: /device:TPU:127 before, /device:TPU:103 now
where the time goes in v5:
time: 140 us; the launch traced here: 139 us
  starting transfers between devices  50.2 us (36%)
  blocking collectives  47.2 us (34%)
  waiting for transfers between devices  24 us (17%)
  Pallas kernels  17.2 us (12%)
    all_gather x1, blocking collectives, program(): got = lax.all_gather(piece, 'grp', axis=0, axis_index_groups=OVER_Z)  40.5 us
    ppermute x6, starting transfers between devices, seq_permute(): return lax.ppermute(array, AXES, pairs)  21.4 us
    ppermute x6, waiting for transfers between devices, seq_permute(): return lax.ppermute(array, AXES, pairs)  12.9 us
    all_to_all x2, starting transfers between devices, exchange_x(): lax.all_to_all(array, 'grp', 0, 0, axis_index_groups=OVER_X, tiled=True)  10.5 us
    all_to_all x1, starting transfers between devices, program(): vis = lax.all_to_all(vis, 'seq', 0, 0, tiled=True)  9.87 us
    ppermute x3, starting transfers between devices, x_permute(): lax.ppermute(array, AXES, [(i, (i + d * step) % size) for i in range(size)])  8.36 us
    ppermute x3, waiting for transfers between devices, x_permute(): lax.ppermute(array, AXES, [(i, (i + d * step) % size) for i in range(size)])  6.94 us
    all_gather x1, blocking collectives, program(): mine = lax.all_gather(got, 'seq', axis=0, axis_index_groups=OVER_NEAR)  6.69 us
  transfers between devices with their start and end apart: 12, of which 7 were waited for; matrix products, arithmetic and copies ran while one was open for 0% of the time, Pallas kernels for 2%

profile of v5, /device:TPU:103, one launch (start us, length us, event | category | flops | bytes accessed | tf_op | source)
XLA Modules:
  0.0 139.2 jit_solution(361158397177503066)
XLA Ops:
  0.0 0.1 pad_add_fusion.place_ref
  0.1 3.4 %pack.1 = (bf16[4,192,2048]{2,1,0:T(8,128)(2,1)}, bf16[256,128]{1,0:T(8,128)(2,1)S(1)}) custom-call(s32[2]{0:T(128)S(1)} %pad_add_fusion.place_ref, bf16[128,8192]{1,0:T(8,128)(2,1)} %text_ref.1, bf16[1,16,4,8192]{3,2,1,0:T(4,128)(2,1)} %extra_ref.1, bf16[512,128]{1,0:T(8,128)(2,1)} %key_ref.1, bf16[512,128]{1,0:T(8,128)(2,1)} %value_ref.1), custom_call_target="tpu_custom_call" | custom-call | tf_op jit(solution)/shard_map/pack/pallas_call | solution.py:112
  3.5 4.2 %all-to-all-start = ((bf16[4,192,2048]{2,1,0:T(8,128)(2,1)}), bf16[4,192,2048]{2,1,0:T(8,128)(2,1)S(1)}, u32[]{:S(2)}, u32[]{:S(2)}) async-start(bf16[4,192,2048]{2,1,0:T(8,128)(2,1)} %get-tuple-element.11), calls=%async_computation | async-start | bytes 6291456 | tf_op jit(solution)/shard_map/all_to_all | solution.py:323
  7.7 0.0 copy-start.1
  7.8 40.5 %all-gather = bf16[1024,128]{1,0:T(8,128)(2,1)S(1)} all-gather(bf16[256,128]{1,0:T(8,128)(2,1)S(1)} %get-tuple-element.12), channel_id=2, replica_groups={{0,64,128,192},{256,320,384,448},{512,576,640,704},{768,832,896,960},{1..., dimensions={0}, use_global_device_ids=true | all-gather | bytes 327680 | tf_op jit(solution)/shard_map/all_gather | solution.py:332
  48.3 0.0 copy-start.2
  48.3 6.7 %all-gather.1 = bf16[8,256,128]{2,1,0:T(8,128)(2,1)S(1)} all-gather(bf16[4,256,128]{2,1,0:T(8,128)(2,1)S(1)} %bitcast.23), channel_id=3, replica_groups={{0,8},{4,12},{16,24},{20,28},{32,40},{36,44},{48,56},{52,60},{1,9},{5,1..., dimensions={0}, use_global_device_ids=true | all-gather | bytes 786432 | tf_op jit(solution)/shard_map/all_gather | solution.py:336
  55.0 0.0 copy-start
  55.0 7.0 %collective-permute-start = (bf16[2,4,256,128]{3,2,1,0:T(8,128)(2,1)S(1)}, bf16[2,4,256,128]{3,2,1,0:T(8,128)(2,1)}, u32[]{:S(2)}, u32[]{:S(2)}) collective-permute-start(bf16[2,4,256,128]{3,2,1,0:T(8,128)(2,1)S(1)} %bitcast.20), channel_id=1, source_target_pairs={{0,4},{1,5},{2,6},{3,7},{4,0},{5,1},{6,2},{7,3},{8,12},{9,13},{10,... | collective-permute-start | bytes 1572872 | tf_op jit(solution)/shard_map/ppermute | solution.py:37
  62.0 0.0 copy-done
  62.0 1.6 %collective-permute-done.other_ref = bf16[2,4,256,128]{3,2,1,0:T(8,128)(2,1)} collective-permute-done((bf16[2,4,256,128]{3,2,1,0:T(8,128)(2,1)S(1)}, bf16[2,4,256,128]{3,2,1,0:T(8,128)(2,1)}, u32[]{:S(2)}, u32[]{:S(2)}) %collective-permute-start) | collective-permute-done | bytes 524320 | tf_op jit(solution)/shard_map/ppermute | solution.py:37
  63.6 0.0 all-to-all-done.rows_ref
  63.6 3.5 %project_extra.1 = f32[4,64,256]{2,1,0:T(8,128)} custom-call(s32[2]{0:T(128)S(1)} %pad_add_fusion.place_ref, bf16[4,192,2048]{2,1,0:T(8,128)(2,1)S(1)} %all-to-all-done.rows_ref, bf16[2,4,256,128]{3,2,1,0:T(8,128)(2,1)} %bitcast.21, bf16[2,4,256,128]{3,2,1,0:T(8,128)(2,1)} %collective-permute-done.other_ref), custom_call_target="tpu_custom_call" | custom-call | tf_op jit(solution)/shard_map/project_extra/pallas_call | solution.py:161
  67.1 6.3 %all-to-all-start.1 = ((f32[4,64,256]{2,1,0:T(8,128)}), f32[4,64,256]{2,1,0:T(8,128)S(1)}, u32[]{:S(2)}, u32[]{:S(2)}) async-start(f32[4,64,256]{2,1,0:T(8,128)} %project_extra.1), calls=%async_computation.1 | async-start | bytes 524288 | tf_op jit(solution)/shard_map/all_to_all | solution.py:323
  73.4 0.0 copy-done.1
  73.4 0.1 copy.12
  73.5 0.1 convert_element_type.18
  73.6 4.1 %all-to-all-done.1.sums_ref = f32[4,64,256]{2,1,0:T(8,128)S(1)} async-done(((f32[4,64,256]{2,1,0:T(8,128)}), f32[4,64,256]{2,1,0:T(8,128)S(1)}, u32[]{:S(2)}, u32[]{:S(2)}) %all-to-all-start.1) | async-done | bytes 262176 | tf_op jit(solution)/shard_map/all_to_all | solution.py:323
  77.7 0.1 broadcast_in_dim.4.marks_ref
  77.8 0.6 settle.1
  78.4 9.9 %all-to-all-start.2 = ((bf16[16,4,384]{2,1,0:T(4,128)(2,1)}), bf16[16,4,384]{2,1,0:T(4,128)(2,1)S(1)}, u32[]{:S(2)}, u32[]{:S(2)}) async-start(bf16[16,4,384]{2,1,0:T(4,128)(2,1)} %settle.1), calls=%async_computation.2 | async-start | bytes 98304 | tf_op jit(solution)/shard_map/all_to_all | solution.py:346
  88.3 0.0 copy-done.2
  88.3 3.5 %project_text.1 = (f32[128,256]{1,0:T(8,128)S(1)}, f32[128,256]{1,0:T(8,128)}, f32[128,256]{1,0:T(8,128)}, f32[128,256]{1,0:T(8,128)}) custom-call(s32[2]{0:T(128)S(1)} %pad_add_fusion.place_ref, bf16[4,192,2048]{2,1,0:T(8,128)(2,1)S(1)} %all-to-all-done.rows_ref, bf16[2,4,256,128]{3,2,1,0:T(8,128)(2,1)} %bitcast.22, ...), custom_call_target="tpu_custom_call" | custom-call | tf_op jit(solution)/shard_map/project_text/pallas_call | solution.py:191
  91.8 3.7 %collective-permute-start.1 = (f32[128,256]{1,0:T(8,128)}, f32[128,256]{1,0:T(8,128)S(1)}, u32[]{:S(2)}, u32[]{:S(2)}) collective-permute-start(f32[128,256]{1,0:T(8,128)} %get-tuple-element.14), channel_id=1, source_target_pairs={{0,256},{1,257},{2,258},{3,259},{4,260},{5,261},{6,262},{7,263},{8... | collective-permute-start | bytes 393224 | tf_op jit(solution)/shard_map/ppermute | solution.py:42
  95.5 1.9 %collective-permute-start.2 = (f32[128,256]{1,0:T(8,128)}, f32[128,256]{1,0:T(8,128)S(1)}, u32[]{:S(2)}, u32[]{:S(2)}) collective-permute-start(f32[128,256]{1,0:T(8,128)} %get-tuple-element.15), channel_id=1, source_target_pairs={{0,512},{1,513},{2,514},{3,515},{4,516},{5,517},{6,518},{7,519},{8... | collective-permute-start | bytes 393224 | tf_op jit(solution)/shard_map/ppermute | solution.py:42
  97.4 2.8 %collective-permute-start.3 = (f32[128,256]{1,0:T(8,128)}, f32[128,256]{1,0:T(8,128)S(1)}, u32[]{:S(2)}, u32[]{:S(2)}) collective-permute-start(f32[128,256]{1,0:T(8,128)} %get-tuple-element.16), channel_id=1, source_target_pairs={{0,768},{1,769},{2,770},{3,771},{4,772},{5,773},{6,774},{7,775},{8... | collective-permute-start | bytes 393224 | tf_op jit(solution)/shard_map/ppermute | solution.py:42
  100.2 0.0 collective-permute-done.1.refs_1_
  100.2 3.3 %collective-permute-done.2.refs_2_ = f32[128,256]{1,0:T(8,128)S(1)} collective-permute-done((f32[128,256]{1,0:T(8,128)}, f32[128,256]{1,0:T(8,128)S(1)}, u32[]{:S(2)}, u32[]{:S(2)}) %collective-permute-start.2) | collective-permute-done | bytes 131104 | tf_op jit(solution)/shard_map/ppermute | solution.py:42
  103.5 3.7 %collective-permute-done.3.refs_3_ = f32[128,256]{1,0:T(8,128)S(1)} collective-permute-done((f32[128,256]{1,0:T(8,128)}, f32[128,256]{1,0:T(8,128)S(1)}, u32[]{:S(2)}, u32[]{:S(2)}) %collective-permute-start.3) | collective-permute-done | bytes 131104 | tf_op jit(solution)/shard_map/ppermute | solution.py:42
  107.1 0.0 all-to-all-done.2.vis_ref
  107.1 0.2 merge.1
  107.3 4.3 %collective-permute-start.4 = (bf16[136,256]{1,0:T(8,128)(2,1)S(1)}, bf16[136,256]{1,0:T(8,128)(2,1)S(1)}, u32[]{:S(2)}, u32[]{:S(2)}) collective-permute-start(bf16[136,256]{1,0:T(8,128)(2,1)S(1)} %merge.1), channel_id=1, source_target_pairs={{0,8},{1,9},{2,10},{3,11},{4,12},{5,13},{6,14},{7,15},{8,16},{9,17... | collective-permute-start | bytes 208904 | tf_op jit(solution)/shard_map/ppermute | solution.py:37
  111.7 4.0 %collective-permute-start.5 = (bf16[136,256]{1,0:T(8,128)(2,1)S(1)}, bf16[136,256]{1,0:T(8,128)(2,1)S(1)}, u32[]{:S(2)}, u32[]{:S(2)}) collective-permute-start(bf16[136,256]{1,0:T(8,128)(2,1)S(1)} %merge.1), channel_id=1, source_target_pairs={{0,16},{1,17},{2,18},{3,19},{4,20},{5,21},{6,22},{7,23},{8,24},{9,... | collective-permute-start | bytes 208904 | tf_op jit(solution)/shard_map/ppermute | solution.py:37
  115.7 2.2 %collective-permute-start.6 = (bf16[136,256]{1,0:T(8,128)(2,1)S(1)}, bf16[136,256]{1,0:T(8,128)(2,1)S(1)}, u32[]{:S(2)}, u32[]{:S(2)}) collective-permute-start(bf16[136,256]{1,0:T(8,128)(2,1)S(1)} %merge.1), channel_id=1, source_target_pairs={{0,24},{1,25},{2,26},{3,27},{4,28},{5,29},{6,30},{7,31},{8,32},{9,... | collective-permute-start | bytes 208904 | tf_op jit(solution)/shard_map/ppermute | solution.py:37
  117.9 1.3 collective-permute-start.7
  119.2 0.0 collective-permute-done.4
  119.3 0.0 collective-permute-done.5
  119.3 3.5 %collective-permute-done.6 = bf16[136,256]{1,0:T(8,128)(2,1)S(1)} collective-permute-done((bf16[136,256]{1,0:T(8,128)(2,1)S(1)}, bf16[136,256]{1,0:T(8,128)(2,1)S(1)}, u32[]{:S(2)}, u32[]{:S(2)}) %collective-permute-start.6) | collective-permute-done | bytes 69664 | tf_op jit(solution)/shard_map/ppermute | solution.py:37
  122.7 6.6 %collective-permute-done.7 = bf16[136,256]{1,0:T(8,128)(2,1)S(1)} collective-permute-done((bf16[136,256]{1,0:T(8,128)(2,1)S(1)}, bf16[136,256]{1,0:T(8,128)(2,1)S(1)}, u32[]{:S(2)}, u32[]{:S(2)}) %collective-permute-start.7) | collective-permute-done | bytes 69664 | tf_op jit(solution)/shard_map/ppermute | solution.py:37
  129.4 2.6 %collective-permute-start.8 = (bf16[5,136,256]{2,1,0:T(8,128)(2,1)S(1)}, bf16[5,136,256]{2,1,0:T(8,128)(2,1)S(1)}, u32[]{:S(2)}, u32[]{:S(2)}) collective-permute-start(bf16[5,136,256]{2,1,0:T(8,128)(2,1)S(1)} %bitcast_dynamic-update-slice_fusion.mine_ref), channel_id=1, source_target_pairs={{0,4},{1,5},{2,6},{3,7},{4,0},{5,1},{6,2},{7,3},{8,12},{9,13},{10,... | collective-permute-start | bytes 1044488 | tf_op jit(solution)/shard_map/ppermute | solution.py:37
  132.0 0.1 copy.13.my_docs_ref
  132.1 1.1 collective-permute-done.8.other_ref
  133.3 6.0 %attend.1 = bf16[128,1024]{1,0:T(8,128)(2,1)} custom-call(s32[2]{0:T(128)S(1)} %pad_add_fusion.place_ref, bf16[128,1024]{1,0:T(8,128)(2,1)} %q_ref.1, bf16[5,136,256]{2,1,0:T(8,128)(2,1)S(1)} %bitcast_dynamic-update-slice_fusion.mine_ref, bf16[5,136,256]{2,1,0:T(8,128)(2,1)S(1)} %collective-permute-done.8.other_ref, f32[128,1]{1,0:T(8,128)S(1)} %copy.13.my_docs_ref), custom_call_target="tpu_custom_call" | custom-call | tf_op jit(solution)/shard_map/attend/pallas_call | solution.py:298
  (9 shorter events, 0.0 us)
Async XLA Ops:
  3.5 60.1 %all-to-all-start = ((bf16[4,192,2048]{2,1,0:T(8,128)(2,1)}), bf16[4,192,2048]{2,1,0:T(8,128)(2,1)S(1)}, u32[]{:S(2)}, u32[]{:S(2)}) async-start(bf16[4,192,2048]{2,1,0:T(8,128)(2,1)} %get-tuple-element.11), calls=%async_computation | async-start | bytes 6291456 | tf_op jit(solution)/shard_map/all_to_all | solution.py:323
  7.7 65.6 %copy-start.1 = (s32[1,16,4]{1,2,0:T(4,128)S(1)}, s32[1,16,4]{1,2,0:T(4,128)}, u32[]{:S(2)}) copy-start(s32[1,16,4]{1,2,0:T(4,128)} %param.10) | copy-start | bytes 772
  48.3 40.0 %copy-start.2 = (s32[1,128]{1,0:T(1,128)S(1)}, s32[1,128]{1,0:T(1,128)}, u32[]{:S(2)}) copy-start(s32[1,128]{1,0:T(1,128)} %param.11) | copy-start | bytes 1540
  55.0 7.0 %copy-start = (bf16[8,256,128]{2,1,0:T(8,128)(2,1)}, bf16[8,256,128]{2,1,0:T(8,128)(2,1)S(1)}, u32[]{:S(2)}) copy-start(bf16[8,256,128]{2,1,0:T(8,128)(2,1)S(1)} %all-gather.1) | copy-start | bytes 1572868
  55.0 8.7 %collective-permute-start = (bf16[2,4,256,128]{3,2,1,0:T(8,128)(2,1)S(1)}, bf16[2,4,256,128]{3,2,1,0:T(8,128)(2,1)}, u32[]{:S(2)}, u32[]{:S(2)}) collective-permute-start(bf16[2,4,256,128]{3,2,1,0:T(8,128)(2,1)S(1)} %bitcast.20), channel_id=1, source_target_pairs={{0,4},{1,5},{2,6},{3,7},{4,0},{5,1},{6,2},{7,3},{8,12},{9,13},{10,... | collective-permute-start | bytes 1572872 | tf_op jit(solution)/shard_map/ppermute | solution.py:37
  67.1 10.6 %all-to-all-start.1 = ((f32[4,64,256]{2,1,0:T(8,128)}), f32[4,64,256]{2,1,0:T(8,128)S(1)}, u32[]{:S(2)}, u32[]{:S(2)}) async-start(f32[4,64,256]{2,1,0:T(8,128)} %project_extra.1), calls=%async_computation.1 | async-start | bytes 524288 | tf_op jit(solution)/shard_map/all_to_all | solution.py:323
  78.4 28.7 %all-to-all-start.2 = ((bf16[16,4,384]{2,1,0:T(4,128)(2,1)}), bf16[16,4,384]{2,1,0:T(4,128)(2,1)S(1)}, u32[]{:S(2)}, u32[]{:S(2)}) async-start(bf16[16,4,384]{2,1,0:T(4,128)(2,1)} %settle.1), calls=%async_computation.2 | async-start | bytes 98304 | tf_op jit(solution)/shard_map/all_to_all | solution.py:346
  91.8 8.4 %collective-permute-start.1 = (f32[128,256]{1,0:T(8,128)}, f32[128,256]{1,0:T(8,128)S(1)}, u32[]{:S(2)}, u32[]{:S(2)}) collective-permute-start(f32[128,256]{1,0:T(8,128)} %get-tuple-element.14), channel_id=1, source_target_pairs={{0,256},{1,257},{2,258},{3,259},{4,260},{5,261},{6,262},{7,263},{8... | collective-permute-start | bytes 393224 | tf_op jit(solution)/shard_map/ppermute | solution.py:42
  95.5 8.0 %collective-permute-start.2 = (f32[128,256]{1,0:T(8,128)}, f32[128,256]{1,0:T(8,128)S(1)}, u32[]{:S(2)}, u32[]{:S(2)}) collective-permute-start(f32[128,256]{1,0:T(8,128)} %get-tuple-element.15), channel_id=1, source_target_pairs={{0,512},{1,513},{2,514},{3,515},{4,516},{5,517},{6,518},{7,519},{8... | collective-permute-start | bytes 393224 | tf_op jit(solution)/shard_map/ppermute | solution.py:42
  97.4 9.7 %collective-permute-start.3 = (f32[128,256]{1,0:T(8,128)}, f32[128,256]{1,0:T(8,128)S(1)}, u32[]{:S(2)}, u32[]{:S(2)}) collective-permute-start(f32[128,256]{1,0:T(8,128)} %get-tuple-element.16), channel_id=1, source_target_pairs={{0,768},{1,769},{2,770},{3,771},{4,772},{5,773},{6,774},{7,775},{8... | collective-permute-start | bytes 393224 | tf_op jit(solution)/shard_map/ppermute | solution.py:42
  107.3 11.9 %collective-permute-start.4 = (bf16[136,256]{1,0:T(8,128)(2,1)S(1)}, bf16[136,256]{1,0:T(8,128)(2,1)S(1)}, u32[]{:S(2)}, u32[]{:S(2)}) collective-permute-start(bf16[136,256]{1,0:T(8,128)(2,1)S(1)} %merge.1), channel_id=1, source_target_pairs={{0,8},{1,9},{2,10},{3,11},{4,12},{5,13},{6,14},{7,15},{8,16},{9,17... | collective-permute-start | bytes 208904 | tf_op jit(solution)/shard_map/ppermute | solution.py:37
  111.7 7.6 %collective-permute-start.5 = (bf16[136,256]{1,0:T(8,128)(2,1)S(1)}, bf16[136,256]{1,0:T(8,128)(2,1)S(1)}, u32[]{:S(2)}, u32[]{:S(2)}) collective-permute-start(bf16[136,256]{1,0:T(8,128)(2,1)S(1)} %merge.1), channel_id=1, source_target_pairs={{0,16},{1,17},{2,18},{3,19},{4,20},{5,21},{6,22},{7,23},{8,24},{9,... | collective-permute-start | bytes 208904 | tf_op jit(solution)/shard_map/ppermute | solution.py:37
  115.7 7.0 %collective-permute-start.6 = (bf16[136,256]{1,0:T(8,128)(2,1)S(1)}, bf16[136,256]{1,0:T(8,128)(2,1)S(1)}, u32[]{:S(2)}, u32[]{:S(2)}) collective-permute-start(bf16[136,256]{1,0:T(8,128)(2,1)S(1)} %merge.1), channel_id=1, source_target_pairs={{0,24},{1,25},{2,26},{3,27},{4,28},{5,29},{6,30},{7,31},{8,32},{9,... | collective-permute-start | bytes 208904 | tf_op jit(solution)/shard_map/ppermute | solution.py:37
  117.9 11.5 %collective-permute-start.7 = (bf16[136,256]{1,0:T(8,128)(2,1)S(1)}, bf16[136,256]{1,0:T(8,128)(2,1)S(1)}, u32[]{:S(2)}, u32[]{:S(2)}) collective-permute-start(bf16[136,256]{1,0:T(8,128)(2,1)S(1)} %merge.1), channel_id=1, source_target_pairs={{0,32},{1,33},{2,34},{3,35},{4,36},{5,37},{6,38},{7,39},{8,40},{9,... | collective-permute-start | bytes 208904 | tf_op jit(solution)/shard_map/ppermute | solution.py:37
  129.4 3.9 %collective-permute-start.8 = (bf16[5,136,256]{2,1,0:T(8,128)(2,1)S(1)}, bf16[5,136,256]{2,1,0:T(8,128)(2,1)S(1)}, u32[]{:S(2)}, u32[]{:S(2)}) collective-permute-start(bf16[5,136,256]{2,1,0:T(8,128)(2,1)S(1)} %bitcast_dynamic-update-slice_fusion.mine_ref), channel_id=1, source_target_pairs={{0,4},{1,5},{2,6},{3,7},{4,0},{5,1},{6,2},{7,3},{8,12},{9,13},{10,... | collective-permute-start | bytes 1044488 | tf_op jit(solution)/shard_map/ppermute | solution.py:37

commit v6 on v5

--- a/solution.py
+++ b/solution.py
@@ -20,9 +20,7 @@
 OVER_X = [[x * NZ + z for x in range(NX)] for z in range(NZ)]
 OVER_Z = [[x * NZ + z for z in range(NZ)] for x in range(NX)]
 NEAR = 2
-OVER_NEAR = [
-    [(first + i) * 2 + core for i in range(NEAR)] for first in range(0, NLO, NEAR) for core in range(2)
-]
+OVER_NEAR = [[first + i for i in range(2 * NEAR)] for first in range(0, NS, 2 * NEAR)]
 
 
 def seq_permute(array, move):
@@ -133,51 +131,57 @@
     )(place, *map(in_hbm, (hidden, vis_rows, w_key, w_value)))
 
 
-def order(place_ref, mine_ref, other_ref, weights_ref):
-    steps, sources, part, cols = mine_ref.shape
-    core = lax.rem(place_ref[0], 2)
-    for side, ref in enumerate((mine_ref, other_ref)):
-        at = pl.ds(pl.multiple_of(jnp.where(core == side, 0, cols), cols), cols)
-        for k in range(steps):
-            for z in range(sources):
-                row = (z * steps + k) * part
-                weights_ref[row : row + part, at] = ref[k, z]
-
-
-def project_extra(place_ref, rows_ref, mine_ref, other_ref, vis_ref, weights_ref):
+def project_extra(
+    place_ref, rows_ref, key_ref, value_ref, far_ref, vis_ref, out_ref, weights_ref, out_sem
+):
+    members, sources, part, cols = far_ref.shape
     tokens = rows_ref.shape[1] - NS * CAP
-    order(place_ref, mine_ref, other_ref, weights_ref)
+    z = place_ref[2]
+    shard = NEAR * part
+    own = pl.ds(pl.multiple_of(z * shard, shard), shard)
+    weights_ref[own, :cols] = key_ref[...]
+    weights_ref[own, cols:] = value_ref[...]
+    for i in range(sources):
+        first = lax.rem(z + 1 + i, NZ) * shard
+        for m in range(members):
+            chip, core = divmod(m, 2)
+            at = pl.ds(pl.multiple_of(first + chip * part, part), part)
+            weights_ref[at, core * cols : (core + 1) * cols] = far_ref[m, i]
+    copy = pltpu.make_async_copy(weights_ref, out_ref, out_sem)
+    copy.start()
     weights = weights_ref[...]
     for block in range(NX):
         vis_ref[block] = jnp.dot(
             rows_ref[block, tokens:, :], weights, preferred_element_type=jnp.float32
         )
-
-
-def projected_extra(place, rows, mine, other):
+    copy.wait()
+
+
+def projected_extra(place, rows, w_key, w_value, far):
     blocks, _, part = rows.shape
-    cols = 2 * mine.shape[-1]
+    cols = 2 * far.shape[-1]
     vis = pltpu.HBM((blocks, NS * CAP, cols), jnp.float32)
     return pl.pallas_call(
         project_extra,
         grid_spec=pltpu.PrefetchScalarGridSpec(
             num_scalar_prefetch=1,
             grid=(1,),
-            in_specs=[IN_VMEM, whole(mine.shape), whole(other.shape)],
-            out_specs=pl.BlockSpec(vis.shape, lambda i, _: (0, 0, 0)),
-            scratch_shapes=[pltpu.VMEM((part, cols), jnp.bfloat16)],
-        ),
-        out_shape=vis,
+            in_specs=[IN_VMEM, whole(w_key.shape), whole(w_value.shape), IN_VMEM],
+            out_specs=[
+                pl.BlockSpec(vis.shape, lambda i, _: (0, 0, 0)),
+                pl.BlockSpec(memory_space=pl.ANY),
+            ],
+            scratch_shapes=[pltpu.VMEM((part, cols), jnp.bfloat16), pltpu.SemaphoreType.DMA],
+        ),
+        out_shape=[vis, pltpu.HBM((part, cols), jnp.bfloat16)],
         compiler_params=pltpu.CompilerParams(vmem_limit_bytes=16 * MIB),
         name="project_extra",
-    )(place, in_vmem(rows), in_hbm(mine), in_hbm(other))
-
-
-def project_text(place_ref, rows_ref, mine_ref, other_ref, own_ref, *refs):
-    *text_refs, weights_ref = refs
+    )(place, in_vmem(rows), in_hbm(w_key), in_hbm(w_value), far)
+
+
+def project_text(place_ref, rows_ref, weights_ref, own_ref, *text_refs):
     tokens = own_ref.shape[0]
     x = place_ref[1]
-    order(place_ref, mine_ref, other_ref, weights_ref)
     weights = weights_ref[...]
     for d, ref in enumerate((own_ref, *text_refs)):
         ref[...] = jnp.dot(
@@ -185,23 +189,22 @@
         )
 
 
-def projected_text(place, rows, mine, other):
-    blocks, count, part = rows.shape
-    shape = (count - NS * CAP, 2 * mine.shape[-1])
+def projected_text(place, rows, weights):
+    blocks, count, _ = rows.shape
+    shape = (count - NS * CAP, weights.shape[1])
     return pl.pallas_call(
         project_text,
         grid_spec=pltpu.PrefetchScalarGridSpec(
             num_scalar_prefetch=1,
             grid=(1,),
-            in_specs=[IN_VMEM, whole(mine.shape), whole(other.shape)],
+            in_specs=[IN_VMEM, whole(weights.shape)],
             out_specs=[IN_VMEM] + [pl.BlockSpec(shape, lambda i, _: (0, 0))] * (blocks - 1),
-            scratch_shapes=[pltpu.VMEM((part, shape[1]), jnp.bfloat16)],
         ),
         out_shape=[pltpu.VMEM(shape, jnp.float32)]
         + [pltpu.HBM(shape, jnp.float32)] * (blocks - 1),
         compiler_params=pltpu.CompilerParams(vmem_limit_bytes=16 * MIB),
         name="project_text",
-    )(place, in_vmem(rows), in_hbm(mine), in_hbm(other))
+    )(place, in_vmem(rows), in_hbm(weights))
 
 
 def settle(sums_ref, marks_ref, out_ref):
@@ -254,12 +257,15 @@
     )(in_vmem(vis), docs, *map(in_vmem, text))
 
 
-def attend(place_ref, q_ref, mine_ref, other_ref, my_docs_ref, out_ref, bias_ref, keys_ref, values_ref):
-    tokens = q_ref.shape[0]
+def attend(place_ref, q_hbm, mine_ref, other_ref, my_docs_ref, out_ref, *scratch):
+    bias_ref, keys_ref, values_ref, q_ref, q_sem = scratch
+    tokens = q_hbm.shape[0]
     blocks = mine_ref.shape[0]
 
     @pl.when(pl.program_id(0) == 0)
     def _():
+        copy = pltpu.make_async_copy(q_hbm, q_ref, q_sem)
+        copy.start()
         s = place_ref[0]
         core, chip = lax.rem(s, 2), s // 2
         my_docs = jnp.broadcast_to(my_docs_ref[...], (tokens, tokens))
@@ -275,12 +281,14 @@
                 bias_ref[:, at : at + tokens] = jnp.where(allowed, 0.0, -1e30)
                 keys_ref[at : at + tokens, :] = ref[d, :tokens, :HEAD]
                 values_ref[at : at + tokens, :] = ref[d, :tokens, HEAD:]
+        copy.wait()
 
     scale = 1.0 / jnp.sqrt(jnp.float32(HEAD))
+    first = pl.multiple_of(pl.program_id(0) * HEADS_STEP * HEAD, HEAD)
     for h in range(HEADS_STEP):
         head = slice(h * HEAD, (h + 1) * HEAD)
         scores = lax.dot_general(
-            q_ref[:, head], keys_ref[...], (((1,), (1,)), ((), ())), preferred_element_type=jnp.float32
+            q_ref[:, pl.ds(first + h * HEAD, HEAD)], keys_ref[...], (((1,), (1,)), ((), ())), preferred_element_type=jnp.float32
         )
         scores = scores * scale + bias_ref[...]
         top = jnp.max(scores, axis=1, keepdims=True)
@@ -301,7 +309,7 @@
             num_scalar_prefetch=1,
             grid=(QPK // HEADS_STEP,),
             in_specs=[
-                pl.BlockSpec((tokens, HEADS_STEP * HEAD), lambda h, *_: (0, h)),
+                pl.BlockSpec(memory_space=pl.ANY),
                 IN_VMEM,
                 IN_VMEM,
                 IN_VMEM,
@@ -311,6 +319,8 @@
                 pltpu.VMEM((tokens, span), jnp.float32),
                 pltpu.VMEM((span, HEAD), jnp.bfloat16),
                 pltpu.VMEM((span, HEAD), jnp.bfloat16),
+                pltpu.VMEM(queries.shape, queries.dtype),
+                pltpu.SemaphoreType.DMA,
             ],
         ),
         out_shape=jax.ShapeDtypeStruct(queries.shape, jnp.bfloat16),
@@ -326,19 +336,21 @@
 def program(hidden, queries, vis_rows, vis_slot, doc_ids, w_key, w_value):
     tokens = hidden.shape[0]
     cols = 2 * w_key.shape[1]
-    where = jnp.stack([lax.axis_index("seq"), lax.axis_index("grp") // NZ])
+    grp = lax.axis_index("grp")
+    where = jnp.stack([lax.axis_index("seq"), grp // NZ, grp % NZ])
     rows, piece = packed(where, hidden, vis_rows, w_key, w_value)
 
     got = lax.all_gather(piece, "grp", axis=0, axis_index_groups=OVER_Z)
 
     rows = exchange_x(rows)
 
-    mine = lax.all_gather(got, "seq", axis=0, axis_index_groups=OVER_NEAR)
-    other = seq_permute(mine, sibling)
-
-    vis = projected_extra(where, rows, mine, other)
+    z = lax.axis_index("grp") % NZ
+    far = jnp.stack([lax.dynamic_index_in_dim(got, (z + 1 + i) % NZ, 0, False) for i in range(NZ - 1)])
+    far = lax.all_gather(far, "seq", axis=0, axis_index_groups=OVER_NEAR)
+
+    vis, weights = projected_extra(where, rows, w_key, w_value, far)
     vis = exchange_x(vis)
-    text = list(projected_text(where, rows, mine, other))
+    text = list(projected_text(where, rows, weights))
     for d in (2, 1, 3):
         text[d] = x_permute(text[d], d)
     marks = jnp.broadcast_to(vis_slot.reshape(NS * CAP, 1), (NS * CAP, tokens)).astype(jnp.float32)

time: 140 us -> 137 us (0.979)
  starting transfers between devices: 50.2 us -> 41.2 us
  blocking collectives: 47.2 us -> 54 us
    ppermute x6 -> x5, starting transfers between devices: 21.4 us -> 14.4 us  [seq_permute(): return lax.ppermute(array, AXES, pairs)]
    all_gather x1, blocking collectives: 6.69 us -> 13.7 us  [program(): far = lax.all_gather(far, 'seq', axis=0, axis_index_groups=OVER_NEAR)]
    ppermute x6 -> x5, waiting for transfers between devices: 12.9 us -> 11.3 us  [seq_permute(): return lax.ppermute(array, AXES, pairs)]
    all_to_all x2, starting transfers between devices: 10.5 us -> 9 us  [exchange_x(): lax.all_to_all(array, 'grp', 0, 0, axis_index_groups=OVER_X, tiled=True)]
  transfers between devices with their start and end apart: 12 -> 11, of which waited for: 7 -> 6; matrix products, arithmetic and copies ran while one was open for 0% -> 0% of each run, Pallas kernels for 2% -> 2%
where the time goes in v6:
time: 137 us
  blocking collectives  54 us (39%)
  starting transfers between devices  41.2 us (30%)
  waiting for transfers between devices  22.8 us (17%)
  Pallas kernels  16.7 us (12%)
  local copies, waits for them, and re-layouts  1.56 us (1%)
    all_gather x1, blocking collectives, program(): got = lax.all_gather(piece, 'grp', axis=0, axis_index_groups=OVER_Z)  40.4 us
    ppermute x5, starting transfers between devices, seq_permute(): return lax.ppermute(array, AXES, pairs)  14.4 us
    all_gather x1, blocking collectives, program(): far = lax.all_gather(far, 'seq', axis=0, axis_index_groups=OVER_NEAR)  13.7 us
    ppermute x5, waiting for transfers between devices, seq_permute(): return lax.ppermute(array, AXES, pairs)  11.3 us
    all_to_all x1, starting transfers between devices, program(): vis = lax.all_to_all(vis, 'seq', 0, 0, tiled=True)  9.43 us
    all_to_all x2, starting transfers between devices, exchange_x(): lax.all_to_all(array, 'grp', 0, 0, axis_index_groups=OVER_X, tiled=True)  9 us
    ppermute x3, starting transfers between devices, x_permute(): lax.ppermute(array, AXES, [(i, (i + d * step) % size) for i in range(size)])  8.36 us
    ppermute x3, waiting for transfers between devices, x_permute(): lax.ppermute(array, AXES, [(i, (i + d * step) % size) for i in range(size)])  6.94 us
  transfers between devices with their start and end apart: 11, of which 6 were waited for; matrix products, arithmetic and copies ran while one was open for 0% of the time, Pallas kernels for 2%

profile of v6, /device:TPU:103, one launch (start us, length us, event | category | flops | bytes accessed | tf_op | source)
XLA Modules:
  0.0 136.7 jit_solution(14564704225362117196)
XLA Ops:
  0.0 0.1 pad_add_fusion.place_ref
  0.1 3.4 %pack.1 = (bf16[4,192,2048]{2,1,0:T(8,128)(2,1)}, bf16[256,128]{1,0:T(8,128)(2,1)S(1)}) custom-call(s32[3]{0:T(128)S(1)} %pad_add_fusion.place_ref, bf16[128,8192]{1,0:T(8,128)(2,1)} %text_ref.1, bf16[1,16,4,8192]{3,2,1,0:T(4,128)(2,1)} %extra_ref.1, bf16[512,128]{1,0:T(8,128)(2,1)} %key_ref.3, bf16[512,128]{1,0:T(8,128)(2,1)} %value_ref.3), custom_call_target="tpu_custom_call" | custom-call | tf_op jit(solution)/shard_map/pack/pallas_call | solution.py:110
  3.5 4.2 %all-to-all-start = ((bf16[4,192,2048]{2,1,0:T(8,128)(2,1)}), bf16[4,192,2048]{2,1,0:T(8,128)(2,1)S(1)}, u32[]{:S(2)}, u32[]{:S(2)}) async-start(bf16[4,192,2048]{2,1,0:T(8,128)(2,1)} %get-tuple-element.13), calls=%async_computation | async-start | bytes 6291456 | tf_op jit(solution)/shard_map/all_to_all | solution.py:333
  7.7 40.4 %all-gather = bf16[1024,128]{1,0:T(8,128)(2,1)S(1)} all-gather(bf16[256,128]{1,0:T(8,128)(2,1)S(1)} %get-tuple-element.14), channel_id=2, replica_groups={{0,64,128,192},{256,320,384,448},{512,576,640,704},{768,832,896,960},{1..., dimensions={0}, use_global_device_ids=true | all-gather | bytes 327680 | tf_op jit(solution)/shard_map/all_gather | solution.py:343
  48.1 0.0 copy-start.1
  48.2 0.0 copy-start.2
  48.2 13.7 %all-gather.1 = bf16[12,256,128]{2,1,0:T(8,128)(2,1)} all-gather(bf16[3,256,128]{2,1,0:T(8,128)(2,1)S(1)} %pad_maximum_fusion), channel_id=3, replica_groups={{0,4,8,12},{16,20,24,28},{32,36,40,44},{48,52,56,60},{1,5,9,13},{17,21,..., dimensions={0}, use_global_device_ids=true | all-gather | bytes 983040 | tf_op jit(solution)/shard_map/all_gather | solution.py:349
  61.9 0.0 all-to-all-done.rows_ref
  61.9 0.0 copy-start
  61.9 1.1 copy-done
  63.0 3.4 %project_extra.1 = (f32[4,64,256]{2,1,0:T(8,128)}, bf16[2048,256]{1,0:T(8,128)(2,1)}) custom-call(s32[3]{0:T(128)S(1)} %pad_add_fusion.place_ref, bf16[4,192,2048]{2,1,0:T(8,128)(2,1)S(1)} %all-to-all-done.rows_ref, bf16[512,128]{1,0:T(8,128)(2,1)} %key_ref.3, bf16[512,128]{1,0:T(8,128)(2,1)} %value_ref.3, bf16[4,3,256,128]{3,2,1,0:T(8,128)(2,1)S(1)} %bitcast.21), custom_call_target="tpu_custom_call" | custom-call | tf_op jit(solution)/shard_map/project_extra/pallas_call | solution.py:164
  66.5 4.8 %all-to-all-start.1 = ((f32[4,64,256]{2,1,0:T(8,128)}), f32[4,64,256]{2,1,0:T(8,128)S(1)}, u32[]{:S(2)}, u32[]{:S(2)}) async-start(f32[4,64,256]{2,1,0:T(8,128)} %get-tuple-element.15), calls=%async_computation.1 | async-start | bytes 524288 | tf_op jit(solution)/shard_map/all_to_all | solution.py:333
  71.2 0.0 copy-done.1
  71.2 0.1 copy.12
  71.3 0.1 convert_element_type.18
  71.4 4.6 %all-to-all-done.1.sums_ref = f32[4,64,256]{2,1,0:T(8,128)S(1)} async-done(((f32[4,64,256]{2,1,0:T(8,128)}), f32[4,64,256]{2,1,0:T(8,128)S(1)}, u32[]{:S(2)}, u32[]{:S(2)}) %all-to-all-start.1) | async-done | bytes 262176 | tf_op jit(solution)/shard_map/all_to_all | solution.py:333
  76.1 0.1 broadcast_in_dim.4.marks_ref
  76.1 0.6 settle.1
  76.8 9.4 %all-to-all-start.2 = ((bf16[16,4,384]{2,1,0:T(4,128)(2,1)}), bf16[16,4,384]{2,1,0:T(4,128)(2,1)S(1)}, u32[]{:S(2)}, u32[]{:S(2)}) async-start(bf16[16,4,384]{2,1,0:T(4,128)(2,1)} %settle.1), calls=%async_computation.2 | async-start | bytes 98304 | tf_op jit(solution)/shard_map/all_to_all | solution.py:358
  86.2 0.0 copy-done.2
  86.2 3.2 %project_text.1 = (f32[128,256]{1,0:T(8,128)S(1)}, f32[128,256]{1,0:T(8,128)}, f32[128,256]{1,0:T(8,128)}, f32[128,256]{1,0:T(8,128)}) custom-call(s32[3]{0:T(128)S(1)} %pad_add_fusion.place_ref, bf16[4,192,2048]{2,1,0:T(8,128)(2,1)S(1)} %all-to-all-done.rows_ref, bf16[2048,256]{1,0:T(8,128)(2,1)} %get-tuple-element.16.weights_ref), custom_call_target="tpu_custom_call" | custom-call | tf_op jit(solution)/shard_map/project_text/pallas_call | solution.py:195
  89.4 3.7 %collective-permute-start = (f32[128,256]{1,0:T(8,128)}, f32[128,256]{1,0:T(8,128)S(1)}, u32[]{:S(2)}, u32[]{:S(2)}) collective-permute-start(f32[128,256]{1,0:T(8,128)} %get-tuple-element.18), channel_id=1, source_target_pairs={{0,256},{1,257},{2,258},{3,259},{4,260},{5,261},{6,262},{7,263},{8... | collective-permute-start | bytes 393224 | tf_op jit(solution)/shard_map/ppermute | solution.py:40
  93.1 1.9 %collective-permute-start.1 = (f32[128,256]{1,0:T(8,128)}, f32[128,256]{1,0:T(8,128)S(1)}, u32[]{:S(2)}, u32[]{:S(2)}) collective-permute-start(f32[128,256]{1,0:T(8,128)} %get-tuple-element.19), channel_id=1, source_target_pairs={{0,512},{1,513},{2,514},{3,515},{4,516},{5,517},{6,518},{7,519},{8... | collective-permute-start | bytes 393224 | tf_op jit(solution)/shard_map/ppermute | solution.py:40
  95.0 2.8 %collective-permute-start.2 = (f32[128,256]{1,0:T(8,128)}, f32[128,256]{1,0:T(8,128)S(1)}, u32[]{:S(2)}, u32[]{:S(2)}) collective-permute-start(f32[128,256]{1,0:T(8,128)} %get-tuple-element.20), channel_id=1, source_target_pairs={{0,768},{1,769},{2,770},{3,771},{4,772},{5,773},{6,774},{7,775},{8... | collective-permute-start | bytes 393224 | tf_op jit(solution)/shard_map/ppermute | solution.py:40
  97.8 0.0 collective-permute-done.refs_1_
  97.8 3.3 %collective-permute-done.1.refs_2_ = f32[128,256]{1,0:T(8,128)S(1)} collective-permute-done((f32[128,256]{1,0:T(8,128)}, f32[128,256]{1,0:T(8,128)S(1)}, u32[]{:S(2)}, u32[]{:S(2)}) %collective-permute-start.1) | collective-permute-done | bytes 131104 | tf_op jit(solution)/shard_map/ppermute | solution.py:40
  101.1 3.7 %collective-permute-done.2.refs_3_ = f32[128,256]{1,0:T(8,128)S(1)} collective-permute-done((f32[128,256]{1,0:T(8,128)}, f32[128,256]{1,0:T(8,128)S(1)}, u32[]{:S(2)}, u32[]{:S(2)}) %collective-permute-start.2) | collective-permute-done | bytes 131104 | tf_op jit(solution)/shard_map/ppermute | solution.py:40
  104.7 0.0 all-to-all-done.2.vis_ref
  104.7 0.2 merge.1
  105.0 4.3 %collective-permute-start.3 = (bf16[136,256]{1,0:T(8,128)(2,1)S(1)}, bf16[136,256]{1,0:T(8,128)(2,1)S(1)}, u32[]{:S(2)}, u32[]{:S(2)}) collective-permute-start(bf16[136,256]{1,0:T(8,128)(2,1)S(1)} %merge.1), channel_id=1, source_target_pairs={{0,8},{1,9},{2,10},{3,11},{4,12},{5,13},{6,14},{7,15},{8,16},{9,17... | collective-permute-start | bytes 208904 | tf_op jit(solution)/shard_map/ppermute | solution.py:35
  109.3 4.0 %collective-permute-start.4 = (bf16[136,256]{1,0:T(8,128)(2,1)S(1)}, bf16[136,256]{1,0:T(8,128)(2,1)S(1)}, u32[]{:S(2)}, u32[]{:S(2)}) collective-permute-start(bf16[136,256]{1,0:T(8,128)(2,1)S(1)} %merge.1), channel_id=1, source_target_pairs={{0,16},{1,17},{2,18},{3,19},{4,20},{5,21},{6,22},{7,23},{8,24},{9,... | collective-permute-start | bytes 208904 | tf_op jit(solution)/shard_map/ppermute | solution.py:35
  113.3 2.2 %collective-permute-start.5 = (bf16[136,256]{1,0:T(8,128)(2,1)S(1)}, bf16[136,256]{1,0:T(8,128)(2,1)S(1)}, u32[]{:S(2)}, u32[]{:S(2)}) collective-permute-start(bf16[136,256]{1,0:T(8,128)(2,1)S(1)} %merge.1), channel_id=1, source_target_pairs={{0,24},{1,25},{2,26},{3,27},{4,28},{5,29},{6,30},{7,31},{8,32},{9,... | collective-permute-start | bytes 208904 | tf_op jit(solution)/shard_map/ppermute | solution.py:35
  115.5 1.3 collective-permute-start.6
  116.9 0.0 collective-permute-done.3
  116.9 0.0 collective-permute-done.4
  116.9 3.5 %collective-permute-done.5 = bf16[136,256]{1,0:T(8,128)(2,1)S(1)} collective-permute-done((bf16[136,256]{1,0:T(8,128)(2,1)S(1)}, bf16[136,256]{1,0:T(8,128)(2,1)S(1)}, u32[]{:S(2)}, u32[]{:S(2)}) %collective-permute-start.5) | collective-permute-done | bytes 69664 | tf_op jit(solution)/shard_map/ppermute | solution.py:35
  120.4 6.6 %collective-permute-done.6 = bf16[136,256]{1,0:T(8,128)(2,1)S(1)} collective-permute-done((bf16[136,256]{1,0:T(8,128)(2,1)S(1)}, bf16[136,256]{1,0:T(8,128)(2,1)S(1)}, u32[]{:S(2)}, u32[]{:S(2)}) %collective-permute-start.6) | collective-permute-done | bytes 69664 | tf_op jit(solution)/shard_map/ppermute | solution.py:35
  127.0 2.6 %collective-permute-start.7 = (bf16[5,136,256]{2,1,0:T(8,128)(2,1)S(1)}, bf16[5,136,256]{2,1,0:T(8,128)(2,1)S(1)}, u32[]{:S(2)}, u32[]{:S(2)}) collective-permute-start(bf16[5,136,256]{2,1,0:T(8,128)(2,1)S(1)} %bitcast_dynamic-update-slice_fusion.mine_ref), channel_id=1, source_target_pairs={{0,4},{1,5},{2,6},{3,7},{4,0},{5,1},{6,2},{7,3},{8,12},{9,13},{10,... | collective-permute-start | bytes 1044488 | tf_op jit(solution)/shard_map/ppermute | solution.py:35
  129.6 0.1 copy.13.my_docs_ref
  129.7 1.1 collective-permute-done.7.other_ref
  130.9 5.8 %attend.1 = bf16[128,1024]{1,0:T(8,128)(2,1)} custom-call(s32[3]{0:T(128)S(1)} %pad_add_fusion.place_ref, bf16[128,1024]{1,0:T(8,128)(2,1)} %q_hbm.1, bf16[5,136,256]{2,1,0:T(8,128)(2,1)S(1)} %bitcast_dynamic-update-slice_fusion.mine_ref, bf16[5,136,256]{2,1,0:T(8,128)(2,1)S(1)} %collective-permute-done.7.other_ref, f32[128,1]{1,0:T(8,128)S(1)} %copy.13.my_docs_ref), custom_call_target="tpu_custom_call" | custom-call | tf_op jit(solution)/shard_map/attend/pallas_call | solution.py:306
  (11 shorter events, 0.1 us)
Async XLA Ops:
  3.5 58.3 %all-to-all-start = ((bf16[4,192,2048]{2,1,0:T(8,128)(2,1)}), bf16[4,192,2048]{2,1,0:T(8,128)(2,1)S(1)}, u32[]{:S(2)}, u32[]{:S(2)}) async-start(bf16[4,192,2048]{2,1,0:T(8,128)(2,1)} %get-tuple-element.13), calls=%async_computation | async-start | bytes 6291456 | tf_op jit(solution)/shard_map/all_to_all | solution.py:333
  48.1 23.1 %copy-start.1 = (s32[1,16,4]{1,2,0:T(4,128)S(1)}, s32[1,16,4]{1,2,0:T(4,128)}, u32[]{:S(2)}) copy-start(s32[1,16,4]{1,2,0:T(4,128)} %param.10) | copy-start | bytes 772
  48.2 38.0 %copy-start.2 = (s32[1,128]{1,0:T(1,128)S(1)}, s32[1,128]{1,0:T(1,128)}, u32[]{:S(2)}) copy-start(s32[1,128]{1,0:T(1,128)} %param.11) | copy-start | bytes 1540
  61.9 1.1 copy-start
  66.5 9.6 %all-to-all-start.1 = ((f32[4,64,256]{2,1,0:T(8,128)}), f32[4,64,256]{2,1,0:T(8,128)S(1)}, u32[]{:S(2)}, u32[]{:S(2)}) async-start(f32[4,64,256]{2,1,0:T(8,128)} %get-tuple-element.15), calls=%async_computation.1 | async-start | bytes 524288 | tf_op jit(solution)/shard_map/all_to_all | solution.py:333
  76.8 28.0 %all-to-all-start.2 = ((bf16[16,4,384]{2,1,0:T(4,128)(2,1)}), bf16[16,4,384]{2,1,0:T(4,128)(2,1)S(1)}, u32[]{:S(2)}, u32[]{:S(2)}) async-start(bf16[16,4,384]{2,1,0:T(4,128)(2,1)} %settle.1), calls=%async_computation.2 | async-start | bytes 98304 | tf_op jit(solution)/shard_map/all_to_all | solution.py:358
  89.4 8.4 %collective-permute-start = (f32[128,256]{1,0:T(8,128)}, f32[128,256]{1,0:T(8,128)S(1)}, u32[]{:S(2)}, u32[]{:S(2)}) collective-permute-start(f32[128,256]{1,0:T(8,128)} %get-tuple-element.18), channel_id=1, source_target_pairs={{0,256},{1,257},{2,258},{3,259},{4,260},{5,261},{6,262},{7,263},{8... | collective-permute-start | bytes 393224 | tf_op jit(solution)/shard_map/ppermute | solution.py:40
  93.1 8.0 %collective-permute-start.1 = (f32[128,256]{1,0:T(8,128)}, f32[128,256]{1,0:T(8,128)S(1)}, u32[]{:S(2)}, u32[]{:S(2)}) collective-permute-start(f32[128,256]{1,0:T(8,128)} %get-tuple-element.19), channel_id=1, source_target_pairs={{0,512},{1,513},{2,514},{3,515},{4,516},{5,517},{6,518},{7,519},{8... | collective-permute-start | bytes 393224 | tf_op jit(solution)/shard_map/ppermute | solution.py:40
  95.0 9.7 %collective-permute-start.2 = (f32[128,256]{1,0:T(8,128)}, f32[128,256]{1,0:T(8,128)S(1)}, u32[]{:S(2)}, u32[]{:S(2)}) collective-permute-start(f32[128,256]{1,0:T(8,128)} %get-tuple-element.20), channel_id=1, source_target_pairs={{0,768},{1,769},{2,770},{3,771},{4,772},{5,773},{6,774},{7,775},{8... | collective-permute-start | bytes 393224 | tf_op jit(solution)/shard_map/ppermute | solution.py:40
  105.0 11.9 %collective-permute-start.3 = (bf16[136,256]{1,0:T(8,128)(2,1)S(1)}, bf16[136,256]{1,0:T(8,128)(2,1)S(1)}, u32[]{:S(2)}, u32[]{:S(2)}) collective-permute-start(bf16[136,256]{1,0:T(8,128)(2,1)S(1)} %merge.1), channel_id=1, source_target_pairs={{0,8},{1,9},{2,10},{3,11},{4,12},{5,13},{6,14},{7,15},{8,16},{9,17... | collective-permute-start | bytes 208904 | tf_op jit(solution)/shard_map/ppermute | solution.py:35
  109.3 7.6 %collective-permute-start.4 = (bf16[136,256]{1,0:T(8,128)(2,1)S(1)}, bf16[136,256]{1,0:T(8,128)(2,1)S(1)}, u32[]{:S(2)}, u32[]{:S(2)}) collective-permute-start(bf16[136,256]{1,0:T(8,128)(2,1)S(1)} %merge.1), channel_id=1, source_target_pairs={{0,16},{1,17},{2,18},{3,19},{4,20},{5,21},{6,22},{7,23},{8,24},{9,... | collective-permute-start | bytes 208904 | tf_op jit(solution)/shard_map/ppermute | solution.py:35
  113.3 7.0 %collective-permute-start.5 = (bf16[136,256]{1,0:T(8,128)(2,1)S(1)}, bf16[136,256]{1,0:T(8,128)(2,1)S(1)}, u32[]{:S(2)}, u32[]{:S(2)}) collective-permute-start(bf16[136,256]{1,0:T(8,128)(2,1)S(1)} %merge.1), channel_id=1, source_target_pairs={{0,24},{1,25},{2,26},{3,27},{4,28},{5,29},{6,30},{7,31},{8,32},{9,... | collective-permute-start | bytes 208904 | tf_op jit(solution)/shard_map/ppermute | solution.py:35
  115.5 11.5 %collective-permute-start.6 = (bf16[136,256]{1,0:T(8,128)(2,1)S(1)}, bf16[136,256]{1,0:T(8,128)(2,1)S(1)}, u32[]{:S(2)}, u32[]{:S(2)}) collective-permute-start(bf16[136,256]{1,0:T(8,128)(2,1)S(1)} %merge.1), channel_id=1, source_target_pairs={{0,32},{1,33},{2,34},{3,35},{4,36},{5,37},{6,38},{7,39},{8,40},{9,... | collective-permute-start | bytes 208904 | tf_op jit(solution)/shard_map/ppermute | solution.py:35
  127.0 3.9 %collective-permute-start.7 = (bf16[5,136,256]{2,1,0:T(8,128)(2,1)S(1)}, bf16[5,136,256]{2,1,0:T(8,128)(2,1)S(1)}, u32[]{:S(2)}, u32[]{:S(2)}) collective-permute-start(bf16[5,136,256]{2,1,0:T(8,128)(2,1)S(1)} %bitcast_dynamic-update-slice_fusion.mine_ref), channel_id=1, source_target_pairs={{0,4},{1,5},{2,6},{3,7},{4,0},{5,1},{6,2},{7,3},{8,12},{9,13},{10,... | collective-permute-start | bytes 1044488 | tf_op jit(solution)/shard_map/ppermute | solution.py:35

commit v7 on v6

--- a/solution.py
+++ b/solution.py
@@ -9,6 +9,7 @@
 HEAD = 128
 QPK = 8
 CAP = 4
+LOG2E = 1.4426950408889634
 HEADS_STEP = 4
 NX = 4
 NZ = 4
@@ -132,21 +133,30 @@
 
 
 def project_extra(
-    place_ref, rows_ref, key_ref, value_ref, far_ref, vis_ref, out_ref, weights_ref, out_sem
+    place_ref, rows_ref, key_ref, value_ref, far_ref, vis_ref, out_ref, weights_ref, in_sem, out_sem
 ):
     members, sources, part, cols = far_ref.shape
     tokens = rows_ref.shape[1] - NS * CAP
     z = place_ref[2]
     shard = NEAR * part
     own = pl.ds(pl.multiple_of(z * shard, shard), shard)
-    weights_ref[own, :cols] = key_ref[...]
-    weights_ref[own, cols:] = value_ref[...]
+    copies = [(key_ref, own, 0), (value_ref, own, 1)]
     for i in range(sources):
         first = lax.rem(z + 1 + i, NZ) * shard
         for m in range(members):
             chip, core = divmod(m, 2)
             at = pl.ds(pl.multiple_of(first + chip * part, part), part)
-            weights_ref[at, core * cols : (core + 1) * cols] = far_ref[m, i]
+            copies.append((far_ref.at[m, i], at, core))
+    copies = [
+        pltpu.make_async_copy(
+            ref, weights_ref.at[at, pl.ds(side * cols, cols)], in_sem.at[k]
+        )
+        for k, (ref, at, side) in enumerate(copies)
+    ]
+    for copy in copies:
+        copy.start()
+    for copy in copies:
+        copy.wait()
     copy = pltpu.make_async_copy(weights_ref, out_ref, out_sem)
     copy.start()
     weights = weights_ref[...]
@@ -166,17 +176,21 @@
         grid_spec=pltpu.PrefetchScalarGridSpec(
             num_scalar_prefetch=1,
             grid=(1,),
-            in_specs=[IN_VMEM, whole(w_key.shape), whole(w_value.shape), IN_VMEM],
+            in_specs=[IN_VMEM] + [pl.BlockSpec(memory_space=pl.ANY)] * 3,
             out_specs=[
                 pl.BlockSpec(vis.shape, lambda i, _: (0, 0, 0)),
                 pl.BlockSpec(memory_space=pl.ANY),
             ],
-            scratch_shapes=[pltpu.VMEM((part, cols), jnp.bfloat16), pltpu.SemaphoreType.DMA],
+            scratch_shapes=[
+                pltpu.VMEM((part, cols), jnp.bfloat16),
+                pltpu.SemaphoreType.DMA((2 + far.shape[0] * far.shape[1],)),
+                pltpu.SemaphoreType.DMA,
+            ],
         ),
         out_shape=[vis, pltpu.HBM((part, cols), jnp.bfloat16)],
         compiler_params=pltpu.CompilerParams(vmem_limit_bytes=16 * MIB),
         name="project_extra",
-    )(place, in_vmem(rows), in_hbm(w_key), in_hbm(w_value), far)
+    )(place, in_vmem(rows), in_hbm(w_key), in_hbm(w_value), in_hbm(far))
 
 
 def project_text(place_ref, rows_ref, weights_ref, own_ref, *text_refs):
@@ -258,7 +272,7 @@
 
 
 def attend(place_ref, q_hbm, mine_ref, other_ref, my_docs_ref, out_ref, *scratch):
-    bias_ref, keys_ref, values_ref, q_ref, q_sem = scratch
+    bias_ref, keys_ref, values_ref, q_ref, q_rows, q_sem = scratch
     tokens = q_hbm.shape[0]
     blocks = mine_ref.shape[0]
 
@@ -282,22 +296,27 @@
                 keys_ref[at : at + tokens, :] = ref[d, :tokens, :HEAD]
                 values_ref[at : at + tokens, :] = ref[d, :tokens, HEAD:]
         copy.wait()
-
-    scale = 1.0 / jnp.sqrt(jnp.float32(HEAD))
-    first = pl.multiple_of(pl.program_id(0) * HEADS_STEP * HEAD, HEAD)
+        for h in range(QPK):
+            q_rows[h * tokens : (h + 1) * tokens, :] = q_ref[:, h * HEAD : (h + 1) * HEAD]
+
+    scale = jnp.float32(LOG2E) / jnp.sqrt(jnp.float32(HEAD))
+    rows = HEADS_STEP * tokens
+    at = pl.ds(pl.multiple_of(pl.program_id(0) * rows, rows), rows)
+    scores = lax.dot_general(
+        q_rows[at, :], keys_ref[...], (((1,), (1,)), ((), ())), preferred_element_type=jnp.float32
+    )
+    scores = scores.reshape(HEADS_STEP, tokens, -1) * scale + bias_ref[...][None]
+    top = jnp.max(scores, axis=2, keepdims=True)
+    weights = jnp.exp2(scores - top)
+    total = jnp.sum(weights, axis=2, keepdims=True)
+    mixed = jnp.dot(
+        weights.astype(jnp.bfloat16).reshape(rows, -1),
+        values_ref[...],
+        preferred_element_type=jnp.float32,
+    )
+    mixed = mixed.reshape(HEADS_STEP, tokens, HEAD) / total
     for h in range(HEADS_STEP):
-        head = slice(h * HEAD, (h + 1) * HEAD)
-        scores = lax.dot_general(
-            q_ref[:, pl.ds(first + h * HEAD, HEAD)], keys_ref[...], (((1,), (1,)), ((), ())), preferred_element_type=jnp.float32
-        )
-        scores = scores * scale + bias_ref[...]
-        top = jnp.max(scores, axis=1, keepdims=True)
-        weights = jnp.exp(scores - top)
-        total = jnp.sum(weights, axis=1, keepdims=True)
-        mixed = jnp.dot(
-            weights.astype(jnp.bfloat16), values_ref[...], preferred_element_type=jnp.float32
-        )
-        out_ref[:, head] = (mixed / total).astype(out_ref.dtype)
+        out_ref[:, h * HEAD : (h + 1) * HEAD] = mixed[h].astype(out_ref.dtype)
 
 
 def attention(place, queries, mine, other, my_docs):
@@ -320,6 +339,7 @@
                 pltpu.VMEM((span, HEAD), jnp.bfloat16),
                 pltpu.VMEM((span, HEAD), jnp.bfloat16),
                 pltpu.VMEM(queries.shape, queries.dtype),
+                pltpu.VMEM((QPK * tokens, HEAD), queries.dtype),
                 pltpu.SemaphoreType.DMA,
             ],
         ),

time: 137 us -> 137 us (level)
  the two profiles are of different devices: /device:TPU:103 before, /device:TPU:127 now
where the time goes in v7:
time: 137 us; the launch traced here: 136 us
  blocking collectives  54 us (39%)
  starting transfers between devices  41.2 us (30%)
  waiting for transfers between devices  22.8 us (17%)
  Pallas kernels  17.2 us (13%)
    all_gather x1, blocking collectives, program(): got = lax.all_gather(piece, 'grp', axis=0, axis_index_groups=OVER_Z)  40.4 us
    ppermute x5, starting transfers between devices, seq_permute(): return lax.ppermute(array, AXES, pairs)  14.4 us
    all_gather x1, blocking collectives, program(): far = lax.all_gather(far, 'seq', axis=0, axis_index_groups=OVER_NEAR)  13.7 us
    ppermute x5, waiting for transfers between devices, seq_permute(): return lax.ppermute(array, AXES, pairs)  11.3 us
    all_to_all x1, starting transfers between devices, program(): vis = lax.all_to_all(vis, 'seq', 0, 0, tiled=True)  9.43 us
    all_to_all x2, starting transfers between devices, exchange_x(): lax.all_to_all(array, 'grp', 0, 0, axis_index_groups=OVER_X, tiled=True)  9 us
    ppermute x3, starting transfers between devices, x_permute(): lax.ppermute(array, AXES, [(i, (i + d * step) % size) for i in range(size)])  8.37 us
    ppermute x3, waiting for transfers between devices, x_permute(): lax.ppermute(array, AXES, [(i, (i + d * step) % size) for i in range(size)])  6.93 us
  transfers between devices with their start and end apart: 11, of which 6 were waited for; matrix products, arithmetic and copies ran while one was open for 0% of the time, Pallas kernels for 2%

profile of v7, /device:TPU:127, one launch (start us, length us, event | category | flops | bytes accessed | tf_op | source)
XLA Modules:
  0.0 136.0 jit_solution(6307990803317451822)
XLA Ops:
  0.0 0.1 pad_add_fusion.place_ref
  0.1 3.4 %pack.1 = (bf16[4,192,2048]{2,1,0:T(8,128)(2,1)}, bf16[256,128]{1,0:T(8,128)(2,1)S(1)}) custom-call(s32[3]{0:T(128)S(1)} %pad_add_fusion.place_ref, bf16[128,8192]{1,0:T(8,128)(2,1)} %text_ref.1, bf16[1,16,4,8192]{3,2,1,0:T(4,128)(2,1)} %extra_ref.1, bf16[512,128]{1,0:T(8,128)(2,1)} %key_ref.3, bf16[512,128]{1,0:T(8,128)(2,1)} %value_ref.3), custom_call_target="tpu_custom_call" | custom-call | tf_op jit(solution)/shard_map/pack/pallas_call | solution.py:111
  3.5 4.2 %all-to-all-start = ((bf16[4,192,2048]{2,1,0:T(8,128)(2,1)}), bf16[4,192,2048]{2,1,0:T(8,128)(2,1)S(1)}, u32[]{:S(2)}, u32[]{:S(2)}) async-start(bf16[4,192,2048]{2,1,0:T(8,128)(2,1)} %get-tuple-element.13), calls=%async_computation | async-start | bytes 6291456 | tf_op jit(solution)/shard_map/all_to_all | solution.py:353
  7.8 40.4 %all-gather = bf16[1024,128]{1,0:T(8,128)(2,1)S(1)} all-gather(bf16[256,128]{1,0:T(8,128)(2,1)S(1)} %get-tuple-element.14), channel_id=2, replica_groups={{0,64,128,192},{256,320,384,448},{512,576,640,704},{768,832,896,960},{1..., dimensions={0}, use_global_device_ids=true | all-gather | bytes 327680 | tf_op jit(solution)/shard_map/all_gather | solution.py:363
  48.2 0.0 copy-start
  48.2 0.0 copy-start.1
  48.2 13.7 %all-gather.1 = bf16[12,256,128]{2,1,0:T(8,128)(2,1)} all-gather(bf16[3,256,128]{2,1,0:T(8,128)(2,1)S(1)} %pad_maximum_fusion), channel_id=3, replica_groups={{0,4,8,12},{16,20,24,28},{32,36,40,44},{48,52,56,60},{1,5,9,13},{17,21,..., dimensions={0}, use_global_device_ids=true | all-gather | bytes 983040 | tf_op jit(solution)/shard_map/all_gather | solution.py:369
  61.9 0.0 all-to-all-done.rows_ref
  61.9 3.6 %project_extra.1 = (f32[4,64,256]{2,1,0:T(8,128)}, bf16[2048,256]{1,0:T(8,128)(2,1)}) custom-call(s32[3]{0:T(128)S(1)} %pad_add_fusion.place_ref, bf16[4,192,2048]{2,1,0:T(8,128)(2,1)S(1)} %all-to-all-done.rows_ref, bf16[512,128]{1,0:T(8,128)(2,1)} %key_ref.3, bf16[512,128]{1,0:T(8,128)(2,1)} %value_ref.3, bf16[4,3,256,128]{3,2,1,0:T(8,128)(2,1)} %bitcast.21), custom_call_target="tpu_custom_call" | custom-call | tf_op jit(solution)/shard_map/project_extra/pallas_call | solution.py:174
  65.5 4.8 %all-to-all-start.1 = ((f32[4,64,256]{2,1,0:T(8,128)}), f32[4,64,256]{2,1,0:T(8,128)S(1)}, u32[]{:S(2)}, u32[]{:S(2)}) async-start(f32[4,64,256]{2,1,0:T(8,128)} %get-tuple-element.15), calls=%async_computation.1 | async-start | bytes 524288 | tf_op jit(solution)/shard_map/all_to_all | solution.py:353
  70.3 0.0 copy-done
  70.3 0.1 copy.12
  70.4 0.1 convert_element_type.18
  70.5 4.6 %all-to-all-done.1.sums_ref = f32[4,64,256]{2,1,0:T(8,128)S(1)} async-done(((f32[4,64,256]{2,1,0:T(8,128)}), f32[4,64,256]{2,1,0:T(8,128)S(1)}, u32[]{:S(2)}, u32[]{:S(2)}) %all-to-all-start.1) | async-done | bytes 262176 | tf_op jit(solution)/shard_map/all_to_all | solution.py:353
  75.1 0.1 broadcast_in_dim.4.marks_ref
  75.2 0.6 settle.1
  75.8 9.4 %all-to-all-start.2 = ((bf16[16,4,384]{2,1,0:T(4,128)(2,1)}), bf16[16,4,384]{2,1,0:T(4,128)(2,1)S(1)}, u32[]{:S(2)}, u32[]{:S(2)}) async-start(bf16[16,4,384]{2,1,0:T(4,128)(2,1)} %settle.1), calls=%async_computation.2 | async-start | bytes 98304 | tf_op jit(solution)/shard_map/all_to_all | solution.py:378
  85.2 0.0 copy-done.1
  85.3 3.2 %project_text.1 = (f32[128,256]{1,0:T(8,128)S(1)}, f32[128,256]{1,0:T(8,128)}, f32[128,256]{1,0:T(8,128)}, f32[128,256]{1,0:T(8,128)}) custom-call(s32[3]{0:T(128)S(1)} %pad_add_fusion.place_ref, bf16[4,192,2048]{2,1,0:T(8,128)(2,1)S(1)} %all-to-all-done.rows_ref, bf16[2048,256]{1,0:T(8,128)(2,1)} %get-tuple-element.16.weights_ref), custom_call_target="tpu_custom_call" | custom-call | tf_op jit(solution)/shard_map/project_text/pallas_call | solution.py:209
  88.4 3.7 %collective-permute-start = (f32[128,256]{1,0:T(8,128)}, f32[128,256]{1,0:T(8,128)S(1)}, u32[]{:S(2)}, u32[]{:S(2)}) collective-permute-start(f32[128,256]{1,0:T(8,128)} %get-tuple-element.18), channel_id=1, source_target_pairs={{0,256},{1,257},{2,258},{3,259},{4,260},{5,261},{6,262},{7,263},{8... | collective-permute-start | bytes 393224 | tf_op jit(solution)/shard_map/ppermute | solution.py:41
  92.1 1.9 %collective-permute-start.1 = (f32[128,256]{1,0:T(8,128)}, f32[128,256]{1,0:T(8,128)S(1)}, u32[]{:S(2)}, u32[]{:S(2)}) collective-permute-start(f32[128,256]{1,0:T(8,128)} %get-tuple-element.19), channel_id=1, source_target_pairs={{0,512},{1,513},{2,514},{3,515},{4,516},{5,517},{6,518},{7,519},{8... | collective-permute-start | bytes 393224 | tf_op jit(solution)/shard_map/ppermute | solution.py:41
  94.1 2.8 %collective-permute-start.2 = (f32[128,256]{1,0:T(8,128)}, f32[128,256]{1,0:T(8,128)S(1)}, u32[]{:S(2)}, u32[]{:S(2)}) collective-permute-start(f32[128,256]{1,0:T(8,128)} %get-tuple-element.20), channel_id=1, source_target_pairs={{0,768},{1,769},{2,770},{3,771},{4,772},{5,773},{6,774},{7,775},{8... | collective-permute-start | bytes 393224 | tf_op jit(solution)/shard_map/ppermute | solution.py:41
  96.8 0.0 collective-permute-done.refs_1_
  96.9 3.3 %collective-permute-done.1.refs_2_ = f32[128,256]{1,0:T(8,128)S(1)} collective-permute-done((f32[128,256]{1,0:T(8,128)}, f32[128,256]{1,0:T(8,128)S(1)}, u32[]{:S(2)}, u32[]{:S(2)}) %collective-permute-start.1) | collective-permute-done | bytes 131104 | tf_op jit(solution)/shard_map/ppermute | solution.py:41
  100.1 3.7 %collective-permute-done.2.refs_3_ = f32[128,256]{1,0:T(8,128)S(1)} collective-permute-done((f32[128,256]{1,0:T(8,128)}, f32[128,256]{1,0:T(8,128)S(1)}, u32[]{:S(2)}, u32[]{:S(2)}) %collective-permute-start.2) | collective-permute-done | bytes 131104 | tf_op jit(solution)/shard_map/ppermute | solution.py:41
  103.8 0.0 all-to-all-done.2.vis_ref
  103.8 0.2 merge.1
  104.0 4.3 %collective-permute-start.3 = (bf16[136,256]{1,0:T(8,128)(2,1)S(1)}, bf16[136,256]{1,0:T(8,128)(2,1)S(1)}, u32[]{:S(2)}, u32[]{:S(2)}) collective-permute-start(bf16[136,256]{1,0:T(8,128)(2,1)S(1)} %merge.1), channel_id=1, source_target_pairs={{0,8},{1,9},{2,10},{3,11},{4,12},{5,13},{6,14},{7,15},{8,16},{9,17... | collective-permute-start | bytes 208904 | tf_op jit(solution)/shard_map/ppermute | solution.py:36
  108.4 4.0 %collective-permute-start.4 = (bf16[136,256]{1,0:T(8,128)(2,1)S(1)}, bf16[136,256]{1,0:T(8,128)(2,1)S(1)}, u32[]{:S(2)}, u32[]{:S(2)}) collective-permute-start(bf16[136,256]{1,0:T(8,128)(2,1)S(1)} %merge.1), channel_id=1, source_target_pairs={{0,16},{1,17},{2,18},{3,19},{4,20},{5,21},{6,22},{7,23},{8,24},{9,... | collective-permute-start | bytes 208904 | tf_op jit(solution)/shard_map/ppermute | solution.py:36
  112.4 2.2 %collective-permute-start.5 = (bf16[136,256]{1,0:T(8,128)(2,1)S(1)}, bf16[136,256]{1,0:T(8,128)(2,1)S(1)}, u32[]{:S(2)}, u32[]{:S(2)}) collective-permute-start(bf16[136,256]{1,0:T(8,128)(2,1)S(1)} %merge.1), channel_id=1, source_target_pairs={{0,24},{1,25},{2,26},{3,27},{4,28},{5,29},{6,30},{7,31},{8,32},{9,... | collective-permute-start | bytes 208904 | tf_op jit(solution)/shard_map/ppermute | solution.py:36
  114.6 1.3 collective-permute-start.6
  115.9 0.0 collective-permute-done.3
  115.9 0.0 collective-permute-done.4
  116.0 3.5 %collective-permute-done.5 = bf16[136,256]{1,0:T(8,128)(2,1)S(1)} collective-permute-done((bf16[136,256]{1,0:T(8,128)(2,1)S(1)}, bf16[136,256]{1,0:T(8,128)(2,1)S(1)}, u32[]{:S(2)}, u32[]{:S(2)}) %collective-permute-start.5) | collective-permute-done | bytes 69664 | tf_op jit(solution)/shard_map/ppermute | solution.py:36
  119.4 6.6 %collective-permute-done.6 = bf16[136,256]{1,0:T(8,128)(2,1)S(1)} collective-permute-done((bf16[136,256]{1,0:T(8,128)(2,1)S(1)}, bf16[136,256]{1,0:T(8,128)(2,1)S(1)}, u32[]{:S(2)}, u32[]{:S(2)}) %collective-permute-start.6) | collective-permute-done | bytes 69664 | tf_op jit(solution)/shard_map/ppermute | solution.py:36
  126.1 2.6 %collective-permute-start.7 = (bf16[5,136,256]{2,1,0:T(8,128)(2,1)S(1)}, bf16[5,136,256]{2,1,0:T(8,128)(2,1)S(1)}, u32[]{:S(2)}, u32[]{:S(2)}) collective-permute-start(bf16[5,136,256]{2,1,0:T(8,128)(2,1)S(1)} %bitcast_dynamic-update-slice_fusion.mine_ref), channel_id=1, source_target_pairs={{0,4},{1,5},{2,6},{3,7},{4,0},{5,1},{6,2},{7,3},{8,12},{9,13},{10,... | collective-permute-start | bytes 1044488 | tf_op jit(solution)/shard_map/ppermute | solution.py:36
  128.7 0.1 copy.13.my_docs_ref
  128.8 1.1 collective-permute-done.7.other_ref
  129.9 6.1 %attend.1 = bf16[128,1024]{1,0:T(8,128)(2,1)} custom-call(s32[3]{0:T(128)S(1)} %pad_add_fusion.place_ref, bf16[128,1024]{1,0:T(8,128)(2,1)} %q_hbm.1, bf16[5,136,256]{2,1,0:T(8,128)(2,1)S(1)} %bitcast_dynamic-update-slice_fusion.mine_ref, bf16[5,136,256]{2,1,0:T(8,128)(2,1)S(1)} %collective-permute-done.7.other_ref, f32[128,1]{1,0:T(8,128)S(1)} %copy.13.my_docs_ref), custom_call_target="tpu_custom_call" | custom-call | tf_op jit(solution)/shard_map/attend/pallas_call | solution.py:325
  (11 shorter events, 0.1 us)
Async XLA Ops:
  3.5 58.3 %all-to-all-start = ((bf16[4,192,2048]{2,1,0:T(8,128)(2,1)}), bf16[4,192,2048]{2,1,0:T(8,128)(2,1)S(1)}, u32[]{:S(2)}, u32[]{:S(2)}) async-start(bf16[4,192,2048]{2,1,0:T(8,128)(2,1)} %get-tuple-element.13), calls=%async_computation | async-start | bytes 6291456 | tf_op jit(solution)/shard_map/all_to_all | solution.py:353
  48.2 22.1 %copy-start = (s32[1,16,4]{1,2,0:T(4,128)S(1)}, s32[1,16,4]{1,2,0:T(4,128)}, u32[]{:S(2)}) copy-start(s32[1,16,4]{1,2,0:T(4,128)} %param.10) | copy-start | bytes 772
  48.2 37.0 %copy-start.1 = (s32[1,128]{1,0:T(1,128)S(1)}, s32[1,128]{1,0:T(1,128)}, u32[]{:S(2)}) copy-start(s32[1,128]{1,0:T(1,128)} %param.11) | copy-start | bytes 1540
  65.5 9.6 %all-to-all-start.1 = ((f32[4,64,256]{2,1,0:T(8,128)}), f32[4,64,256]{2,1,0:T(8,128)S(1)}, u32[]{:S(2)}, u32[]{:S(2)}) async-start(f32[4,64,256]{2,1,0:T(8,128)} %get-tuple-element.15), calls=%async_computation.1 | async-start | bytes 524288 | tf_op jit(solution)/shard_map/all_to_all | solution.py:353
  75.8 28.0 %all-to-all-start.2 = ((bf16[16,4,384]{2,1,0:T(4,128)(2,1)}), bf16[16,4,384]{2,1,0:T(4,128)(2,1)S(1)}, u32[]{:S(2)}, u32[]{:S(2)}) async-start(bf16[16,4,384]{2,1,0:T(4,128)(2,1)} %settle.1), calls=%async_computation.2 | async-start | bytes 98304 | tf_op jit(solution)/shard_map/all_to_all | solution.py:378
  88.4 8.4 %collective-permute-start = (f32[128,256]{1,0:T(8,128)}, f32[128,256]{1,0:T(8,128)S(1)}, u32[]{:S(2)}, u32[]{:S(2)}) collective-permute-start(f32[128,256]{1,0:T(8,128)} %get-tuple-element.18), channel_id=1, source_target_pairs={{0,256},{1,257},{2,258},{3,259},{4,260},{5,261},{6,262},{7,263},{8... | collective-permute-start | bytes 393224 | tf_op jit(solution)/shard_map/ppermute | solution.py:41
  92.1 8.0 %collective-permute-start.1 = (f32[128,256]{1,0:T(8,128)}, f32[128,256]{1,0:T(8,128)S(1)}, u32[]{:S(2)}, u32[]{:S(2)}) collective-permute-start(f32[128,256]{1,0:T(8,128)} %get-tuple-element.19), channel_id=1, source_target_pairs={{0,512},{1,513},{2,514},{3,515},{4,516},{5,517},{6,518},{7,519},{8... | collective-permute-start | bytes 393224 | tf_op jit(solution)/shard_map/ppermute | solution.py:41
  94.1 9.7 %collective-permute-start.2 = (f32[128,256]{1,0:T(8,128)}, f32[128,256]{1,0:T(8,128)S(1)}, u32[]{:S(2)}, u32[]{:S(2)}) collective-permute-start(f32[128,256]{1,0:T(8,128)} %get-tuple-element.20), channel_id=1, source_target_pairs={{0,768},{1,769},{2,770},{3,771},{4,772},{5,773},{6,774},{7,775},{8... | collective-permute-start | bytes 393224 | tf_op jit(solution)/shard_map/ppermute | solution.py:41
  104.0 11.9 %collective-permute-start.3 = (bf16[136,256]{1,0:T(8,128)(2,1)S(1)}, bf16[136,256]{1,0:T(8,128)(2,1)S(1)}, u32[]{:S(2)}, u32[]{:S(2)}) collective-permute-start(bf16[136,256]{1,0:T(8,128)(2,1)S(1)} %merge.1), channel_id=1, source_target_pairs={{0,8},{1,9},{2,10},{3,11},{4,12},{5,13},{6,14},{7,15},{8,16},{9,17... | collective-permute-start | bytes 208904 | tf_op jit(solution)/shard_map/ppermute | solution.py:36
  108.4 7.6 %collective-permute-start.4 = (bf16[136,256]{1,0:T(8,128)(2,1)S(1)}, bf16[136,256]{1,0:T(8,128)(2,1)S(1)}, u32[]{:S(2)}, u32[]{:S(2)}) collective-permute-start(bf16[136,256]{1,0:T(8,128)(2,1)S(1)} %merge.1), channel_id=1, source_target_pairs={{0,16},{1,17},{2,18},{3,19},{4,20},{5,21},{6,22},{7,23},{8,24},{9,... | collective-permute-start | bytes 208904 | tf_op jit(solution)/shard_map/ppermute | solution.py:36
  112.4 7.0 %collective-permute-start.5 = (bf16[136,256]{1,0:T(8,128)(2,1)S(1)}, bf16[136,256]{1,0:T(8,128)(2,1)S(1)}, u32[]{:S(2)}, u32[]{:S(2)}) collective-permute-start(bf16[136,256]{1,0:T(8,128)(2,1)S(1)} %merge.1), channel_id=1, source_target_pairs={{0,24},{1,25},{2,26},{3,27},{4,28},{5,29},{6,30},{7,31},{8,32},{9,... | collective-permute-start | bytes 208904 | tf_op jit(solution)/shard_map/ppermute | solution.py:36
  114.6 11.5 %collective-permute-start.6 = (bf16[136,256]{1,0:T(8,128)(2,1)S(1)}, bf16[136,256]{1,0:T(8,128)(2,1)S(1)}, u32[]{:S(2)}, u32[]{:S(2)}) collective-permute-start(bf16[136,256]{1,0:T(8,128)(2,1)S(1)} %merge.1), channel_id=1, source_target_pairs={{0,32},{1,33},{2,34},{3,35},{4,36},{5,37},{6,38},{7,39},{8,40},{9,... | collective-permute-start | bytes 208904 | tf_op jit(solution)/shard_map/ppermute | solution.py:36
  126.1 3.9 %collective-permute-start.7 = (bf16[5,136,256]{2,1,0:T(8,128)(2,1)S(1)}, bf16[5,136,256]{2,1,0:T(8,128)(2,1)S(1)}, u32[]{:S(2)}, u32[]{:S(2)}) collective-permute-start(bf16[5,136,256]{2,1,0:T(8,128)(2,1)S(1)} %bitcast_dynamic-update-slice_fusion.mine_ref), channel_id=1, source_target_pairs={{0,4},{1,5},{2,6},{3,7},{4,0},{5,1},{6,2},{7,3},{8,12},{9,13},{10,... | collective-permute-start | bytes 1044488 | tf_op jit(solution)/shard_map/ppermute | solution.py:36

commit v8 on v6

--- a/solution.py
+++ b/solution.py
@@ -9,6 +9,7 @@
 HEAD = 128
 QPK = 8
 CAP = 4
+LOG2E = 1.4426950408889634
 HEADS_STEP = 4
 NX = 4
 NZ = 4
@@ -132,21 +133,30 @@
 
 
 def project_extra(
-    place_ref, rows_ref, key_ref, value_ref, far_ref, vis_ref, out_ref, weights_ref, out_sem
+    place_ref, rows_ref, key_ref, value_ref, far_ref, vis_ref, out_ref, weights_ref, in_sem, out_sem
 ):
     members, sources, part, cols = far_ref.shape
     tokens = rows_ref.shape[1] - NS * CAP
     z = place_ref[2]
     shard = NEAR * part
     own = pl.ds(pl.multiple_of(z * shard, shard), shard)
-    weights_ref[own, :cols] = key_ref[...]
-    weights_ref[own, cols:] = value_ref[...]
+    copies = [(key_ref, own, 0), (value_ref, own, 1)]
     for i in range(sources):
         first = lax.rem(z + 1 + i, NZ) * shard
         for m in range(members):
             chip, core = divmod(m, 2)
             at = pl.ds(pl.multiple_of(first + chip * part, part), part)
-            weights_ref[at, core * cols : (core + 1) * cols] = far_ref[m, i]
+            copies.append((far_ref.at[m, i], at, core))
+    copies = [
+        pltpu.make_async_copy(
+            ref, weights_ref.at[at, pl.ds(side * cols, cols)], in_sem.at[k]
+        )
+        for k, (ref, at, side) in enumerate(copies)
+    ]
+    for copy in copies:
+        copy.start()
+    for copy in copies:
+        copy.wait()
     copy = pltpu.make_async_copy(weights_ref, out_ref, out_sem)
     copy.start()
     weights = weights_ref[...]
@@ -166,17 +176,21 @@
         grid_spec=pltpu.PrefetchScalarGridSpec(
             num_scalar_prefetch=1,
             grid=(1,),
-            in_specs=[IN_VMEM, whole(w_key.shape), whole(w_value.shape), IN_VMEM],
+            in_specs=[IN_VMEM] + [pl.BlockSpec(memory_space=pl.ANY)] * 3,
             out_specs=[
                 pl.BlockSpec(vis.shape, lambda i, _: (0, 0, 0)),
                 pl.BlockSpec(memory_space=pl.ANY),
             ],
-            scratch_shapes=[pltpu.VMEM((part, cols), jnp.bfloat16), pltpu.SemaphoreType.DMA],
+            scratch_shapes=[
+                pltpu.VMEM((part, cols), jnp.bfloat16),
+                pltpu.SemaphoreType.DMA((2 + far.shape[0] * far.shape[1],)),
+                pltpu.SemaphoreType.DMA,
+            ],
         ),
         out_shape=[vis, pltpu.HBM((part, cols), jnp.bfloat16)],
         compiler_params=pltpu.CompilerParams(vmem_limit_bytes=16 * MIB),
         name="project_extra",
-    )(place, in_vmem(rows), in_hbm(w_key), in_hbm(w_value), far)
+    )(place, in_vmem(rows), in_hbm(w_key), in_hbm(w_value), in_hbm(far))
 
 
 def project_text(place_ref, rows_ref, weights_ref, own_ref, *text_refs):
@@ -283,7 +297,7 @@
                 values_ref[at : at + tokens, :] = ref[d, :tokens, HEAD:]
         copy.wait()
 
-    scale = 1.0 / jnp.sqrt(jnp.float32(HEAD))
+    scale = jnp.float32(LOG2E) / jnp.sqrt(jnp.float32(HEAD))
     first = pl.multiple_of(pl.program_id(0) * HEADS_STEP * HEAD, HEAD)
     for h in range(HEADS_STEP):
         head = slice(h * HEAD, (h + 1) * HEAD)
@@ -292,7 +306,7 @@
         )
         scores = scores * scale + bias_ref[...]
         top = jnp.max(scores, axis=1, keepdims=True)
-        weights = jnp.exp(scores - top)
+        weights = jnp.exp2(scores - top)
         total = jnp.sum(weights, axis=1, keepdims=True)
         mixed = jnp.dot(
             weights.astype(jnp.bfloat16), values_ref[...], preferred_element_type=jnp.float32
@@ -359,10 +373,10 @@
     docs = jnp.broadcast_to(jnp.tile(doc_ids, (1, cols // tokens)), (8, cols)).astype(jnp.bfloat16)
     block = merged_block(vis, docs, text)
 
-    back = [None] * REACH
-    for d in range(REACH, 0, -1):
-        back[d - 1] = seq_permute(block, later(d))
-    mine = jnp.stack([block, *back])
+    back = {}
+    for d in (2, 3, 1, 4):
+        back[d] = seq_permute(back[2] if d == 4 else block, later(2 if d == 4 else d))
+    mine = jnp.stack([block, *(back[d] for d in range(1, REACH + 1))])
     other = seq_permute(mine, sibling)
     my_docs = doc_ids.reshape(tokens, 1).astype(jnp.float32)
     return attention(where, queries, mine, other, my_docs)

time: 137 us -> 137 us (level)
  the two profiles are of different devices: /device:TPU:103 before, /device:TPU:91 now
where the time goes in v8:
time: 137 us; the launch traced here: 136 us
  blocking collectives  54.7 us (40%)
  starting transfers between devices  50.6 us (37%)
  Pallas kernels  16.9 us (12%)
  waiting for transfers between devices  13.5 us (10%)
    all_gather x1, blocking collectives, program(): got = lax.all_gather(piece, 'grp', axis=0, axis_index_groups=OVER_Z)  42.5 us
    ppermute x5, starting transfers between devices, seq_permute(): return lax.ppermute(array, AXES, pairs)  23.3 us
    all_gather x1, blocking collectives, program(): far = lax.all_gather(far, 'seq', axis=0, axis_index_groups=OVER_NEAR)  12.1 us
    all_to_all x2, starting transfers between devices, exchange_x(): lax.all_to_all(array, 'grp', 0, 0, axis_index_groups=OVER_X, tiled=True)  10.2 us
    ppermute x3, starting transfers between devices, x_permute(): lax.ppermute(array, AXES, [(i, (i + d * step) % size) for i in range(size)])  8.96 us
    all_to_all x1, starting transfers between devices, program(): vis = lax.all_to_all(vis, 'seq', 0, 0, tiled=True)  8.07 us
    pallas_call x1, Pallas kernels, attention(): pl.pallas_call(attend, grid_spec=pltpu.PrefetchScalarGridSpec(num_scalar_...  5.8 us
    all_to_all x2, waiting for transfers between devices, exchange_x(): lax.all_to_all(array, 'grp', 0, 0, axis_index_groups=OVER_X, tiled=True)  5.25 us
  transfers between devices with their start and end apart: 11, of which 5 were waited for; matrix products, arithmetic and copies ran while one was open for 0% of the time, Pallas kernels for 2%

profile of v8, /device:TPU:91, one launch (start us, length us, event | category | flops | bytes accessed | tf_op | source)
XLA Modules:
  0.0 136.4 jit_solution(6823287443629898581)
XLA Ops:
  0.0 0.1 pad_add_fusion.place_ref
  0.1 3.4 %pack.1 = (bf16[4,192,2048]{2,1,0:T(8,128)(2,1)}, bf16[256,128]{1,0:T(8,128)(2,1)S(1)}) custom-call(s32[3]{0:T(128)S(1)} %pad_add_fusion.place_ref, bf16[128,8192]{1,0:T(8,128)(2,1)} %text_ref.1, bf16[1,16,4,8192]{3,2,1,0:T(4,128)(2,1)} %extra_ref.1, bf16[512,128]{1,0:T(8,128)(2,1)} %key_ref.3, bf16[512,128]{1,0:T(8,128)(2,1)} %value_ref.3), custom_call_target="tpu_custom_call" | custom-call | tf_op jit(solution)/shard_map/pack/pallas_call | solution.py:111
  3.5 4.3 %all-to-all-start = ((bf16[4,192,2048]{2,1,0:T(8,128)(2,1)}), bf16[4,192,2048]{2,1,0:T(8,128)(2,1)S(1)}, u32[]{:S(2)}, u32[]{:S(2)}) async-start(bf16[4,192,2048]{2,1,0:T(8,128)(2,1)} %get-tuple-element.13), calls=%async_computation | async-start | bytes 6291456 | tf_op jit(solution)/shard_map/all_to_all | solution.py:347
  7.8 42.5 %all-gather = bf16[1024,128]{1,0:T(8,128)(2,1)S(1)} all-gather(bf16[256,128]{1,0:T(8,128)(2,1)S(1)} %get-tuple-element.14), channel_id=2, replica_groups={{0,64,128,192},{256,320,384,448},{512,576,640,704},{768,832,896,960},{1..., dimensions={0}, use_global_device_ids=true | all-gather | bytes 327680 | tf_op jit(solution)/shard_map/all_gather | solution.py:357
  50.4 0.0 copy-start
  50.4 0.0 copy-start.1
  50.4 12.1 %all-gather.1 = bf16[12,256,128]{2,1,0:T(8,128)(2,1)} all-gather(bf16[3,256,128]{2,1,0:T(8,128)(2,1)S(1)} %pad_maximum_fusion), channel_id=3, replica_groups={{0,4,8,12},{16,20,24,28},{32,36,40,44},{48,52,56,60},{1,5,9,13},{17,21,..., dimensions={0}, use_global_device_ids=true | all-gather | bytes 983040 | tf_op jit(solution)/shard_map/all_gather | solution.py:363
  62.6 0.0 all-to-all-done.rows_ref
  62.6 3.6 %project_extra.1 = (f32[4,64,256]{2,1,0:T(8,128)}, bf16[2048,256]{1,0:T(8,128)(2,1)}) custom-call(s32[3]{0:T(128)S(1)} %pad_add_fusion.place_ref, bf16[4,192,2048]{2,1,0:T(8,128)(2,1)S(1)} %all-to-all-done.rows_ref, bf16[512,128]{1,0:T(8,128)(2,1)} %key_ref.3, bf16[512,128]{1,0:T(8,128)(2,1)} %value_ref.3, bf16[4,3,256,128]{3,2,1,0:T(8,128)(2,1)} %bitcast.21), custom_call_target="tpu_custom_call" | custom-call | tf_op jit(solution)/shard_map/project_extra/pallas_call | solution.py:174
  66.2 5.9 %all-to-all-start.1 = ((f32[4,64,256]{2,1,0:T(8,128)}), f32[4,64,256]{2,1,0:T(8,128)S(1)}, u32[]{:S(2)}, u32[]{:S(2)}) async-start(f32[4,64,256]{2,1,0:T(8,128)} %get-tuple-element.15), calls=%async_computation.1 | async-start | bytes 524288 | tf_op jit(solution)/shard_map/all_to_all | solution.py:347
  72.1 0.0 copy-done
  72.1 0.1 copy.12
  72.2 0.1 convert_element_type.18
  72.3 5.3 %all-to-all-done.1.sums_ref = f32[4,64,256]{2,1,0:T(8,128)S(1)} async-done(((f32[4,64,256]{2,1,0:T(8,128)}), f32[4,64,256]{2,1,0:T(8,128)S(1)}, u32[]{:S(2)}, u32[]{:S(2)}) %all-to-all-start.1) | async-done | bytes 262176 | tf_op jit(solution)/shard_map/all_to_all | solution.py:347
  77.6 0.1 broadcast_in_dim.4.marks_ref
  77.6 0.6 settle.1
  78.3 8.1 %all-to-all-start.2 = ((bf16[16,4,384]{2,1,0:T(4,128)(2,1)}), bf16[16,4,384]{2,1,0:T(4,128)(2,1)S(1)}, u32[]{:S(2)}, u32[]{:S(2)}) async-start(bf16[16,4,384]{2,1,0:T(4,128)(2,1)} %settle.1), calls=%async_computation.2 | async-start | bytes 98304 | tf_op jit(solution)/shard_map/all_to_all | solution.py:372
  86.3 0.0 copy-done.1
  86.4 3.2 %project_text.1 = (f32[128,256]{1,0:T(8,128)S(1)}, f32[128,256]{1,0:T(8,128)}, f32[128,256]{1,0:T(8,128)}, f32[128,256]{1,0:T(8,128)}) custom-call(s32[3]{0:T(128)S(1)} %pad_add_fusion.place_ref, bf16[4,192,2048]{2,1,0:T(8,128)(2,1)S(1)} %all-to-all-done.rows_ref, bf16[2048,256]{1,0:T(8,128)(2,1)} %get-tuple-element.16.weights_ref), custom_call_target="tpu_custom_call" | custom-call | tf_op jit(solution)/shard_map/project_text/pallas_call | solution.py:209
  89.5 1.9 %collective-permute-start = (f32[128,256]{1,0:T(8,128)}, f32[128,256]{1,0:T(8,128)S(1)}, u32[]{:S(2)}, u32[]{:S(2)}) collective-permute-start(f32[128,256]{1,0:T(8,128)} %get-tuple-element.18), channel_id=1, source_target_pairs={{0,256},{1,257},{2,258},{3,259},{4,260},{5,261},{6,262},{7,263},{8... | collective-permute-start | bytes 393224 | tf_op jit(solution)/shard_map/ppermute | solution.py:41
  91.5 4.9 %collective-permute-start.1 = (f32[128,256]{1,0:T(8,128)}, f32[128,256]{1,0:T(8,128)S(1)}, u32[]{:S(2)}, u32[]{:S(2)}) collective-permute-start(f32[128,256]{1,0:T(8,128)} %get-tuple-element.19), channel_id=1, source_target_pairs={{0,512},{1,513},{2,514},{3,515},{4,516},{5,517},{6,518},{7,519},{8... | collective-permute-start | bytes 393224 | tf_op jit(solution)/shard_map/ppermute | solution.py:41
  96.3 2.2 %collective-permute-start.2 = (f32[128,256]{1,0:T(8,128)}, f32[128,256]{1,0:T(8,128)S(1)}, u32[]{:S(2)}, u32[]{:S(2)}) collective-permute-start(f32[128,256]{1,0:T(8,128)} %get-tuple-element.20), channel_id=1, source_target_pairs={{0,768},{1,769},{2,770},{3,771},{4,772},{5,773},{6,774},{7,775},{8... | collective-permute-start | bytes 393224 | tf_op jit(solution)/shard_map/ppermute | solution.py:41
  98.5 0.0 collective-permute-done.refs_1_
  98.6 1.2 collective-permute-done.1.refs_2_
  99.7 2.5 %collective-permute-done.2.refs_3_ = f32[128,256]{1,0:T(8,128)S(1)} collective-permute-done((f32[128,256]{1,0:T(8,128)}, f32[128,256]{1,0:T(8,128)S(1)}, u32[]{:S(2)}, u32[]{:S(2)}) %collective-permute-start.2) | collective-permute-done | bytes 131104 | tf_op jit(solution)/shard_map/ppermute | solution.py:41
  102.3 0.0 all-to-all-done.2.vis_ref
  102.3 0.2 merge.1
  102.5 3.1 %collective-permute-start.3 = (bf16[136,256]{1,0:T(8,128)(2,1)S(1)}, bf16[136,256]{1,0:T(8,128)(2,1)S(1)}, u32[]{:S(2)}, u32[]{:S(2)}) collective-permute-start(bf16[136,256]{1,0:T(8,128)(2,1)S(1)} %merge.1), channel_id=1, source_target_pairs={{0,8},{1,9},{2,10},{3,11},{4,12},{5,13},{6,14},{7,15},{8,16},{9,17... | collective-permute-start | bytes 208904 | tf_op jit(solution)/shard_map/ppermute | solution.py:36
  105.6 5.2 %collective-permute-start.4 = (bf16[136,256]{1,0:T(8,128)(2,1)S(1)}, bf16[136,256]{1,0:T(8,128)(2,1)S(1)}, u32[]{:S(2)}, u32[]{:S(2)}) collective-permute-start(bf16[136,256]{1,0:T(8,128)(2,1)S(1)} %merge.1), channel_id=1, source_target_pairs={{0,16},{1,17},{2,18},{3,19},{4,20},{5,21},{6,22},{7,23},{8,24},{9,... | collective-permute-start | bytes 208904 | tf_op jit(solution)/shard_map/ppermute | solution.py:36
  110.9 3.1 %collective-permute-start.5 = (bf16[136,256]{1,0:T(8,128)(2,1)S(1)}, bf16[136,256]{1,0:T(8,128)(2,1)S(1)}, u32[]{:S(2)}, u32[]{:S(2)}) collective-permute-start(bf16[136,256]{1,0:T(8,128)(2,1)S(1)} %merge.1), channel_id=1, source_target_pairs={{0,24},{1,25},{2,26},{3,27},{4,28},{5,29},{6,30},{7,31},{8,32},{9,... | collective-permute-start | bytes 208904 | tf_op jit(solution)/shard_map/ppermute | solution.py:36
  114.0 0.0 collective-permute-done.4
  114.0 4.8 %collective-permute-start.6 = (bf16[136,256]{1,0:T(8,128)(2,1)S(1)}, bf16[136,256]{1,0:T(8,128)(2,1)S(1)}, u32[]{:S(2)}, u32[]{:S(2)}) collective-permute-start(bf16[136,256]{1,0:T(8,128)(2,1)S(1)} %collective-permute-done.4), channel_id=1, source_target_pairs={{0,16},{1,17},{2,18},{3,19},{4,20},{5,21},{6,22},{7,23},{8,24},{9,... | collective-permute-start | bytes 208904 | tf_op jit(solution)/shard_map/ppermute | solution.py:36
  118.8 0.0 collective-permute-done.3
  118.8 0.0 collective-permute-done.5
  118.8 3.4 %collective-permute-done.6 = bf16[136,256]{1,0:T(8,128)(2,1)S(1)} collective-permute-done((bf16[136,256]{1,0:T(8,128)(2,1)S(1)}, bf16[136,256]{1,0:T(8,128)(2,1)S(1)}, u32[]{:S(2)}, u32[]{:S(2)}) %collective-permute-start.6) | collective-permute-done | bytes 69664 | tf_op jit(solution)/shard_map/ppermute | solution.py:36
  122.2 7.1 %collective-permute-start.7 = (bf16[5,136,256]{2,1,0:T(8,128)(2,1)S(1)}, bf16[5,136,256]{2,1,0:T(8,128)(2,1)S(1)}, u32[]{:S(2)}, u32[]{:S(2)}) collective-permute-start(bf16[5,136,256]{2,1,0:T(8,128)(2,1)S(1)} %bitcast_dynamic-update-slice_fusion.mine_ref), channel_id=1, source_target_pairs={{0,4},{1,5},{2,6},{3,7},{4,0},{5,1},{6,2},{7,3},{8,12},{9,13},{10,... | collective-permute-start | bytes 1044488 | tf_op jit(solution)/shard_map/ppermute | solution.py:36
  129.4 0.1 copy.13.my_docs_ref
  129.5 1.1 collective-permute-done.7.other_ref
  130.6 5.8 %attend.1 = bf16[128,1024]{1,0:T(8,128)(2,1)} custom-call(s32[3]{0:T(128)S(1)} %pad_add_fusion.place_ref, bf16[128,1024]{1,0:T(8,128)(2,1)} %q_hbm.1, bf16[5,136,256]{2,1,0:T(8,128)(2,1)S(1)} %bitcast_dynamic-update-slice_fusion.mine_ref, bf16[5,136,256]{2,1,0:T(8,128)(2,1)S(1)} %collective-permute-done.7.other_ref, f32[128,1]{1,0:T(8,128)S(1)} %copy.13.my_docs_ref), custom_call_target="tpu_custom_call" | custom-call | tf_op jit(solution)/shard_map/attend/pallas_call | solution.py:320
  (11 shorter events, 0.1 us)
Async XLA Ops:
  3.5 59.0 %all-to-all-start = ((bf16[4,192,2048]{2,1,0:T(8,128)(2,1)}), bf16[4,192,2048]{2,1,0:T(8,128)(2,1)S(1)}, u32[]{:S(2)}, u32[]{:S(2)}) async-start(bf16[4,192,2048]{2,1,0:T(8,128)(2,1)} %get-tuple-element.13), calls=%async_computation | async-start | bytes 6291456 | tf_op jit(solution)/shard_map/all_to_all | solution.py:347
  50.4 21.8 %copy-start = (s32[1,16,4]{1,2,0:T(4,128)S(1)}, s32[1,16,4]{1,2,0:T(4,128)}, u32[]{:S(2)}) copy-start(s32[1,16,4]{1,2,0:T(4,128)} %param.10) | copy-start | bytes 772
  50.4 35.9 %copy-start.1 = (s32[1,128]{1,0:T(1,128)S(1)}, s32[1,128]{1,0:T(1,128)}, u32[]{:S(2)}) copy-start(s32[1,128]{1,0:T(1,128)} %param.11) | copy-start | bytes 1540
  66.2 11.4 %all-to-all-start.1 = ((f32[4,64,256]{2,1,0:T(8,128)}), f32[4,64,256]{2,1,0:T(8,128)S(1)}, u32[]{:S(2)}, u32[]{:S(2)}) async-start(f32[4,64,256]{2,1,0:T(8,128)} %get-tuple-element.15), calls=%async_computation.1 | async-start | bytes 524288 | tf_op jit(solution)/shard_map/all_to_all | solution.py:347
  78.3 24.0 %all-to-all-start.2 = ((bf16[16,4,384]{2,1,0:T(4,128)(2,1)}), bf16[16,4,384]{2,1,0:T(4,128)(2,1)S(1)}, u32[]{:S(2)}, u32[]{:S(2)}) async-start(bf16[16,4,384]{2,1,0:T(4,128)(2,1)} %settle.1), calls=%async_computation.2 | async-start | bytes 98304 | tf_op jit(solution)/shard_map/all_to_all | solution.py:372
  89.5 9.0 %collective-permute-start = (f32[128,256]{1,0:T(8,128)}, f32[128,256]{1,0:T(8,128)S(1)}, u32[]{:S(2)}, u32[]{:S(2)}) collective-permute-start(f32[128,256]{1,0:T(8,128)} %get-tuple-element.18), channel_id=1, source_target_pairs={{0,256},{1,257},{2,258},{3,259},{4,260},{5,261},{6,262},{7,263},{8... | collective-permute-start | bytes 393224 | tf_op jit(solution)/shard_map/ppermute | solution.py:41
  91.5 8.3 %collective-permute-start.1 = (f32[128,256]{1,0:T(8,128)}, f32[128,256]{1,0:T(8,128)S(1)}, u32[]{:S(2)}, u32[]{:S(2)}) collective-permute-start(f32[128,256]{1,0:T(8,128)} %get-tuple-element.19), channel_id=1, source_target_pairs={{0,512},{1,513},{2,514},{3,515},{4,516},{5,517},{6,518},{7,519},{8... | collective-permute-start | bytes 393224 | tf_op jit(solution)/shard_map/ppermute | solution.py:41
  96.3 5.9 %collective-permute-start.2 = (f32[128,256]{1,0:T(8,128)}, f32[128,256]{1,0:T(8,128)S(1)}, u32[]{:S(2)}, u32[]{:S(2)}) collective-permute-start(f32[128,256]{1,0:T(8,128)} %get-tuple-element.20), channel_id=1, source_target_pairs={{0,768},{1,769},{2,770},{3,771},{4,772},{5,773},{6,774},{7,775},{8... | collective-permute-start | bytes 393224 | tf_op jit(solution)/shard_map/ppermute | solution.py:41
  102.5 16.3 %collective-permute-start.3 = (bf16[136,256]{1,0:T(8,128)(2,1)S(1)}, bf16[136,256]{1,0:T(8,128)(2,1)S(1)}, u32[]{:S(2)}, u32[]{:S(2)}) collective-permute-start(bf16[136,256]{1,0:T(8,128)(2,1)S(1)} %merge.1), channel_id=1, source_target_pairs={{0,8},{1,9},{2,10},{3,11},{4,12},{5,13},{6,14},{7,15},{8,16},{9,17... | collective-permute-start | bytes 208904 | tf_op jit(solution)/shard_map/ppermute | solution.py:36
  105.6 8.4 %collective-permute-start.4 = (bf16[136,256]{1,0:T(8,128)(2,1)S(1)}, bf16[136,256]{1,0:T(8,128)(2,1)S(1)}, u32[]{:S(2)}, u32[]{:S(2)}) collective-permute-start(bf16[136,256]{1,0:T(8,128)(2,1)S(1)} %merge.1), channel_id=1, source_target_pairs={{0,16},{1,17},{2,18},{3,19},{4,20},{5,21},{6,22},{7,23},{8,24},{9,... | collective-permute-start | bytes 208904 | tf_op jit(solution)/shard_map/ppermute | solution.py:36
  110.9 7.9 %collective-permute-start.5 = (bf16[136,256]{1,0:T(8,128)(2,1)S(1)}, bf16[136,256]{1,0:T(8,128)(2,1)S(1)}, u32[]{:S(2)}, u32[]{:S(2)}) collective-permute-start(bf16[136,256]{1,0:T(8,128)(2,1)S(1)} %merge.1), channel_id=1, source_target_pairs={{0,24},{1,25},{2,26},{3,27},{4,28},{5,29},{6,30},{7,31},{8,32},{9,... | collective-permute-start | bytes 208904 | tf_op jit(solution)/shard_map/ppermute | solution.py:36
  114.0 8.2 %collective-permute-start.6 = (bf16[136,256]{1,0:T(8,128)(2,1)S(1)}, bf16[136,256]{1,0:T(8,128)(2,1)S(1)}, u32[]{:S(2)}, u32[]{:S(2)}) collective-permute-start(bf16[136,256]{1,0:T(8,128)(2,1)S(1)} %collective-permute-done.4), channel_id=1, source_target_pairs={{0,16},{1,17},{2,18},{3,19},{4,20},{5,21},{6,22},{7,23},{8,24},{9,... | collective-permute-start | bytes 208904 | tf_op jit(solution)/shard_map/ppermute | solution.py:36
  122.2 8.4 %collective-permute-start.7 = (bf16[5,136,256]{2,1,0:T(8,128)(2,1)S(1)}, bf16[5,136,256]{2,1,0:T(8,128)(2,1)S(1)}, u32[]{:S(2)}, u32[]{:S(2)}) collective-permute-start(bf16[5,136,256]{2,1,0:T(8,128)(2,1)S(1)} %bitcast_dynamic-update-slice_fusion.mine_ref), channel_id=1, source_target_pairs={{0,4},{1,5},{2,6},{3,7},{4,0},{5,1},{6,2},{7,3},{8,12},{9,13},{10,... | collective-permute-start | bytes 1044488 | tf_op jit(solution)/shard_map/ppermute | solution.py:36

commit v9 on v8

--- a/solution.py
+++ b/solution.py
@@ -373,9 +373,9 @@
     docs = jnp.broadcast_to(jnp.tile(doc_ids, (1, cols // tokens)), (8, cols)).astype(jnp.bfloat16)
     block = merged_block(vis, docs, text)
 
-    back = {}
-    for d in (2, 3, 1, 4):
-        back[d] = seq_permute(back[2] if d == 4 else block, later(2 if d == 4 else d))
+    back = {0: block}
+    for d in (2, 1, 4, 3):
+        back[d] = seq_permute(back[max(d - 2, 0)], later(min(d, 2)))
     mine = jnp.stack([block, *(back[d] for d in range(1, REACH + 1))])
     other = seq_permute(mine, sibling)
     my_docs = doc_ids.reshape(tokens, 1).astype(jnp.float32)

time: 137 us -> 136 us (level)
  the two profiles are of different devices: /device:TPU:91 before, /device:TPU:1 now
where the time goes in v9:
time: 136 us; the launch traced here: 135 us
  blocking collectives  60.9 us (45%)
  starting transfers between devices  43.5 us (32%)
  Pallas kernels  16.9 us (12%)
  waiting for transfers between devices  13.4 us (10%)
    all_gather x1, blocking collectives, program(): got = lax.all_gather(piece, 'grp', axis=0, axis_index_groups=OVER_Z)  50.3 us
    ppermute x5, starting transfers between devices, seq_permute(): return lax.ppermute(array, AXES, pairs)  21.1 us
    all_gather x1, blocking collectives, program(): far = lax.all_gather(far, 'seq', axis=0, axis_index_groups=OVER_NEAR)  10.6 us
    all_to_all x2, starting transfers between devices, exchange_x(): lax.all_to_all(array, 'grp', 0, 0, axis_index_groups=OVER_X, tiled=True)  9.07 us
    ppermute x3, starting transfers between devices, x_permute(): lax.ppermute(array, AXES, [(i, (i + d * step) % size) for i in range(size)])  8.4 us
    all_to_all x2, waiting for transfers between devices, exchange_x(): lax.all_to_all(array, 'grp', 0, 0, axis_index_groups=OVER_X, tiled=True)  5.86 us
    pallas_call x1, Pallas kernels, attention(): pl.pallas_call(attend, grid_spec=pltpu.PrefetchScalarGridSpec(num_scalar_...  5.79 us
    ppermute x3, waiting for transfers between devices, x_permute(): lax.ppermute(array, AXES, [(i, (i + d * step) % size) for i in range(size)])  5.05 us
  transfers between devices with their start and end apart: 11, of which 5 were waited for; matrix products, arithmetic and copies ran while one was open for 0% of the time, Pallas kernels for 2%

profile of v9, /device:TPU:1, one launch (start us, length us, event | category | flops | bytes accessed | tf_op | source)
XLA Modules:
  0.0 135.4 jit_solution(14581988900488841396)
XLA Ops:
  0.0 0.1 pad_add_fusion.place_ref
  0.1 3.4 %pack.1 = (bf16[4,192,2048]{2,1,0:T(8,128)(2,1)}, bf16[256,128]{1,0:T(8,128)(2,1)S(1)}) custom-call(s32[3]{0:T(128)S(1)} %pad_add_fusion.place_ref, bf16[128,8192]{1,0:T(8,128)(2,1)} %text_ref.1, bf16[1,16,4,8192]{3,2,1,0:T(4,128)(2,1)} %extra_ref.1, bf16[512,128]{1,0:T(8,128)(2,1)} %key_ref.3, bf16[512,128]{1,0:T(8,128)(2,1)} %value_ref.3), custom_call_target="tpu_custom_call" | custom-call | tf_op jit(solution)/shard_map/pack/pallas_call | solution.py:111
  3.5 4.8 %all-to-all-start = ((bf16[4,192,2048]{2,1,0:T(8,128)(2,1)}), bf16[4,192,2048]{2,1,0:T(8,128)(2,1)S(1)}, u32[]{:S(2)}, u32[]{:S(2)}) async-start(bf16[4,192,2048]{2,1,0:T(8,128)(2,1)} %get-tuple-element.13), calls=%async_computation | async-start | bytes 6291456 | tf_op jit(solution)/shard_map/all_to_all | solution.py:347
  8.4 50.3 %all-gather = bf16[1024,128]{1,0:T(8,128)(2,1)S(1)} all-gather(bf16[256,128]{1,0:T(8,128)(2,1)S(1)} %get-tuple-element.14), channel_id=2, replica_groups={{0,64,128,192},{256,320,384,448},{512,576,640,704},{768,832,896,960},{1..., dimensions={0}, use_global_device_ids=true | all-gather | bytes 327680 | tf_op jit(solution)/shard_map/all_gather | solution.py:357
  58.7 0.0 copy-start
  58.7 0.0 copy-start.1
  58.8 10.6 %all-gather.1 = bf16[12,256,128]{2,1,0:T(8,128)(2,1)} all-gather(bf16[3,256,128]{2,1,0:T(8,128)(2,1)S(1)} %pad_maximum_fusion), channel_id=3, replica_groups={{0,4,8,12},{16,20,24,28},{32,36,40,44},{48,52,56,60},{1,5,9,13},{17,21,..., dimensions={0}, use_global_device_ids=true | all-gather | bytes 983040 | tf_op jit(solution)/shard_map/all_gather | solution.py:363
  69.3 0.0 all-to-all-done.rows_ref
  69.3 3.6 %project_extra.1 = (f32[4,64,256]{2,1,0:T(8,128)}, bf16[2048,256]{1,0:T(8,128)(2,1)}) custom-call(s32[3]{0:T(128)S(1)} %pad_add_fusion.place_ref, bf16[4,192,2048]{2,1,0:T(8,128)(2,1)S(1)} %all-to-all-done.rows_ref, bf16[512,128]{1,0:T(8,128)(2,1)} %key_ref.3, bf16[512,128]{1,0:T(8,128)(2,1)} %value_ref.3, bf16[4,3,256,128]{3,2,1,0:T(8,128)(2,1)} %bitcast.21), custom_call_target="tpu_custom_call" | custom-call | tf_op jit(solution)/shard_map/project_extra/pallas_call | solution.py:174
  72.9 4.2 %all-to-all-start.1 = ((f32[4,64,256]{2,1,0:T(8,128)}), f32[4,64,256]{2,1,0:T(8,128)S(1)}, u32[]{:S(2)}, u32[]{:S(2)}) async-start(f32[4,64,256]{2,1,0:T(8,128)} %get-tuple-element.15), calls=%async_computation.1 | async-start | bytes 524288 | tf_op jit(solution)/shard_map/all_to_all | solution.py:347
  77.2 0.0 copy-done
  77.2 0.1 copy.12
  77.3 0.1 convert_element_type.18
  77.4 5.9 %all-to-all-done.1.sums_ref = f32[4,64,256]{2,1,0:T(8,128)S(1)} async-done(((f32[4,64,256]{2,1,0:T(8,128)}), f32[4,64,256]{2,1,0:T(8,128)S(1)}, u32[]{:S(2)}, u32[]{:S(2)}) %all-to-all-start.1) | async-done | bytes 262176 | tf_op jit(solution)/shard_map/all_to_all | solution.py:347
  83.2 0.1 broadcast_in_dim.4.marks_ref
  83.3 0.6 settle.1
  83.9 4.9 %all-to-all-start.2 = ((bf16[16,4,384]{2,1,0:T(4,128)(2,1)}), bf16[16,4,384]{2,1,0:T(4,128)(2,1)S(1)}, u32[]{:S(2)}, u32[]{:S(2)}) async-start(bf16[16,4,384]{2,1,0:T(4,128)(2,1)} %settle.1), calls=%async_computation.2 | async-start | bytes 98304 | tf_op jit(solution)/shard_map/all_to_all | solution.py:372
  88.8 0.0 copy-done.1
  88.8 3.2 %project_text.1 = (f32[128,256]{1,0:T(8,128)S(1)}, f32[128,256]{1,0:T(8,128)}, f32[128,256]{1,0:T(8,128)}, f32[128,256]{1,0:T(8,128)}) custom-call(s32[3]{0:T(128)S(1)} %pad_add_fusion.place_ref, bf16[4,192,2048]{2,1,0:T(8,128)(2,1)S(1)} %all-to-all-done.rows_ref, bf16[2048,256]{1,0:T(8,128)(2,1)} %get-tuple-element.16.weights_ref), custom_call_target="tpu_custom_call" | custom-call | tf_op jit(solution)/shard_map/project_text/pallas_call | solution.py:209
  92.0 2.2 %collective-permute-start = (f32[128,256]{1,0:T(8,128)}, f32[128,256]{1,0:T(8,128)S(1)}, u32[]{:S(2)}, u32[]{:S(2)}) collective-permute-start(f32[128,256]{1,0:T(8,128)} %get-tuple-element.18), channel_id=1, source_target_pairs={{0,256},{1,257},{2,258},{3,259},{4,260},{5,261},{6,262},{7,263},{8... | collective-permute-start | bytes 393224 | tf_op jit(solution)/shard_map/ppermute | solution.py:41
  94.2 3.7 %collective-permute-start.1 = (f32[128,256]{1,0:T(8,128)}, f32[128,256]{1,0:T(8,128)S(1)}, u32[]{:S(2)}, u32[]{:S(2)}) collective-permute-start(f32[128,256]{1,0:T(8,128)} %get-tuple-element.19), channel_id=1, source_target_pairs={{0,512},{1,513},{2,514},{3,515},{4,516},{5,517},{6,518},{7,519},{8... | collective-permute-start | bytes 393224 | tf_op jit(solution)/shard_map/ppermute | solution.py:41
  97.9 2.5 %collective-permute-start.2 = (f32[128,256]{1,0:T(8,128)}, f32[128,256]{1,0:T(8,128)S(1)}, u32[]{:S(2)}, u32[]{:S(2)}) collective-permute-start(f32[128,256]{1,0:T(8,128)} %get-tuple-element.20), channel_id=1, source_target_pairs={{0,768},{1,769},{2,770},{3,771},{4,772},{5,773},{6,774},{7,775},{8... | collective-permute-start | bytes 393224 | tf_op jit(solution)/shard_map/ppermute | solution.py:41
  100.4 0.0 collective-permute-done.refs_1_
  100.5 1.9 %collective-permute-done.1.refs_2_ = f32[128,256]{1,0:T(8,128)S(1)} collective-permute-done((f32[128,256]{1,0:T(8,128)}, f32[128,256]{1,0:T(8,128)S(1)}, u32[]{:S(2)}, u32[]{:S(2)}) %collective-permute-start.1) | collective-permute-done | bytes 131104 | tf_op jit(solution)/shard_map/ppermute | solution.py:41
  102.4 3.1 %collective-permute-done.2.refs_3_ = f32[128,256]{1,0:T(8,128)S(1)} collective-permute-done((f32[128,256]{1,0:T(8,128)}, f32[128,256]{1,0:T(8,128)S(1)}, u32[]{:S(2)}, u32[]{:S(2)}) %collective-permute-start.2) | collective-permute-done | bytes 131104 | tf_op jit(solution)/shard_map/ppermute | solution.py:41
  105.5 0.0 all-to-all-done.2.vis_ref
  105.5 0.2 merge.1
  105.7 3.1 %collective-permute-start.3 = (bf16[136,256]{1,0:T(8,128)(2,1)S(1)}, bf16[136,256]{1,0:T(8,128)(2,1)S(1)}, u32[]{:S(2)}, u32[]{:S(2)}) collective-permute-start(bf16[136,256]{1,0:T(8,128)(2,1)S(1)} %merge.1), channel_id=1, source_target_pairs={{0,8},{1,9},{2,10},{3,11},{4,12},{5,13},{6,14},{7,15},{8,16},{9,17... | collective-permute-start | bytes 208904 | tf_op jit(solution)/shard_map/ppermute | solution.py:36
  108.9 4.0 %collective-permute-start.4 = (bf16[136,256]{1,0:T(8,128)(2,1)S(1)}, bf16[136,256]{1,0:T(8,128)(2,1)S(1)}, u32[]{:S(2)}, u32[]{:S(2)}) collective-permute-start(bf16[136,256]{1,0:T(8,128)(2,1)S(1)} %merge.1), channel_id=1, source_target_pairs={{0,16},{1,17},{2,18},{3,19},{4,20},{5,21},{6,22},{7,23},{8,24},{9,... | collective-permute-start | bytes 208904 | tf_op jit(solution)/shard_map/ppermute | solution.py:36
  112.9 0.0 collective-permute-done.3
  112.9 5.2 %collective-permute-start.5 = (bf16[136,256]{1,0:T(8,128)(2,1)S(1)}, bf16[136,256]{1,0:T(8,128)(2,1)S(1)}, u32[]{:S(2)}, u32[]{:S(2)}) collective-permute-start(bf16[136,256]{1,0:T(8,128)(2,1)S(1)} %collective-permute-done.3), channel_id=1, source_target_pairs={{0,16},{1,17},{2,18},{3,19},{4,20},{5,21},{6,22},{7,23},{8,24},{9,... | collective-permute-start | bytes 208904 | tf_op jit(solution)/shard_map/ppermute | solution.py:36
  118.1 0.0 collective-permute-done.4
  118.1 4.0 %collective-permute-start.6 = (bf16[136,256]{1,0:T(8,128)(2,1)S(1)}, bf16[136,256]{1,0:T(8,128)(2,1)S(1)}, u32[]{:S(2)}, u32[]{:S(2)}) collective-permute-start(bf16[136,256]{1,0:T(8,128)(2,1)S(1)} %collective-permute-done.4), channel_id=1, source_target_pairs={{0,16},{1,17},{2,18},{3,19},{4,20},{5,21},{6,22},{7,23},{8,24},{9,... | collective-permute-start | bytes 208904 | tf_op jit(solution)/shard_map/ppermute | solution.py:36
  122.2 0.0 collective-permute-done.5
  122.2 1.3 collective-permute-done.6
  123.5 4.8 %collective-permute-start.7 = (bf16[5,136,256]{2,1,0:T(8,128)(2,1)S(1)}, bf16[5,136,256]{2,1,0:T(8,128)(2,1)S(1)}, u32[]{:S(2)}, u32[]{:S(2)}) collective-permute-start(bf16[5,136,256]{2,1,0:T(8,128)(2,1)S(1)} %bitcast_dynamic-update-slice_fusion.mine_ref), channel_id=1, source_target_pairs={{0,4},{1,5},{2,6},{3,7},{4,0},{5,1},{6,2},{7,3},{8,12},{9,13},{10,... | collective-permute-start | bytes 1044488 | tf_op jit(solution)/shard_map/ppermute | solution.py:36
  128.3 0.1 copy.13.my_docs_ref
  128.4 1.1 collective-permute-done.7.other_ref
  129.6 5.8 %attend.1 = bf16[128,1024]{1,0:T(8,128)(2,1)} custom-call(s32[3]{0:T(128)S(1)} %pad_add_fusion.place_ref, bf16[128,1024]{1,0:T(8,128)(2,1)} %q_hbm.1, bf16[5,136,256]{2,1,0:T(8,128)(2,1)S(1)} %bitcast_dynamic-update-slice_fusion.mine_ref, bf16[5,136,256]{2,1,0:T(8,128)(2,1)S(1)} %collective-permute-done.7.other_ref, f32[128,1]{1,0:T(8,128)S(1)} %copy.13.my_docs_ref), custom_call_target="tpu_custom_call" | custom-call | tf_op jit(solution)/shard_map/attend/pallas_call | solution.py:320
  (11 shorter events, 0.1 us)
Async XLA Ops:
  3.5 65.8 %all-to-all-start = ((bf16[4,192,2048]{2,1,0:T(8,128)(2,1)}), bf16[4,192,2048]{2,1,0:T(8,128)(2,1)S(1)}, u32[]{:S(2)}, u32[]{:S(2)}) async-start(bf16[4,192,2048]{2,1,0:T(8,128)(2,1)} %get-tuple-element.13), calls=%async_computation | async-start | bytes 6291456 | tf_op jit(solution)/shard_map/all_to_all | solution.py:347
  58.7 18.5 %copy-start = (s32[1,16,4]{1,2,0:T(4,128)S(1)}, s32[1,16,4]{1,2,0:T(4,128)}, u32[]{:S(2)}) copy-start(s32[1,16,4]{1,2,0:T(4,128)} %param.10) | copy-start | bytes 772
  58.7 30.1 %copy-start.1 = (s32[1,128]{1,0:T(1,128)S(1)}, s32[1,128]{1,0:T(1,128)}, u32[]{:S(2)}) copy-start(s32[1,128]{1,0:T(1,128)} %param.11) | copy-start | bytes 1540
  72.9 10.3 %all-to-all-start.1 = ((f32[4,64,256]{2,1,0:T(8,128)}), f32[4,64,256]{2,1,0:T(8,128)S(1)}, u32[]{:S(2)}, u32[]{:S(2)}) async-start(f32[4,64,256]{2,1,0:T(8,128)} %get-tuple-element.15), calls=%async_computation.1 | async-start | bytes 524288 | tf_op jit(solution)/shard_map/all_to_all | solution.py:347
  83.9 21.6 %all-to-all-start.2 = ((bf16[16,4,384]{2,1,0:T(4,128)(2,1)}), bf16[16,4,384]{2,1,0:T(4,128)(2,1)S(1)}, u32[]{:S(2)}, u32[]{:S(2)}) async-start(bf16[16,4,384]{2,1,0:T(4,128)(2,1)} %settle.1), calls=%async_computation.2 | async-start | bytes 98304 | tf_op jit(solution)/shard_map/all_to_all | solution.py:372
  92.0 8.4 %collective-permute-start = (f32[128,256]{1,0:T(8,128)}, f32[128,256]{1,0:T(8,128)S(1)}, u32[]{:S(2)}, u32[]{:S(2)}) collective-permute-start(f32[128,256]{1,0:T(8,128)} %get-tuple-element.18), channel_id=1, source_target_pairs={{0,256},{1,257},{2,258},{3,259},{4,260},{5,261},{6,262},{7,263},{8... | collective-permute-start | bytes 393224 | tf_op jit(solution)/shard_map/ppermute | solution.py:41
  94.2 8.2 %collective-permute-start.1 = (f32[128,256]{1,0:T(8,128)}, f32[128,256]{1,0:T(8,128)S(1)}, u32[]{:S(2)}, u32[]{:S(2)}) collective-permute-start(f32[128,256]{1,0:T(8,128)} %get-tuple-element.19), channel_id=1, source_target_pairs={{0,512},{1,513},{2,514},{3,515},{4,516},{5,517},{6,518},{7,519},{8... | collective-permute-start | bytes 393224 | tf_op jit(solution)/shard_map/ppermute | solution.py:41
  97.9 7.6 %collective-permute-start.2 = (f32[128,256]{1,0:T(8,128)}, f32[128,256]{1,0:T(8,128)S(1)}, u32[]{:S(2)}, u32[]{:S(2)}) collective-permute-start(f32[128,256]{1,0:T(8,128)} %get-tuple-element.20), channel_id=1, source_target_pairs={{0,768},{1,769},{2,770},{3,771},{4,772},{5,773},{6,774},{7,775},{8... | collective-permute-start | bytes 393224 | tf_op jit(solution)/shard_map/ppermute | solution.py:41
  105.7 7.2 %collective-permute-start.3 = (bf16[136,256]{1,0:T(8,128)(2,1)S(1)}, bf16[136,256]{1,0:T(8,128)(2,1)S(1)}, u32[]{:S(2)}, u32[]{:S(2)}) collective-permute-start(bf16[136,256]{1,0:T(8,128)(2,1)S(1)} %merge.1), channel_id=1, source_target_pairs={{0,8},{1,9},{2,10},{3,11},{4,12},{5,13},{6,14},{7,15},{8,16},{9,17... | collective-permute-start | bytes 208904 | tf_op jit(solution)/shard_map/ppermute | solution.py:36
  108.9 9.3 %collective-permute-start.4 = (bf16[136,256]{1,0:T(8,128)(2,1)S(1)}, bf16[136,256]{1,0:T(8,128)(2,1)S(1)}, u32[]{:S(2)}, u32[]{:S(2)}) collective-permute-start(bf16[136,256]{1,0:T(8,128)(2,1)S(1)} %merge.1), channel_id=1, source_target_pairs={{0,16},{1,17},{2,18},{3,19},{4,20},{5,21},{6,22},{7,23},{8,24},{9,... | collective-permute-start | bytes 208904 | tf_op jit(solution)/shard_map/ppermute | solution.py:36
  112.9 9.3 %collective-permute-start.5 = (bf16[136,256]{1,0:T(8,128)(2,1)S(1)}, bf16[136,256]{1,0:T(8,128)(2,1)S(1)}, u32[]{:S(2)}, u32[]{:S(2)}) collective-permute-start(bf16[136,256]{1,0:T(8,128)(2,1)S(1)} %collective-permute-done.3), channel_id=1, source_target_pairs={{0,16},{1,17},{2,18},{3,19},{4,20},{5,21},{6,22},{7,23},{8,24},{9,... | collective-permute-start | bytes 208904 | tf_op jit(solution)/shard_map/ppermute | solution.py:36
  118.1 5.4 %collective-permute-start.6 = (bf16[136,256]{1,0:T(8,128)(2,1)S(1)}, bf16[136,256]{1,0:T(8,128)(2,1)S(1)}, u32[]{:S(2)}, u32[]{:S(2)}) collective-permute-start(bf16[136,256]{1,0:T(8,128)(2,1)S(1)} %collective-permute-done.4), channel_id=1, source_target_pairs={{0,16},{1,17},{2,18},{3,19},{4,20},{5,21},{6,22},{7,23},{8,24},{9,... | collective-permute-start | bytes 208904 | tf_op jit(solution)/shard_map/ppermute | solution.py:36
  123.5 6.1 %collective-permute-start.7 = (bf16[5,136,256]{2,1,0:T(8,128)(2,1)S(1)}, bf16[5,136,256]{2,1,0:T(8,128)(2,1)S(1)}, u32[]{:S(2)}, u32[]{:S(2)}) collective-permute-start(bf16[5,136,256]{2,1,0:T(8,128)(2,1)S(1)} %bitcast_dynamic-update-slice_fusion.mine_ref), channel_id=1, source_target_pairs={{0,4},{1,5},{2,6},{3,7},{4,0},{5,1},{6,2},{7,3},{8,12},{9,13},{10,... | collective-permute-start | bytes 1044488 | tf_op jit(solution)/shard_map/ppermute | solution.py:36
